TPU v7x, 32 devices: a whole 2x2x4 slice. The times are simulated.
32 devices in a mesh: dp: 4 (over z), row: 2 (over x), col: 4 (over y, core).
Axes of the slice: x: 2, y: 2, z: 4, core: 2. Of those that a mesh axis runs over, the one named last changes fastest.
Arguments:
- images: bfloat16 [32, 729, 1152], P(('dp', 'row', 'col')), may hold values from -6 to 6
- cotangent: bfloat16 [32, 729, 1152], P(('dp', 'row', 'col')), may hold values from -6 to 6
- first_gain: float32 [1152], replicated, may hold values from 0.25 to 1.75
- first_shift: float32 [1152], replicated, may hold values from -3 to 3
- query_weight: bfloat16 [1152, 1152], P('row', 'col'), may hold values from -0.1875 to 0.1875
- query_bias: float32 [1152], P('col'), may hold values from -3 to 3
- key_weight: bfloat16 [1152, 1152], P('row', 'col'), may hold values from -0.1875 to 0.1875
- value_weight: bfloat16 [1152, 1152], P('row', 'col'), may hold values from -0.1875 to 0.1875
- value_bias: float32 [1152], P('col'), may hold values from -3 to 3
- output_weight: bfloat16 [1152, 1152], P('col', 'row'), may hold values from -0.75 to 0.75
- output_bias: float32 [1152], replicated, may hold values from -3 to 3
- second_gain: float32 [1152], replicated, may hold values from 0.1 to 1.9
- second_shift: float32 [1152], replicated, may hold values from -3 to 3
- expand_weight: bfloat16 [1152, 4304], P('row', 'col'), may hold values from -0.1875 to 0.1875
- expand_bias: float32 [4304], P('col'), may hold values from -3 to 3
- shrink_weight: bfloat16 [4304, 1152], P('col', 'row'), may hold values from -0.1875 to 0.1875
- shrink_bias: float32 [1152], replicated, may hold values from -3 to 3
Outputs:
- layer_out: bfloat16 [32, 729, 1152], P(('dp', 'row', 'col'))
- grad_images: bfloat16 [32, 729, 1152], P(('dp', 'row', 'col'))
- grad_first_gain: float32 [1152], replicated
- grad_first_shift: float32 [1152], replicated
- grad_query_weight: float32 [1152, 1152], P('row', 'col')
- grad_query_bias: float32 [1152], P('col')
- grad_key_weight: float32 [1152, 1152], P('row', 'col')
- grad_value_weight: float32 [1152, 1152], P('row', 'col')
- grad_value_bias: float32 [1152], P('col')
- grad_output_weight: float32 [1152, 1152], P('col', 'row')
- grad_output_bias: float32 [1152], replicated
- grad_second_gain: float32 [1152], replicated
- grad_second_shift: float32 [1152], replicated
- grad_expand_weight: float32 [1152, 4304], P('row', 'col')
- grad_expand_bias: float32 [4304], P('col')
- grad_shrink_weight: float32 [4304, 1152], P('col', 'row')
- grad_shrink_bias: float32 [1152], replicated
All inputs are finite; a program needn't handle non-finite values.
Results may differ from a plain program's by a relative error of at most 0.038.
Values may be sent and summed in bfloat16 or wider, within the bound.
A program may use at most 448 MiB of HBM per device.

v0:
```python
import jax
import jax.numpy as jnp
from jax import lax
from jax.sharding import PartitionSpec as P

HEAD_DIM = 72


EPS = 1e-06
contract_last = (((2,), (1,)), ((), ()))
contract_rows = (((0, 1), (0, 1)), ((), ()))


def gelu_tanh(value):
    return jax.nn.gelu(value, approximate=True)


def norm_forward(stream, gain, shift):
    average = jnp.mean(stream, axis=-1, keepdims=True)
    second = jnp.mean(stream * stream, axis=-1, keepdims=True)
    inverse = lax.rsqrt(second - average * average + EPS)
    normed = (stream - average) * inverse
    return (normed, inverse, (normed * gain + shift).astype(jnp.bfloat16))


def norm_backward(grad_out, normed, inverse, gain):
    scaled = grad_out * gain
    first = jnp.mean(scaled, axis=-1, keepdims=True)
    second = jnp.mean(scaled * normed, axis=-1, keepdims=True)
    return inverse * (scaled - first - normed * second)


def spread(block):
    feature_part = lax.all_to_all(block, "row", split_axis=2, concat_axis=0, tiled=True)
    return lax.all_gather(feature_part, "col", axis=0, tiled=True)


def join_back(summed):
    return lax.all_to_all(
        summed.astype(jnp.bfloat16), "row", split_axis=0, concat_axis=2, tiled=True
    ).astype(summed.dtype)


def project_in(normed_bf, weight):
    gathered = spread(normed_bf)
    summed = lax.psum_scatter(
        jnp.dot(gathered, weight, preferred_element_type=jnp.float32).astype(jnp.bfloat16),
        "row",
        scatter_dimension=0,
        tiled=True,
    ).astype(jnp.float32)
    return (summed, gathered)


def project_out(block_bf, weight):
    partial_sums = jnp.dot(
        lax.all_gather(block_bf, "row", axis=0, tiled=True),
        weight,
        preferred_element_type=jnp.float32,
    )
    return join_back(
        lax.psum_scatter(
            partial_sums.astype(jnp.bfloat16), "col", scatter_dimension=0, tiled=True
        ).astype(jnp.float32)
    )


def back_out(grad_bf, acts_bf, weight):
    grads_all = spread(grad_bf)
    grad_acts = lax.psum_scatter(
        lax.dot_general(
            grads_all, weight, contract_last, preferred_element_type=jnp.float32
        ).astype(jnp.bfloat16),
        "row",
        scatter_dimension=0,
        tiled=True,
    ).astype(jnp.float32)
    grad_weight = lax.dot_general(
        lax.all_gather(acts_bf, "row", axis=0, tiled=True),
        grads_all,
        contract_rows,
        preferred_element_type=jnp.float32,
    )
    return (grad_acts, grad_weight)


def back_in(grad_bf, weight, normed_bf):
    inputs_all = spread(normed_bf)
    piece = lax.all_gather(grad_bf, "row", axis=0, tiled=True)
    contrib = lax.dot_general(piece, weight, contract_last, preferred_element_type=jnp.float32)
    partial_sums = contrib
    weight_grad = lax.dot_general(
        inputs_all, piece, contract_rows, preferred_element_type=jnp.float32
    )
    partial_sums, weight_grad = (partial_sums, weight_grad)
    grad_inputs = join_back(
        lax.psum_scatter(
            partial_sums.astype(jnp.bfloat16), "col", scatter_dimension=0, tiled=True
        ).astype(jnp.float32)
    )
    return (grad_inputs, weight_grad)


def split_heads(block):
    return block.reshape(block.shape[0], block.shape[1] // HEAD_DIM, HEAD_DIM)


def head_scores(queries, key_rows):
    scores = jnp.einsum(
        "qhd,khd->hqk",
        split_heads(queries),
        split_heads(key_rows),
        preferred_element_type=jnp.float32,
    )
    return scores * HEAD_DIM ** (-0.5)


def attend(queries, key_rows, value_rows):

    def one_image(triple):
        scores = head_scores(triple[0], triple[1])
        peak = jnp.max(scores, axis=-1, keepdims=True)
        log_total = peak + jnp.log(jnp.sum(jnp.exp(scores - peak), axis=-1, keepdims=True))
        attention = jnp.exp(scores - log_total).astype(jnp.bfloat16)
        mixed = jnp.einsum(
            "hqk,khd->qhd", attention, split_heads(triple[2]), preferred_element_type=jnp.float32
        )
        return (mixed.reshape(triple[0].shape).astype(jnp.bfloat16), log_total)

    return lax.map(one_image, (queries, key_rows, value_rows))


def attend_back(queries, key_rows, value_rows, attended, log_total, grad_attended):
    scale = HEAD_DIM ** (-0.5)

    def one_image(group):
        image_q, image_k, image_v, image_out, image_total, image_grad = group
        attention = jnp.exp(head_scores(image_q, image_k) - image_total)
        grad_heads = split_heads(image_grad)
        grad_probs = jnp.einsum(
            "qhd,khd->hqk", grad_heads, split_heads(image_v), preferred_element_type=jnp.float32
        )
        delta = jnp.einsum(
            "qhd,qhd->hq", grad_heads, split_heads(image_out), preferred_element_type=jnp.float32
        )[..., None]
        grad_scores = (attention * (grad_probs - delta)).astype(jnp.bfloat16)
        grad_queries = (
            jnp.einsum(
                "hqk,khd->qhd",
                grad_scores,
                split_heads(image_k),
                preferred_element_type=jnp.float32,
            )
            * scale
        )
        grad_keys = (
            jnp.einsum(
                "hqk,qhd->khd",
                grad_scores,
                split_heads(image_q),
                preferred_element_type=jnp.float32,
            )
            * scale
        )
        grad_values = jnp.einsum(
            "hqk,qhd->khd",
            attention.astype(jnp.bfloat16),
            grad_heads,
            preferred_element_type=jnp.float32,
        )
        shape = image_q.shape
        return (grad_queries.reshape(shape), grad_keys.reshape(shape), grad_values.reshape(shape))

    return lax.map(one_image, (queries, key_rows, value_rows, attended, log_total, grad_attended))


def feature_terms(grad_input1, normed1, grad_middle, grad_input2, normed2, grad_result):
    token_axes = (0, 1)
    return (
        jnp.sum(grad_input1 * normed1, axis=token_axes),
        jnp.sum(grad_input1, axis=token_axes),
        jnp.sum(grad_middle, axis=token_axes),
        jnp.sum(grad_input2 * normed2, axis=token_axes),
        jnp.sum(grad_input2, axis=token_axes),
        jnp.sum(grad_result, axis=token_axes),
    )


def embed_part(part_sum):
    start = lax.axis_index("col") * part_sum.shape[0]
    whole = jnp.zeros((part_sum.shape[0] * lax.axis_size("col"),), jnp.float32)
    return lax.dynamic_update_slice_in_dim(whole, part_sum, start, 0)


def grid_layer(images, cotangent, params):
    (
        first_gain,
        first_shift,
        query_weight,
        query_bias,
        key_weight,
        value_weight,
        value_bias,
        output_weight,
        output_bias,
        second_gain,
        second_shift,
        expand_weight,
        expand_bias,
        shrink_weight,
        shrink_bias,
    ) = params
    width = query_weight.shape[1]
    joined = jnp.concatenate((query_weight, key_weight, value_weight), axis=1)
    stream = images.astype(jnp.float32)
    normed1, inverse1, input1 = norm_forward(stream, first_gain, first_shift)
    projected, kept_first = project_in(input1, joined)
    queries = (projected[..., :width] + query_bias).astype(jnp.bfloat16)
    key_rows = projected[..., width : 2 * width].astype(jnp.bfloat16)
    value_rows = (projected[..., 2 * width :] + value_bias).astype(jnp.bfloat16)
    attended, log_total = attend(queries, key_rows, value_rows)
    middle = stream + project_out(attended, output_weight) + output_bias
    normed2, inverse2, input2 = norm_forward(middle, second_gain, second_shift)
    expanded, kept_second = project_in(input2, expand_weight)
    before = expanded + expand_bias
    hidden = gelu_tanh(before).astype(jnp.bfloat16)
    result = middle + project_out(hidden, shrink_weight) + shrink_bias
    grad_result = cotangent.astype(jnp.float32)
    grad_hidden, grad_shrink = back_out(cotangent, hidden, shrink_weight)
    gelu_back = jax.vjp(gelu_tanh, before)[1]
    grad_before = gelu_back(grad_hidden)[0]
    grad_input2, grad_expand = back_in(grad_before.astype(jnp.bfloat16), expand_weight, input2)
    grad_middle = grad_result + norm_backward(grad_input2, normed2, inverse2, second_gain)
    grad_attended, grad_output = back_out(grad_middle.astype(jnp.bfloat16), attended, output_weight)
    grad_queries, grad_keys, grad_values = attend_back(
        queries, key_rows, value_rows, attended, log_total, grad_attended.astype(jnp.bfloat16)
    )
    grad_joined_rows = jnp.concatenate((grad_queries, grad_keys, grad_values), axis=-1).astype(
        jnp.bfloat16
    )
    grad_input1, grad_joined = back_in(grad_joined_rows, joined, input1)
    grad_stream = grad_middle + norm_backward(grad_input1, normed1, inverse1, first_gain)
    token_axes = (0, 1)
    features = feature_terms(grad_input1, normed1, grad_middle, grad_input2, normed2, grad_result)
    biases = (
        embed_part(jnp.sum(grad_queries, axis=token_axes)),
        embed_part(jnp.sum(grad_values, axis=token_axes)),
        embed_part(jnp.sum(grad_before, axis=token_axes)),
    )
    blocks = (
        grad_joined[:, :width],
        grad_joined[:, width : 2 * width],
        grad_joined[:, 2 * width :],
        grad_output,
        grad_expand,
        grad_shrink,
    )
    return (result, grad_stream, features, biases, blocks)


def shards(
    images,
    cotangent,
    first_gain,
    first_shift,
    query_weight,
    query_bias,
    key_weight,
    value_weight,
    value_bias,
    output_weight,
    output_bias,
    second_gain,
    second_shift,
    expand_weight,
    expand_bias,
    shrink_weight,
    shrink_bias,
):
    params = (
        first_gain,
        first_shift,
        query_weight,
        query_bias,
        key_weight,
        value_weight,
        value_bias,
        output_weight,
        output_bias,
        second_gain,
        second_shift,
        expand_weight,
        expand_bias,
        shrink_weight,
        shrink_bias,
    )
    result, grad_stream, features, biases, blocks = grid_layer(images, cotangent, params)
    totals = lax.psum(
        (
            features[0],
            features[1],
            features[2],
            features[3],
            features[4],
            features[5],
            biases[0],
            biases[1],
            biases[2],
        ),
        ("dp", "row", "col"),
    )
    col_index = lax.axis_index("col")
    query_part = query_bias.shape[0]
    expand_part = expand_bias.shape[0]
    query_bias_grad = lax.dynamic_slice_in_dim(totals[6], col_index * query_part, query_part, 0)
    value_bias_grad = lax.dynamic_slice_in_dim(totals[7], col_index * query_part, query_part, 0)
    expand_bias_grad = lax.dynamic_slice_in_dim(totals[8], col_index * expand_part, expand_part, 0)
    weight_totals = (
        lax.psum(blocks[0].astype(jnp.bfloat16), "dp").astype(jnp.float32),
        lax.psum(blocks[1].astype(jnp.bfloat16), "dp").astype(jnp.float32),
        lax.psum(blocks[2].astype(jnp.bfloat16), "dp").astype(jnp.float32),
        lax.psum(blocks[3].astype(jnp.bfloat16), "dp").astype(jnp.float32),
        lax.psum(blocks[4].astype(jnp.bfloat16), "dp").astype(jnp.float32),
        lax.psum(blocks[5].astype(jnp.bfloat16), "dp").astype(jnp.float32),
    )
    return (
        result.astype(jnp.bfloat16),
        grad_stream.astype(jnp.bfloat16),
        totals[0],
        totals[1],
        weight_totals[0],
        query_bias_grad,
        weight_totals[1],
        weight_totals[2],
        value_bias_grad,
        weight_totals[3],
        totals[2],
        totals[3],
        totals[4],
        weight_totals[4],
        expand_bias_grad,
        weight_totals[5],
        totals[5],
    )


def solution(mesh):
    placed = (
        P(("dp", "row", "col"), None, None),
        P(("dp", "row", "col"), None, None),
        P(),
        P(),
        P("row", "col"),
        P("col"),
        P("row", "col"),
        P("row", "col"),
        P("col"),
        P("col", "row"),
        P(),
        P(),
        P(),
        P("row", "col"),
        P("col"),
        P("col", "row"),
        P(),
    )
    return jax.shard_map(
        shards,
        mesh=mesh,
        in_specs=placed,
        out_specs=(
            P(("dp", "row", "col"), None, None),
            P(("dp", "row", "col"), None, None),
            P(),
            P(),
            P("row", "col"),
            P("col"),
            P("row", "col"),
            P("row", "col"),
            P("col"),
            P("col", "row"),
            P(),
            P(),
            P(),
            P("row", "col"),
            P("col"),
            P("col", "row"),
            P(),
        ),
        check_vma=False,
    )
```

profile of v0, /device:TPU:0, one launch (start us, length us, event | category | flops | bytes accessed | tf_op | source)
XLA Modules:
  0.0 2109.5 jit_solution(17329852611036355849)
XLA Ops:
  37.9 25.5 %all_to_all.118 = bf16[2,2,209952]{2,1,0:T(2,128)(2,1)S(1)} all-to-all(bf16[2,2,209952]{2,1,0:T(2,128)(2,1)} %reshape.487), channel_id=1, replica_groups=mesh['dp'=4,'row'=2,'col'=4] {'row'}, dimensions={0} | all-to-all | bytes 3359232 | tf_op jit(solution)/shard_map/all_to_all | solution.py:34
  73.8 50.5 %all-gather.21.cloned.1.call-done = bf16[8,1,729,576]{2,3,1,0:T(8,128)(2,1)} async-done(((bf16[2,1,729,576]{2,3,1,0:T(8,128)(2,1)}), bf16[8,1,729,576]{2,3,1,0:T(8,128)(2,1)}) %all-gather.21.cloned.1.call-update) | async-done | bytes 6718480 | tf_op jit(solution)/shard_map/all_gather | solution.py:35
  138.9 122.5 %reduce-scatter.9.cloned.1.call-done = bf16[4,729,864]{2,1,0:T(8,128)(2,1)} async-done(((bf16[8,729,864]{2,1,0:T(8,128)(2,1)}), bf16[4,729,864]{2,1,0:T(8,128)(2,1)}) %reduce-scatter.9.cloned.1.call-update) | async-done | bytes 5038864 | tf_op jit(solution)/shard_map/reduce_scatter | solution.py:46
  283.5 32.8 %while.26 = (s32[]{:T(128)}, bf16[4,729,288]{1,2,0:T(8,128)(2,1)}, f32[4,4,729,1]{2,1,3,0:T(4,128)}, bf16[4,729,288]{1,2,0:T(8,128)(2,1)}, bf16[4,729,288]{1,2,0...) while((s32[]{:T(128)}, bf16[4,729,288]{1,2,0:T(8,128)(2,1)}, f32[4,4,729,1]{2,1,3,0:T(4,128)}, ...), condition=%wide.region_6.7_spmd, body=%wide.region_3.6_spmd.sunk | while | flops 629433152 | bytes 30664516 | solution.py:130
  316.9 49.0 %all-gather.13.cloned.1.call-done = bf16[8,729,288]{1,2,0:T(8,128)(2,1)} async-done(((bf16[4,729,288]{1,2,0:T(8,128)(2,1)}), bf16[8,729,288]{1,2,0:T(8,128)(2,1)}) %all-gather.13.cloned.1.call-update) | async-done | bytes 3359248 | tf_op jit(solution)/shard_map/all_gather | solution.py:57
  401.5 24.2 %all_to_all.119 = bf16[2,2,209952]{2,1,0:T(2,128)(2,1)S(1)} all-to-all(bf16[2,2,209952]{2,1,0:T(2,128)(2,1)} %reshape.489), channel_id=1, replica_groups=mesh['dp'=4,'row'=2,'col'=4] {'row'}, dimensions={0} | all-to-all | bytes 3359232 | tf_op jit(solution)/shard_map/all_to_all | solution.py:34
  439.0 25.3 %all_to_all.120 = bf16[2,729,576]{1,2,0:T(8,128)(2,1)S(1)} all-to-all(bf16[2,729,576]{1,2,0:T(8,128)(2,1)} %reduce-scatter.11.cloned.1.call-done), channel_id=1, replica_groups=mesh['dp'=4,'row'=2,'col'=4] {'row'}, dimensions={0} | all-to-all | bytes 3359232 | tf_op jit(solution)/shard_map/all_to_all | solution.py:39
  502.1 23.4 %all_to_all.121 = bf16[2,2,209952]{2,1,0:T(2,128)(2,1)S(1)} all-to-all(bf16[2,2,209952]{2,1,0:T(2,128)(2,1)} %reshape.491), channel_id=1, replica_groups=mesh['dp'=4,'row'=2,'col'=4] {'row'}, dimensions={0} | all-to-all | bytes 3359232 | tf_op jit(solution)/shard_map/all_to_all | solution.py:34
  535.1 16.6 convolution_convert_fusion
  551.8 33.1 %all-gather.23.cloned.1.call-done = bf16[8,1,729,576]{2,3,1,0:T(8,128)(2,1)} async-done(((bf16[2,1,729,576]{2,3,1,0:T(8,128)(2,1)}), bf16[8,1,729,576]{2,3,1,0:T(8,128)(2,1)}) %all-gather.23.cloned.1.call-update) | async-done | bytes 6718480 | tf_op jit(solution)/shard_map/all_gather | solution.py:35
  601.5 137.7 %reduce-scatter.17.cloned.1.call-done = bf16[4,729,1076]{1,2,0:T(8,128)(2,1)} async-done(((bf16[8,729,1076]{1,2,0:T(8,128)(2,1)}), bf16[4,729,1076]{1,2,0:T(8,128)(2,1)}) %reduce-scatter.17.cloned.1.call-update) | async-done | bytes 6275248 | tf_op jit(solution)/shard_map/reduce_scatter | solution.py:70
  739.2 154.3 %reduce-scatter.13.cloned.1.call-done = bf16[4,729,1076]{1,2,0:T(8,128)(2,1)} async-done(((bf16[8,729,1076]{1,2,0:T(8,128)(2,1)}), bf16[4,729,1076]{1,2,0:T(8,128)(2,1)}) %reduce-scatter.13.cloned.1.call-update) | async-done | bytes 6275248 | tf_op jit(solution)/shard_map/reduce_scatter | solution.py:46
  893.5 17.1 fusion.91
  911.7 159.2 %all-gather.17.cloned.1.call-done = bf16[8,729,1076]{1,2,0:T(8,128)(2,1)} async-done(((bf16[4,729,1076]{1,2,0:T(8,128)(2,1)}), bf16[8,729,1076]{1,2,0:T(8,128)(2,1)}) %all-gather.17.cloned.1.call-update) | async-done | bytes 12550480 | tf_op jit(solution)/shard_map/all_gather | solution.py:89
  1086.8 145.5 %all-gather.15.cloned.1.call-done = bf16[8,729,1076]{1,2,0:T(8,128)(2,1)} async-done(((bf16[4,729,1076]{1,2,0:T(8,128)(2,1)}), bf16[8,729,1076]{1,2,0:T(8,128)(2,1)}) %all-gather.15.cloned.1.call-update) | async-done | bytes 12550480 | tf_op jit(solution)/shard_map/all_gather | solution.py:57
  1248.2 50.8 %reduce-scatter.19.cloned.1.call-done = bf16[2,729,576]{1,2,0:T(8,128)(2,1)} async-done(((bf16[8,729,576]{1,2,0:T(8,128)(2,1)}), bf16[2,729,576]{1,2,0:T(8,128)(2,1)}) %reduce-scatter.19.cloned.1.call-update) | async-done | bytes 1679632 | tf_op jit(solution)/shard_map/reduce_scatter | solution.py:97
  1302.9 62.8 %reduce-scatter.15.cloned.1.call-done = bf16[2,729,576]{1,2,0:T(8,128)(2,1)} async-done(((bf16[8,729,576]{1,2,0:T(8,128)(2,1)}), bf16[2,729,576]{1,2,0:T(8,128)(2,1)}) %reduce-scatter.15.cloned.1.call-update) | async-done | bytes 1679632 | tf_op jit(solution)/shard_map/reduce_scatter | solution.py:62
  1437.5 23.0 %all_to_all.122 = bf16[2,2,209952]{2,1,0:T(2,128)(2,1)} all-to-all(bf16[2,2,209952]{2,1,0:T(2,128)(2,1)S(1)} %reshape.493), channel_id=1, replica_groups=mesh['dp'=4,'row'=2,'col'=4] {'row'}, dimensions={0} | all-to-all | bytes 3359232 | tf_op jit(solution)/shard_map/all_to_all | solution.py:34
  1468.0 49.6 %all-gather.27.cloned.1.call-done = bf16[8,1,729,576]{2,3,1,0:T(8,128)(2,1)} async-done(((bf16[2,1,729,576]{2,3,1,0:T(8,128)(2,1)}), bf16[8,1,729,576]{2,3,1,0:T(8,128)(2,1)}) %all-gather.27.cloned.1.call-update) | async-done | bytes 6718480 | tf_op jit(solution)/shard_map/all_gather | solution.py:35
  1525.4 47.8 %reduce-scatter.21.cloned.1.call-done = bf16[4,729,288]{1,2,0:T(8,128)(2,1)} async-done(((bf16[8,729,288]{1,2,0:T(8,128)(2,1)}), bf16[4,729,288]{1,2,0:T(8,128)(2,1)}) %reduce-scatter.21.cloned.1.call-update) | async-done | bytes 1679632 | tf_op jit(solution)/shard_map/reduce_scatter | solution.py:70
  1573.3 70.2 %while.27 = (s32[]{:T(128)}, f32[4,729,288]{1,2,0:T(8,128)}, bf16[4,729,288]{1,2,0:T(8,128)(2,1)}, f32[4,729,288]{1,2,0:T(8,128)S(1)}, bf16[4,729,288]{1,2,0:T(8...) while((s32[]{:T(128)}, f32[4,729,288]{1,2,0:T(8,128)}, ...), condition=%wide.region_18.19_spmd, body=%wide.region_17.18_spmd.sunk | while | flops 1549022848 | bytes 52812796 | solution.py:174
  1659.0 130.3 %all-gather.19.cloned.1.call-done = bf16[8,729,864]{2,1,0:T(8,128)(2,1)} async-done(((bf16[4,729,864]{2,1,0:T(8,128)(2,1)}), bf16[8,729,864]{2,1,0:T(8,128)(2,1)}) %all-gather.19.cloned.1.call-update) | async-done | bytes 10077712 | tf_op jit(solution)/shard_map/all_gather | solution.py:89
  1871.9 159.5 %all-reduce.4.cloned.1.call-done = (bf16[576,288]{1,0:T(8,128)(2,1)}, bf16[576,288]{1,0:T(8,128)(2,1)}, bf16[576,288]{1,0:T(8,128)(2,1)}, bf16[288,576]{1,0:T(8,...) async-done(((bf16[576,288]{1,0:T(8,128)(2,1)}, bf16[576,288]{1,0:T(8,128)(2,1)}, bf16[576,288]{1,0:T(8,128)(2,1)}, bf16[288,576]{1,0:T(8,128)(2,1)}, ...) | async-done | bytes 3806224 | tf_op jit(solution)/shard_map/psum | solution.py:319
  2054.8 41.5 %all-reduce = (f32[1152]{0:T(1024)}, f32[1152]{0:T(1024)}, f32[1152]{0:T(1024)S(1)}, f32[1152]{0:T(1024)S(1)}, f32[1152]{0:T(1024)}, /*index=5*/f32[1152]{0:T(10...) all-reduce(f32[1152]{0:T(1024)S(1)} %get-tuple-element.309, ...), channel_id=1, replica_groups=mesh['dp'=4,'row'=2,'col'=4] {'dp','row','col'}, use_global_device_ids=true, to_apply=%region_23.24 | all-reduce | flops 13520 | bytes 108160 | tf_op jit(solution)/shard_map/psum | solution.py:298
  (308 shorter events, 545.5 us)
Async XLA Ops:
  7.2 577.7 %copy-start = (bf16[576,1076]{1,0:T(8,128)(2,1)S(1)}, bf16[576,1076]{1,0:T(8,128)(2,1)}, u32[]{:S(2)}) copy-start(bf16[576,1076]{1,0:T(8,128)(2,1)} %param.34) | copy-start | bytes 3718660
  7.2 117.1 %all-gather.21.cloned.1.call-start = ((), (), s32[]{:S(2)}) async-start(), calls=%async_computation.28 | async-start | bytes 8847360 | tf_op jit(solution)/shard_map/all_gather | solution.py:35
  72.7 188.6 %reduce-scatter.9.cloned.1.call-start = ((), (), s32[]{:S(2)}) async-start(), calls=%async_computation.16 | async-start | bytes 15826944 | tf_op jit(solution)/shard_map/reduce_scatter | solution.py:46
  138.6 227.3 %all-gather.13.cloned.1.call-start = ((), (), s32[]{:S(2)}) async-start(), calls=%async_computation.17 | async-start | bytes 5308416 | tf_op jit(solution)/shard_map/all_gather | solution.py:57
  316.4 122.7 %reduce-scatter.11.cloned.1.call-start = ((), (), s32[]{:S(2)}) async-start(), calls=%async_computation.18 | async-start | bytes 8847360 | tf_op jit(solution)/shard_map/reduce_scatter | solution.py:62
  374.7 160.4 %all-gather.25.cloned.1.call-start = ((), (), s32[]{:S(2)}) async-start(), calls=%async_computation.30 | async-start | bytes 8847360 | tf_op jit(solution)/shard_map/all_gather | solution.py:35
  434.8 150.1 %all-gather.23.cloned.1.call-start = ((), (), s32[]{:S(2)}) async-start(), calls=%async_computation.29 | async-start | bytes 8847360 | tf_op jit(solution)/shard_map/all_gather | solution.py:35
  534.8 204.4 %reduce-scatter.17.cloned.1.call-start = ((), (), s32[]{:S(2)}) async-start(), calls=%async_computation.22 | async-start | bytes 19906560 | tf_op jit(solution)/shard_map/reduce_scatter | solution.py:70
  551.7 341.7 %reduce-scatter.13.cloned.1.call-start = ((), (), s32[]{:S(2)}) async-start(), calls=%async_computation.19 | async-start | bytes 19906560 | tf_op jit(solution)/shard_map/reduce_scatter | solution.py:46
  601.4 292.0 %copy-start.34 = (f32[1076]{0:T(1024)S(1)}, f32[1076]{0:T(1024)}, u32[]{:S(2)}) copy-start(f32[1076]{0:T(1024)} %param.35) | copy-start | bytes 12916
  601.5 469.4 %all-gather.17.cloned.1.call-start = ((), (), s32[]{:S(2)}) async-start(), calls=%async_computation.23 | async-start | bytes 19906560 | tf_op jit(solution)/shard_map/all_gather | solution.py:89
  910.6 321.7 %all-gather.15.cloned.1.call-start = ((), (), s32[]{:S(2)}) async-start(), calls=%async_computation.20 | async-start | bytes 19906560 | tf_op jit(solution)/shard_map/all_gather | solution.py:57
  911.2 387.9 %reduce-scatter.19.cloned.1.call-start = ((), (), s32[]{:S(2)}) async-start(), calls=%async_computation.24 | async-start | bytes 8847360 | tf_op jit(solution)/shard_map/reduce_scatter | solution.py:97
  1086.7 279.0 %reduce-scatter.15.cloned.1.call-start = ((), (), s32[]{:S(2)}) async-start(), calls=%async_computation.21 | async-start | bytes 8847360 | tf_op jit(solution)/shard_map/reduce_scatter | solution.py:62
  1299.1 66.6 %all-to-all-start.5 = ((bf16[2,729,576]{1,2,0:T(8,128)(2,1)}), bf16[2,729,576]{1,2,0:T(8,128)(2,1)S(1)}, u32[]{:S(2)}, u32[]{:S(2)}) async-start(bf16[2,729,576]{1,2,0:T(8,128)(2,1)} %reduce-scatter.19.cloned.1.call-done), calls=%async_computation.11 | async-start | bytes 3538944 | tf_op jit(solution)/shard_map/all_to_all | solution.py:39
  1365.7 26.2 %all-to-all-start.3 = ((bf16[2,729,576]{1,2,0:T(8,128)(2,1)}), bf16[2,729,576]{1,2,0:T(8,128)(2,1)}, u32[]{:S(2)}, u32[]{:S(2)}) async-start(bf16[2,729,576]{1,2,0:T(8,128)(2,1)} %reduce-scatter.15.cloned.1.call-done), calls=%async_computation.7 | async-start | bytes 3538944 | tf_op jit(solution)/shard_map/all_to_all | solution.py:39
  1370.4 147.2 %all-gather.27.cloned.1.call-start = ((), (), s32[]{:S(2)}) async-start(), calls=%async_computation.31 | async-start | bytes 8847360 | tf_op jit(solution)/shard_map/all_gather | solution.py:35
  1467.6 105.7 %reduce-scatter.21.cloned.1.call-start = ((), (), s32[]{:S(2)}) async-start(), calls=%async_computation.25 | async-start | bytes 5308416 | tf_op jit(solution)/shard_map/reduce_scatter | solution.py:70
  1525.4 263.9 %all-gather.19.cloned.1.call-start = ((), (), s32[]{:S(2)}) async-start(), calls=%async_computation.26 | async-start | bytes 15826944 | tf_op jit(solution)/shard_map/all_gather | solution.py:89
  1658.9 130.4 %copy-start.14 = (bf16[576,288]{1,0:T(8,128)(2,1)S(1)}, bf16[576,288]{1,0:T(8,128)(2,1)}, u32[]{:S(2)}) copy-start(bf16[576,288]{1,0:T(8,128)(2,1)} %copy-done.13) | copy-start | bytes 995332
  1658.9 130.4 %copy-start.16 = (bf16[576,288]{1,0:T(8,128)(2,1)S(1)}, bf16[576,288]{1,0:T(8,128)(2,1)}, u32[]{:S(2)}) copy-start(bf16[576,288]{1,0:T(8,128)(2,1)} %copy-done.15) | copy-start | bytes 995332
  1658.9 208.3 %reduce-scatter.23.cloned.1.call-start = ((), (), s32[]{:S(2)}) async-start(), calls=%async_computation.27 | async-start | bytes 8847360 | tf_op jit(solution)/shard_map/reduce_scatter | solution.py:97
  1802.9 228.5 %all-reduce.4.cloned.1.call-start = ((), (), s32[]{:S(2)}) async-start(), calls=%async_computation.32 | async-start | bytes 8699904 | tf_op jit(solution)/shard_map/psum | solution.py:319
  1867.2 176.1 %all-to-all-start.7 = ((bf16[2,729,576]{1,2,0:T(8,128)(2,1)}), bf16[2,729,576]{1,2,0:T(8,128)(2,1)S(1)}, u32[]{:S(2)}, u32[]{:S(2)}) async-start(bf16[2,729,576]{1,2,0:T(8,128)(2,1)} %reduce-scatter.23.cloned.1.call-done), calls=%async_computation.15 | async-start | bytes 3538944 | tf_op jit(solution)/shard_map/all_to_all | solution.py:39
  (39 other events, 736.8 us)
Sparse Core Ops, SparseCore 0:
  72.9 51.3 all-gather.20
  138.7 122.6 reduce-scatter.8
  316.5 49.3 all-gather.12
  374.8 64.1 reduce-scatter.10
  440.5 50.8 all-gather.24
  534.9 49.8 all-gather.22
  587.2 151.9 reduce-scatter.16
  741.5 151.9 reduce-scatter.12
  910.7 160.0 all-gather.16
  1072.2 160.0 all-gather.14
  1234.8 64.1 reduce-scatter.18
  1301.5 64.1 reduce-scatter.14
  1467.7 49.8 all-gather.26
  1525.5 47.7 reduce-scatter.20
  1659.0 130.1 all-gather.18
  1803.0 64.1 reduce-scatter.22
  1871.1 160.2 all-reduce.3
where the time goes:
time: 2120 us; the launch traced here: 2110 us
  waiting for transfers between devices  1380 us (65%)
  matrix products  208 us (10%)
  local copies, waits for them, and re-layouts  194 us (9%)
  blocking collectives  163 us (8%)
  other arithmetic  135 us (6%)
    all_gather x2, waiting for transfers between devices, back_in(): piece = lax.all_gather(grad_bf, 'row', axis=0, tiled=True)  289 us
    reduce_scatter x2, waiting for transfers between devices, project_in(): lax.psum_scatter(jnp.dot(gathered, weight, preferred_element_type=jnp.flo...  277 us
    all_gather x2, waiting for transfers between devices, project_out(): lax.all_gather(block_bf, 'row', axis=0, tiled=True)  195 us
    reduce_scatter x2, waiting for transfers between devices, back_out(): lax.psum_scatter(lax.dot_general(grads_all, weight, contract_last, prefer...  185 us
    psum x1, waiting for transfers between devices, shards(): lax.psum(blocks[0].astype(jnp.bfloat16), 'dp').astype(jnp.float32)  159 us
    all_gather x4, waiting for transfers between devices, spread(): return lax.all_gather(feature_part, 'col', axis=0, tiled=True)  133 us
    all_to_all x4, blocking collectives, spread(): lax.all_to_all(block, 'row', split_axis=2, concat_axis=0, tiled=True)  96.1 us
    unnamed x106, local copies, waits for them, and re-layouts  77.6 us
  transfers between devices with their start and end apart: 20, of which 17 were waited for; matrix products, arithmetic and copies ran while one was open for 11% of the time, Pallas kernels for 0%

commit v1 on v0

v1 whole, which is shorter than its diff:
```python
import functools, math
import jax
import jax.numpy as jnp
from jax import lax
from jax.experimental import pallas as pl
from jax.experimental.pallas import tpu as pltpu
from jax.sharding import PartitionSpec as P

HEAD = 72
LANE = 128
F32, BF16 = jnp.float32, jnp.bfloat16
NT = (((1,), (1,)), ((), ()))
TN = (((0,), (0,)), ((), ()))
ANY = pl.BlockSpec(memory_space=pl.ANY)
VM = pl.BlockSpec(memory_space=pltpu.VMEM)
VLIM = 60 * 1024 * 1024


def dot(a, b):
    return jnp.dot(a, b, preferred_element_type=F32)


def dot_nt(a, b):
    return lax.dot_general(a, b, NT, preferred_element_type=F32)


def dot_tn(a, b):
    return lax.dot_general(a, b, TN, preferred_element_type=F32)


def tiles(total, width, body):
    count = -(-total // width)

    def step(i, _):
        body(pl.multiple_of(jnp.minimum(i * width, total - width), LANE))
        return 0

    lax.fori_loop(0, count, step, 0)


class Copies:
    def __init__(self, sems):
        self.sems, self.n = sems, 0

    def __call__(self, src, dst):
        copy = pltpu.make_async_copy(src, dst, self.sems.at[self.n])
        self.n += 1
        copy.start()
        return copy


def load_rows(copies, blocks, dst):
    n = len(blocks)
    size = blocks[0].shape[0]
    me = lax.axis_index("row")
    out = []
    for s, block in enumerate(blocks):
        row = lax.rem(me - s + n, n)
        out.append(copies(block, dst.at[pl.ds(pl.multiple_of(row * size, 16), size), :]))
    return out


def wait(copies):
    for copy in copies:
        copy.wait()


GC = math.sqrt(2.0 / math.pi)


def ff_kernel(n, *refs):
    in2, cot, bias = refs[:3]
    eb, sb = refs[3 : 3 + n], refs[3 + n : 3 + 2 * n]
    res_in, gi_in = refs[3 + 2 * n : 5 + 2 * n]
    hid_o, gb_o, res_o, gi_o, db = refs[5 + 2 * n : 10 + 2 * n]
    in2_v, cot_v, e_v, s_v, hid_v, gb_v, res_v, gi_v, sems = refs[10 + 2 * n :]
    c = Copies(sems)
    first = [c(in2, in2_v)] + load_rows(c, eb, e_v)
    second = [c(cot, cot_v)] + load_rows(c, sb, s_v)
    third = [c(res_in, res_v), c(gi_in, gi_v)]
    wait(first)
    wait(second)
    width = e_v.shape[1]

    def hidden_tile(at):
        cols = pl.ds(at, 256)
        b = dot(in2_v[...], e_v[:, cols]) + bias[:, cols]
        sq = b * b
        t = jnp.tanh(GC * b * (1.0 + 0.044715 * sq))
        half = 0.5 * (1.0 + t)
        hid_v[:, cols] = (b * half).astype(BF16)
        slope = half + (0.5 * GC) * b * (1.0 - t * t) * (1.0 + (3 * 0.044715) * sq)
        g = dot(cot_v[...], s_v[:, cols]) * slope
        gb_v[:, cols] = g.astype(BF16)
        db[:, cols] = jnp.sum(g, axis=0, keepdims=True)

    tiles(width, 256, hidden_tile)
    out = [c(hid_v, hid_o), c(gb_v, gb_o)]
    wait(third)

    for a in range(0, width, 256):
        w = min(256, width - a)
        res_v[:, a : a + w] += dot_nt(hid_v[...], s_v[a : a + w, :])
        gi_v[:, a : a + w] += dot_nt(gb_v[...], e_v[a : a + w, :])
    out += [c(res_v, res_o), c(gi_v, gi_o)]
    wait(out)


def ff(in2, cot, bias, eb, sb, res, gi):
    n, (t, d) = len(eb), in2.shape
    w = eb[0].shape[1]
    o = jax.ShapeDtypeStruct
    return pl.pallas_call(
        functools.partial(ff_kernel, n),
        name="ff",
        in_specs=[ANY, ANY, VM] + [ANY] * (2 * n + 2),
        out_specs=[ANY] * 4 + [VM],
        out_shape=[o((t, w), BF16), o((t, w), BF16), o((t, d), F32), o((t, d), F32), o((1, w), F32)],
        scratch_shapes=[
            pltpu.VMEM((t, d), BF16), pltpu.VMEM((t, d), BF16),
            pltpu.VMEM((d, w), BF16), pltpu.VMEM((d, w), BF16),
            pltpu.VMEM((t, w), BF16), pltpu.VMEM((t, w), BF16),
            pltpu.VMEM((t, d), F32), pltpu.VMEM((t, d), F32),
            pltpu.SemaphoreType.DMA((2 * n + 8,)),
        ],
        input_output_aliases={3 + 2 * n: 2, 4 + 2 * n: 3},
        compiler_params=pltpu.CompilerParams(vmem_limit_bytes=VLIM),
        cost_estimate=pl.CostEstimate(flops=8 * t * d * w, bytes_accessed=4 * d * w + 12 * t * d + 8 * t * d, transcendentals=t * w),
    )(in2, cot, bias, *eb, *sb, res, gi)


def lanes(shape):
    return lax.broadcasted_iota(jnp.int32, shape, 1)


def pick(ref, at):
    base = at // LANE * LANE
    window = ref[:, base : base + 2 * LANE]
    shift = at - base
    if shift:
        window = pltpu.roll(window, 2 * LANE - shift, 1)
    return window[:, :LANE]


def put(ref, at, value):
    base = min(at // LANE * LANE, ref.shape[1] - 2 * LANE)
    wide = jnp.concatenate((value, jnp.zeros_like(value)), axis=1)
    if at - base:
        wide = pltpu.roll(wide, at - base, 1)
    ref[:, base : base + 2 * LANE] += wide


def split3(value):
    hi = value.astype(BF16).astype(F32)
    rest = value - hi
    mid = rest.astype(BF16).astype(F32)
    return hi, mid, rest - mid


SCALE = HEAD ** -0.5
C2 = SCALE * math.log2(math.e)
PENALTY = -1e30


def attn_kernel(n, heads, length, chunk, *refs):
    in1, bias = refs[:2]
    ab = refs[2 : 2 + n]
    mid_in = refs[2 + n]
    q_o, k_o, v_o, att_o, mid_o = refs[3 + n : 8 + n]
    in1_v, a_v, qkv_v, q_v, k_v, v_v, o_v, att_v, mid_v, attb_v, sems = refs[8 + n :]
    t = in1_v.shape[0]
    c = Copies(sems)
    first = [c(in1, in1_v)] + load_rows(c, ab, a_v)
    third = [c(mid_in, mid_v)]
    wait(first)

    def proj(at):
        cols = pl.ds(at, 256)
        qkv_v[:, cols] = dot(in1_v[...], a_v[:, cols]) + bias[:, cols]

    tiles(7 * LANE, 256, proj)
    lane = lanes((t, LANE))
    row = lax.broadcasted_iota(jnp.int32, (t, LANE), 0)
    tail_k = jnp.where(lane < HEAD + 3, 1.0, jnp.where((lane == HEAD + 3) & (row >= length), 1.0, 0.0))
    tail_q = jnp.where(lane == HEAD + 3, PENALTY, 0.0)
    tail_v = jnp.where(lane < HEAD + 2, 1.0, 0.0)
    part = HEAD * heads
    for j in range(heads):
        q_v[j] = jnp.where(lane < HEAD, pick(qkv_v, HEAD * j), tail_q).astype(BF16)
        k_v[j] = jnp.where(lane < HEAD, pick(qkv_v, part + HEAD * j), tail_k).astype(BF16)
        v_v[j] = jnp.where(lane < HEAD, pick(qkv_v, 2 * part + HEAD * j), tail_v).astype(BF16)
    out = [c(k_v, k_o), c(v_v, v_o)]

    def head(j, _):
        def rows(i, _):
            at = pl.ds(pl.multiple_of(i * chunk, 16), chunk)
            q = q_v[j, at, :]
            s = dot_nt(q, k_v[j])
            m = jnp.max(s, axis=1, keepdims=True)
            p = jnp.exp2((s - m) * C2)
            o = dot(p.astype(BF16), v_v[j])
            ln = lanes((chunk, LANE))
            total = jnp.sum(jnp.where(ln == HEAD, o, 0.0), axis=1, keepdims=True)
            o_v[j, at, :] = jnp.where(ln < HEAD, o / total, 0.0)
            hi, mid, lo = split3(m + jnp.log2(total) * (1.0 / C2))
            aug = jnp.where(ln == HEAD, -hi, jnp.where(ln == HEAD + 1, -mid, jnp.where(ln == HEAD + 2, -lo, q.astype(F32))))
            q_v[j, at, :] = aug.astype(BF16)
            return 0

        return lax.fori_loop(0, t // chunk, rows, 0)

    lax.fori_loop(0, heads, head, 0)
    out += [c(q_v, q_o)]
    att_v[...] = jnp.zeros_like(att_v)
    for j in range(heads):
        put(att_v, 3 * LANE - part + HEAD * j, o_v[j])
    attb_v[...] = att_v[...].astype(BF16)
    out += [c(attb_v, att_o)]
    wait(third)
    d = mid_v.shape[1]
    for a in range(0, d, 256):
        w = min(256, d - a)
        mid_v[:, a : a + w] += dot_nt(attb_v[...], a_v[a : a + w, 6 * LANE : 9 * LANE])
    out += [c(mid_v, mid_o)]
    wait(out)


def attn(in1, bias, ab, mid, length, chunk=368):
    n, (t, d) = len(ab), in1.shape
    w = ab[0].shape[1]
    heads = w // 4 // HEAD
    o = jax.ShapeDtypeStruct
    hs = (heads, t, LANE)
    return pl.pallas_call(
        functools.partial(attn_kernel, n, heads, length, chunk),
        name="attn",
        in_specs=[ANY, VM] + [ANY] * (n + 1),
        out_specs=[ANY] * 5,
        out_shape=[o(hs, BF16)] * 3 + [o((t, 3 * LANE), BF16), o((t, d), F32)],
        scratch_shapes=[
            pltpu.VMEM((t, d), BF16), pltpu.VMEM((d, w), BF16), pltpu.VMEM((t, 8 * LANE), F32),
            pltpu.VMEM(hs, BF16), pltpu.VMEM(hs, BF16), pltpu.VMEM(hs, BF16), pltpu.VMEM(hs, F32),
            pltpu.VMEM((t, 3 * LANE), F32), pltpu.VMEM((t, d), F32), pltpu.VMEM((t, 3 * LANE), BF16),
            pltpu.SemaphoreType.DMA((n + 8,)),
        ],
        input_output_aliases={2 + n: 4},
        compiler_params=pltpu.CompilerParams(vmem_limit_bytes=VLIM),
        cost_estimate=pl.CostEstimate(flops=2 * t * d * w + 8 * heads * t * t * LANE, bytes_accessed=2 * d * w + 10 * t * d, transcendentals=heads * t * t),
    )(in1, bias, *ab, mid)


def back_kernel(n, heads, chunk, *refs):
    gm = refs[0]
    ab = refs[1 : 1 + n]
    q_i, k_i, v_i, att_i, gi_in = refs[1 + n : 6 + n]
    dqkv_o, gi_o, db = refs[6 + n : 9 + n]
    gm_v, a_v, ga_v, q_v, k_v, v_v, g_v, att_v, ds_v, dq_v, dk_v, dv_v, pack_v, packb_v, gi_v, sems = refs[9 + n :]
    t = gm_v.shape[0]
    c = Copies(sems)
    first = [c(gm, gm_v)] + load_rows(c, ab, a_v)
    second = [c(att_i, att_v), c(q_i, q_v), c(k_i, k_v), c(v_i, v_v)]
    third = [c(gi_in, gi_v)]
    wait(first)
    ga_v[...] = dot(gm_v[...], a_v[:, 6 * LANE : 9 * LANE])
    lane = lanes((t, LANE))
    part = HEAD * heads
    wait(second)
    att = pack_v.at[:, : 3 * LANE]
    att[...] = att_v[...].astype(F32)
    for j in range(heads):
        at = 3 * LANE - part + HEAD * j
        base = min(at // LANE * LANE, LANE)
        def grab(ref):
            window = ref[:, base : base + 2 * LANE]
            return pltpu.roll(window, 2 * LANE - (at - base), 1)[:, :LANE] if at > base else window[:, :LANE]
        g = jnp.where(lane < HEAD, grab(ga_v), 0.0).astype(BF16).astype(F32)
        delta = jnp.sum(g * grab(att), axis=1, keepdims=True)
        hi = delta.astype(BF16).astype(F32)
        g_v[j] = jnp.where(lane == HEAD, -hi, jnp.where(lane == HEAD + 1, hi - delta, g)).astype(BF16)

    def head(j, _):
        def rows(i, _):
            at = pl.ds(pl.multiple_of(i * chunk, 16), chunk)
            p = jnp.exp2(dot_nt(k_v[j, at, :], q_v[j]) * C2)
            pb = p.astype(BF16)
            ds = (p * dot_nt(v_v[j, at, :], g_v[j])).astype(BF16)
            dv_v[j, at, :] = dot(pb, g_v[j])
            dk_v[j, at, :] = dot(ds, q_v[j]) * SCALE
            ds_v[at, :] = ds
            return 0

        lax.fori_loop(0, t // chunk, rows, 0)
        dq_v[j] = dot_tn(ds_v[...], k_v[j]) * SCALE
        return 0

    lax.fori_loop(0, heads, head, 0)
    pack_v[...] = jnp.zeros_like(pack_v)
    for j in range(heads):
        put(pack_v, HEAD * j, jnp.where(lane < HEAD, dq_v[j], 0.0))
        put(pack_v, part + HEAD * j, jnp.where(lane < HEAD, dk_v[j], 0.0))
        put(pack_v, 2 * part + HEAD * j, jnp.where(lane < HEAD, dv_v[j], 0.0))
    db[...] = jnp.sum(pack_v[...], axis=0, keepdims=True)
    packb_v[...] = pack_v[...].astype(BF16)
    out = [c(packb_v, dqkv_o)]
    wait(third)
    d = gi_v.shape[1]
    for a in range(0, d, 256):
        w = min(256, d - a)
        gi_v[:, a : a + w] += dot_nt(packb_v[...], a_v[a : a + w, : 7 * LANE])
    out += [c(gi_v, gi_o)]
    wait(out)


def back(gm, ab, q, k, v, att, gi, chunk=368):
    n, (t, d) = len(ab), gm.shape
    w = ab[0].shape[1]
    heads = q.shape[0]
    o = jax.ShapeDtypeStruct
    hs = (heads, t, LANE)
    return pl.pallas_call(
        functools.partial(back_kernel, n, heads, chunk),
        name="back",
        in_specs=[ANY] * (n + 6),
        out_specs=[ANY] * 2 + [VM],
        out_shape=[o((t, 7 * LANE), BF16), o((t, d), F32), o((1, 7 * LANE), F32)],
        scratch_shapes=[
            pltpu.VMEM((t, d), BF16), pltpu.VMEM((d, w), BF16), pltpu.VMEM((t, 3 * LANE), F32),
            pltpu.VMEM(hs, BF16), pltpu.VMEM(hs, BF16), pltpu.VMEM(hs, BF16), pltpu.VMEM(hs, BF16),
            pltpu.VMEM((t, 3 * LANE), BF16), pltpu.VMEM((t, t), BF16),
            pltpu.VMEM(hs, F32), pltpu.VMEM(hs, F32), pltpu.VMEM(hs, F32),
            pltpu.VMEM((t, 7 * LANE), F32), pltpu.VMEM((t, 7 * LANE), BF16), pltpu.VMEM((t, d), F32),
            pltpu.SemaphoreType.DMA((n + 8,)),
        ],
        input_output_aliases={5 + n: 1},
        compiler_params=pltpu.CompilerParams(vmem_limit_bytes=VLIM),
        cost_estimate=pl.CostEstimate(flops=2 * t * d * w + 20 * heads * t * t * LANE, bytes_accessed=2 * d * w + 16 * t * d, transcendentals=heads * t * t),
    )(gm, *ab, q, k, v, att, gi)


def grads_kernel(n, groups, *refs):
    k = len(groups)
    ins = refs[: 4 * k]
    outs = refs[4 * k : 4 * k + n]
    scratch = refs[4 * k + n :]
    lhs, rhs = scratch[: 2 * k], scratch[2 * k : 4 * k]
    acc, tile_v, sems, osem = scratch[4 * k :]
    c = Copies(sems)
    cps = []
    for i in range(k):
        cps += [c(ins[4 * i + u], (lhs if u < 2 else rhs)[2 * i + u % 2]) for u in range(4)]
    wait(cps)
    size = outs[0].shape[0]
    me = lax.axis_index("row")

    def step(s, _):
        slot = lax.rem(s, 2)
        row = pl.multiple_of(lax.rem(me + s, n) * size, 16)
        rows = pl.ds(row, size)

        @pl.when(s >= 2)
        def _():
            pltpu.make_async_copy(tile_v.at[slot], outs[0], osem.at[slot]).wait()

        if k == 1:
            def body(at):
                cols = pl.ds(at, 256)
                tile_v[slot, :, cols] = (
                    dot(lhs[0][rows, :], rhs[0][:, cols]) + dot(lhs[1][rows, :], rhs[1][:, cols])
                ).astype(BF16)

            tiles(groups[0][1], 256, body)
        else:
            for i, (start, width) in enumerate(groups):
                done = 0 if i == 0 else groups[i - 1][0] + groups[i - 1][1]
                for a in range(0, width, 256):
                    w = min(256, width - a)
                    value = dot(lhs[2 * i][rows, :], rhs[2 * i][:, a : a + w]) + dot(
                        lhs[2 * i + 1][rows, :], rhs[2 * i + 1][:, a : a + w]
                    )
                    at = start + a
                    if at < done:
                        o = done - at
                        value = jnp.concatenate((value[:, :o] + acc[:, at : at + o], value[:, o:]), axis=1) if o < w else value + acc[:, at : at + w]
                    acc[:, at : at + w] = value
            tile_v[slot] = acc[...].astype(BF16)
        for u in range(n):
            @pl.when(s == u)
            def _():
                pltpu.make_async_copy(tile_v.at[slot], outs[u], osem.at[slot]).start()
        return 0

    lax.fori_loop(0, n, step, 0)
    for u in range(max(0, n - 2), n):
        pltpu.make_async_copy(tile_v.at[u % 2], outs[u], osem.at[u % 2]).wait()


def grads(n, terms, width):
    k = len(terms)
    groups = tuple((term[0], term[3].shape[1]) for term in terms)
    flat = [array for term in terms for array in term[1:]]
    d, t = terms[0][1].shape
    size = d // n
    scratch = [pltpu.VMEM(term[1].shape, BF16) for term in terms for _ in range(2)]
    scratch += [pltpu.VMEM(term[3].shape, BF16) for term in terms for _ in range(2)]
    flops = sum(4 * d * t * w for _, w in groups)
    return pl.pallas_call(
        functools.partial(grads_kernel, n, groups),
        name="grads",
        in_specs=[ANY] * (4 * k),
        out_specs=[ANY] * n,
        out_shape=[jax.ShapeDtypeStruct((size, width), BF16)] * n,
        scratch_shapes=scratch + [
            pltpu.VMEM((size, width if k > 1 else LANE), F32), pltpu.VMEM((2, size, width), BF16),
            pltpu.SemaphoreType.DMA((4 * k,)), pltpu.SemaphoreType.DMA((2,)),
        ],
        compiler_params=pltpu.CompilerParams(vmem_limit_bytes=VLIM),
        cost_estimate=pl.CostEstimate(flops=flops, bytes_accessed=2 * d * width + 8 * t * d, transcendentals=0),
    )(*flat)


def hop_row(value, shift, size):
    return lax.ppermute(value, "row", [(i, (i + shift) % size) for i in range(size)])


def hop_col(value, flip):
    return lax.ppermute(value, "col", [(i, i ^ flip) for i in range(4)])


def hop_dp(value, flip):
    return lax.ppermute(value, "dp", [(i, i ^ flip) for i in range(4)])


CORE, SIDE = 1, 2


def gather(block, n, by_row):
    own = [block] + [hop_row(block, s, n) for s in range(1, n)]
    side = [hop_col(block, SIDE)]
    for s in range(1, n):
        side.append(hop_row(side[0], s, n) if by_row else hop_col(own[s], SIDE))
    return [own, side, [hop_col(b, CORE) for b in own], [hop_col(b, CORE) for b in side]]


def add(a, b):
    return (a.astype(F32) + b.astype(F32)).astype(BF16)


def scatter(own, side, n, row_first):
    def over_row(parts):
        total = parts[0]
        for s in range(1, n):
            total = add(total, hop_row(parts[s], s, n))
        return total

    if row_first:
        total = add(over_row(own), hop_col(over_row(side), SIDE))
    else:
        total = over_row([add(a, hop_col(b, SIDE)) for a, b in zip(own, side)])
    half = total.shape[0] // 2
    z = lax.axis_index("dp")
    low = lax.rem(z, 2)
    mine = lax.dynamic_slice_in_dim(total, low * half, half, 0)
    theirs = lax.dynamic_slice_in_dim(total, (1 - low) * half, half, 0)
    mine = add(mine, hop_dp(theirs, 1))
    mine = add(mine, hop_dp(mine, 2))
    theirs = hop_dp(mine, 1)
    return jnp.where(low == 0, jnp.concatenate((mine, theirs)), jnp.concatenate((theirs, mine)))


def norm(stream, gain, shift):
    average = jnp.mean(stream, axis=-1, keepdims=True)
    second = jnp.mean(stream * stream, axis=-1, keepdims=True)
    inverse = lax.rsqrt(second - average * average + EPS)
    return average, inverse, ((stream - average) * inverse * gain + shift).astype(BF16)


def norm_back(grad, normed, inverse, gain):
    scaled = grad * gain
    first = jnp.mean(scaled, axis=-1, keepdims=True)
    second = jnp.mean(scaled * normed, axis=-1, keepdims=True)
    return inverse * (scaled - first - normed * second)


EPS = 1e-6


def layer(n, images, cotangent, first_gain, first_shift, query_weight, query_bias, key_weight, value_weight, value_bias,
          output_weight, output_bias, second_gain, second_shift, expand_weight, expand_bias, shrink_weight, shrink_bias):
    length, d = images.shape[1:]
    t = -(-length // 16) * 16
    part, ff_part = query_weight.shape[1], expand_weight.shape[1]
    wide = 4 * part
    pad_ff = ((0, 0), (0, wide - ff_part))
    a_own = jnp.concatenate((query_weight, key_weight, value_weight, output_weight.T), axis=1)
    e_own = jnp.pad(expand_weight, pad_ff)
    s_own = jnp.pad(shrink_weight.T, pad_ff)
    zeros = jnp.zeros((part,), F32)
    bias_own = jnp.stack((jnp.concatenate((query_bias, zeros, value_bias, zeros)), jnp.pad(expand_bias, pad_ff[1:])))
    a_all = gather(a_own, n, True)
    bias_side = hop_col(bias_own, SIDE)
    biases = [bias_own, bias_side, hop_col(bias_own, CORE), hop_col(bias_side, CORE)]
    e_all = gather(e_own, n, True)
    s_all = gather(s_own, n, False)

    pad_t = ((0, t - length), (0, 0))
    stream = jnp.pad(images[0], pad_t).astype(F32)
    cot = jnp.pad(cotangent[0], pad_t)
    cot_t = cot.T
    cot_t2 = hop_col(cot_t, CORE)
    average1, inverse1, input1 = norm(stream, first_gain, first_shift)
    in1_t = input1.T
    in1_t2 = hop_col(in1_t, CORE)

    order = (0, 2, 1, 3)
    kept = {}
    middle = stream + output_bias
    for slot in order:
        *kept[slot], middle = attn(input1, biases[slot][:1], a_all[slot], middle, length)
    average2, inverse2, input2 = norm(middle, second_gain, second_shift)
    in2_t = input2.T
    in2_t2 = hop_col(in2_t, CORE)
    result = middle + shrink_bias
    grad2 = jnp.zeros((t, d), F32)
    hidden, before, expand_sums = {}, {}, {}
    for slot in order:
        hidden[slot], before[slot], result, grad2, expand_sums[slot] = ff(
            input2, cot, biases[slot][1:], e_all[slot], s_all[slot], result, grad2)
    ge, gs = [], []
    for slot in (0, 1):
        ge.append(grads(n, [(0, in2_t, in2_t2, before[slot], hop_col(before[slot + 2], CORE))], wide))
        gs.append(grads(n, [(0, cot_t, cot_t2, hidden[slot], hop_col(hidden[slot + 2], CORE))], wide))
    ge = scatter(ge[0], ge[1], n, True)
    gs = scatter(gs[0], gs[1], n, False)

    cot32 = cot.astype(F32)
    normed2 = (middle - average2) * inverse2
    grad_middle = cot32 + norm_back(grad2, normed2, inverse2, second_gain)
    gm = grad_middle.astype(BF16)
    gm_t = gm.T
    gm_t2 = hop_col(gm_t, CORE)
    grad1 = jnp.zeros((t, d), F32)
    joined, joined_sums = {}, {}
    for slot in (2, 0, 3, 1):
        q, k, v, att = kept[slot]
        joined[slot], grad1, joined_sums[slot] = back(gm, a_all[slot], q, k, v, att, grad1)
    ga = []
    for slot in (0, 1):
        ga.append(grads(n, [
            (0, in1_t, in1_t2, joined[slot], hop_col(joined[slot + 2], CORE)),
            (wide - 384, gm_t, gm_t2, kept[slot][3], hop_col(kept[slot + 2][3], CORE)),
        ], wide))
    ga = scatter(ga[0], ga[1], n, True)
    normed1 = (stream - average1) * inverse1
    grad_stream = grad_middle + norm_back(grad1, normed1, inverse1, first_gain)

    features = jnp.stack([jnp.sum(v, axis=0) for v in (
        grad1 * normed1, grad1, grad_middle, grad2 * normed2, grad2, cot32)])
    sums = {s: jnp.concatenate((jnp.pad(joined_sums[s], ((0, 0), (0, wide - joined_sums[s].shape[1]))), expand_sums[s])) for s in range(4)}
    pair = jnp.concatenate((features, sums[0], sums[1])) + hop_col(jnp.concatenate((features, sums[2], sums[3])), CORE)
    one = pair[:8] + hop_col(jnp.concatenate((pair[:6], pair[8:])), SIDE)
    total = one
    for s in range(1, n):
        total = total + hop_row(one, s, n)
    for flip in (1, 2):
        total = total + hop_dp(total, flip)

    return (
        result[:length].astype(BF16)[None],
        grad_stream[:length].astype(BF16)[None],
        total[0],
        total[1],
        ga[:, :part].astype(F32),
        total[6, :part],
        ga[:, part : 2 * part].astype(F32),
        ga[:, 2 * part : 3 * part].astype(F32),
        total[6, 2 * part : 3 * part],
        ga[:, 3 * part :].astype(F32).T,
        total[2],
        total[3],
        total[4],
        ge[:, :ff_part].astype(F32),
        total[7, :ff_part],
        gs[:, :ff_part].astype(F32).T,
        total[5],
    )


def solution(mesh):
    batch = P(("dp", "row", "col"), None, None)
    into, out, cols, whole = P("row", "col"), P("col", "row"), P("col"), P()
    return jax.shard_map(
        functools.partial(layer, mesh.shape["row"]),
        mesh=mesh,
        in_specs=(batch, batch, whole, whole, into, cols, into, into, cols, out, whole, whole, whole, into, cols, out, whole),
        out_specs=(batch, batch, whole, whole, into, cols, into, into, cols, out, whole, whole, whole, into, cols, out, whole),
        check_vma=False,
    )
```

time: 2120 us -> 806 us (0.38)
  waiting for transfers between devices: 1380 us -> 283 us
  Pallas kernels: 0 us -> 296 us
  matrix products: 208 us -> 0 us
  blocking collectives: 163 us -> 0 us
  local copies, waits for them, and re-layouts: 194 us -> 101 us
  other arithmetic: 135 us -> 68.5 us
  starting transfers between devices: 14.9 us -> 45.1 us
    all_gather x8 -> x0, waiting for transfers between devices: 617 us -> none  [the longest x2 289 us: back_in(): piece = lax.all_gather(grad_bf, 'row', axis=0, tiled=True)]
    reduce_scatter x8 -> x0, waiting for transfers between devices: 595 us -> none  [the longest x2 277 us: project_in(): lax.psum_scatter(jnp.dot(gathered, weight, preferred_element_type=jnp.flo...]
    pallas_call x0 -> x18, Pallas kernels: none -> 296 us  [the longest x4 79.9 us: ff(): pl.pallas_call(functools.partial(ff_kernel, n), name='ff', in_specs=[ANY,...]
    ppermute x0 -> x59, waiting for transfers between devices: none -> 283 us  [the longest x11 121 us: hop_dp(): return lax.ppermute(value, 'dp', [(i, i ^ flip) for i in range(4)])]
    dot_general x40 -> x0, matrix products: 208 us -> none  [the longest x2 30.8 us: project_in(): jnp.dot(gathered, weight, preferred_element_type=jnp.float32)]
    psum x1 -> x0, waiting for transfers between devices: 159 us -> none  [shards(): lax.psum(blocks[0].astype(jnp.bfloat16), 'dp').astype(jnp.float32)]
    all_to_all x5 -> x0, blocking collectives: 121 us -> none  [the longest x4 96.1 us: spread(): lax.all_to_all(block, 'row', split_axis=2, concat_axis=0, tiled=True)]
    unnamed x106 -> x105, local copies, waits for them, and re-layouts: 77.6 us -> 17.1 us
  transfers between devices with their start and end apart: 20 -> 59, of which waited for: 17 -> 19; matrix products, arithmetic and copies ran while one was open for 11% -> 13% of each run, Pallas kernels for 0% -> 25%
where the time goes in v1:
time: 806 us; the launch traced here: 796 us
  Pallas kernels  296 us (37%)
  waiting for transfers between devices  283 us (35%)
  local copies, waits for them, and re-layouts  101 us (13%)
  other arithmetic  68.5 us (8%)
  starting transfers between devices  45.1 us (6%)
    ppermute x11, waiting for transfers between devices, hop_dp(): return lax.ppermute(value, 'dp', [(i, i ^ flip) for i in range(4)])  121 us
    ppermute x11, waiting for transfers between devices, hop_row(): lax.ppermute(value, 'row', [(i, (i + shift) % size) for i in range(size)])  117 us
    pallas_call x4, Pallas kernels, ff(): pl.pallas_call(functools.partial(ff_kernel, n), name='ff', in_specs=[ANY,...  79.9 us
    pallas_call x4, Pallas kernels, back(): pl.pallas_call(functools.partial(back_kernel, n, heads, chunk), name='bac...  78.2 us
    pallas_call x4, Pallas kernels, attn(): pl.pallas_call(functools.partial(attn_kernel, n, heads, length, chunk), n...  73.9 us
    pallas_call x6, Pallas kernels, grads(): pl.pallas_call(functools.partial(grads_kernel, n, groups), name='grads',...  64.3 us
    ppermute x37, waiting for transfers between devices, hop_col(): return lax.ppermute(value, 'col', [(i, i ^ flip) for i in range(4)])  44.2 us
    reduce_sum x5, other arithmetic, layer(): jnp.sum(v, axis=0)  18.5 us
  transfers between devices with their start and end apart: 59, of which 19 were waited for; matrix products, arithmetic and copies ran while one was open for 13% of the time, Pallas kernels for 25%

profile of v1, /device:TPU:0, one launch (start us, length us, event | category | flops | bytes accessed | tf_op | source)
XLA Modules:
  0.0 796.0 jit_solution(9244987164100726627)
XLA Ops:
  21.4 17.1 %collective-permute-done.2.refs_2_.refs_1_ = bf16[576,1152]{1,0:T(8,128)(2,1)} collective-permute-done((bf16[576,1152]{1,0:T(8,128)(2,1)}, bf16[576,1152]{1,0:T(8,128)(2,1)}, u32[]{:S(2)}, u32[]{:S(2)}) %collective-permute-start.2) | collective-permute-done | bytes 1327136 | tf_op jit(solution)/shard_map/ppermute | solution.py:426
  71.8 18.3 %attn.4 = (bf16[4,736,128]{2,1,0:T(8,128)(2,1)}, bf16[4,736,128]{2,1,0:T(8,128)(2,1)}, bf16[4,736,128]{2,1,0:T(8,128)(2,1)}, bf16[736,384]{1,0:T(8,128)(2,1)}, f32[736,1152]{1,0:T(8,128)}) custom-call(bf16[736,1152]{1,0:T(8,128)(2,1)} %copy.136.refs_0_, f32[1,1152]{1,0:T(1,128)} %copy-done.34, ...), custom_call_target="tpu_custom_call", output_to_operand_aliasing={{4}: (4, {})} | custom-call | flops 4172283904 | bytes 11132928 | tf_op jit(solution)/shard_map/attn/pallas_call | solution.py:234
  98.5 18.5 %attn.5 = (bf16[4,736,128]{2,1,0:T(8,128)(2,1)}, bf16[4,736,128]{2,1,0:T(8,128)(2,1)}, bf16[4,736,128]{2,1,0:T(8,128)(2,1)}, bf16[736,384]{1,0:T(8,128)(2,1)}, f32[736,1152]{1,0:T(8,128)}) custom-call(bf16[736,1152]{1,0:T(8,128)(2,1)} %copy.136.refs_0_, f32[1,1152]{1,0:T(1,128)} %get-tuple-element.227.refs_1_, ...), custom_call_target="tpu_custom_call", output_to_operand_aliasing={{4}: (4, {})} | custom-call | flops 4172283904 | bytes 11132928 | tf_op jit(solution)/shard_map/attn/pallas_call | solution.py:234
  118.7 18.3 %attn.6 = (bf16[4,736,128]{2,1,0:T(8,128)(2,1)}, bf16[4,736,128]{2,1,0:T(8,128)(2,1)}, bf16[4,736,128]{2,1,0:T(8,128)(2,1)}, bf16[736,384]{1,0:T(8,128)(2,1)}, f32[736,1152]{1,0:T(8,128)}) custom-call(bf16[736,1152]{1,0:T(8,128)(2,1)} %copy.136.refs_0_, f32[1,1152]{1,0:T(1,128)} %get-tuple-element.229.refs_1_, ...), custom_call_target="tpu_custom_call", output_to_operand_aliasing={{4}: (4, {})} | custom-call | flops 4172283904 | bytes 11132928 | tf_op jit(solution)/shard_map/attn/pallas_call | solution.py:234
  137.0 18.7 %attn.7 = (bf16[4,736,128]{2,1,0:T(8,128)(2,1)}, bf16[4,736,128]{2,1,0:T(8,128)(2,1)}, bf16[4,736,128]{2,1,0:T(8,128)(2,1)}, bf16[736,384]{1,0:T(8,128)(2,1)}, f32[736,1152]{1,0:T(8,128)}) custom-call(bf16[736,1152]{1,0:T(8,128)(2,1)} %copy.136.refs_0_, f32[1,1152]{1,0:T(1,128)} %get-tuple-element.231.refs_1_, ...), custom_call_target="tpu_custom_call", output_to_operand_aliasing={{4}: (4, {})} | custom-call | flops 4172283904 | bytes 11132928 | tf_op jit(solution)/shard_map/attn/pallas_call | solution.py:234
  174.5 20.0 %ff.4 = (bf16[736,1152]{1,0:T(8,128)(2,1)}, bf16[736,1152]{1,0:T(8,128)(2,1)}, f32[736,1152]{1,0:T(8,128)}, f32[736,1152]{1,0:T(8,128)}, f32[1,1152]{1,0:T(1,128)}) custom-call(bf16[736,1152]{1,0:T(8,128)(2,1)} %copy.145.refs_0_, bf16[736,1152]{1,0:T(8,128)(2,1)} %pad.33.clone.refs_1_, ...), custom_call_target="tpu_custom_call", output_to_operand_aliasing={{2}: (7, {}), {3}: (8, {})} | custom-call | flops 7813988352 | bytes 22265856 | tf_op jit(solution)/shard_map/ff/pallas_call | solution.py:113
  197.1 26.0 %collective-permute-done.17.refs_6_ = bf16[576,1152]{1,0:T(8,128)(2,1)} collective-permute-done((bf16[576,1152]{1,0:T(8,128)(2,1)}, bf16[576,1152]{1,0:T(8,128)(2,1)}, u32[]{:S(2)}, u32[]{:S(2)}) %collective-permute-start.17) | collective-permute-done | bytes 1327136 | tf_op jit(solution)/shard_map/ppermute | solution.py:426
  223.1 20.1 %ff.5 = (bf16[736,1152]{1,0:T(8,128)(2,1)}, bf16[736,1152]{1,0:T(8,128)(2,1)}, f32[736,1152]{1,0:T(8,128)}, f32[736,1152]{1,0:T(8,128)}, f32[1,1152]{1,0:T(1,128)}) custom-call(bf16[736,1152]{1,0:T(8,128)(2,1)} %copy.145.refs_0_, bf16[736,1152]{1,0:T(8,128)(2,1)} %pad.33.clone.refs_1_, ...), custom_call_target="tpu_custom_call", output_to_operand_aliasing={{2}: (7, {}), {3}: (8, {})} | custom-call | flops 7813988352 | bytes 22265856 | tf_op jit(solution)/shard_map/ff/pallas_call | solution.py:113
  243.2 19.9 %ff.6 = (bf16[736,1152]{1,0:T(8,128)(2,1)}, bf16[736,1152]{1,0:T(8,128)(2,1)}, f32[736,1152]{1,0:T(8,128)}, f32[736,1152]{1,0:T(8,128)}, f32[1,1152]{1,0:T(1,128)}) custom-call(bf16[736,1152]{1,0:T(8,128)(2,1)} %copy.145.refs_0_, bf16[736,1152]{1,0:T(8,128)(2,1)} %pad.33.clone.refs_1_, ...), custom_call_target="tpu_custom_call", output_to_operand_aliasing={{2}: (7, {}), {3}: (8, {})} | custom-call | flops 7813988352 | bytes 22265856 | tf_op jit(solution)/shard_map/ff/pallas_call | solution.py:113
  263.2 19.9 %ff.7 = (bf16[736,1152]{1,0:T(8,128)(2,1)}, bf16[736,1152]{1,0:T(8,128)(2,1)}, f32[736,1152]{1,0:T(8,128)}, f32[736,1152]{1,0:T(8,128)}, f32[1,1152]{1,0:T(1,128)}) custom-call(bf16[736,1152]{1,0:T(8,128)(2,1)} %copy.145.refs_0_, bf16[736,1152]{1,0:T(8,128)(2,1)} %pad.33.clone.refs_1_, ...), custom_call_target="tpu_custom_call", output_to_operand_aliasing={{2}: (7, {}), {3}: (8, {})} | custom-call | flops 7813988352 | bytes 22265856 | tf_op jit(solution)/shard_map/ff/pallas_call | solution.py:113
  303.9 19.8 %back.4 = (bf16[736,896]{1,0:T(8,128)(2,1)}, f32[736,1152]{1,0:T(8,128)}, f32[1,896]{1,0:T(1,128)}) custom-call(bf16[736,1152]{1,0:T(8,128)(2,1)} %copy.151.refs_0_, bf16[576,1152]{1,0:T(8,128)(2,1)} %collective-permute-done.7.refs_2_.refs_1_, bf16[576,1152]{1,0:T(8,128)(2,1)} %collective-permute-done.9.refs_3_.refs_2_, ...), custom_call_target="tpu_custom_call", output_to_operand_aliasing={{1}: (7, {})} | custom-call | flops 7500464128 | bytes 16220160 | tf_op jit(solution)/shard_map/back/pallas_call | solution.py:320
  323.7 19.4 %back.5 = (bf16[736,896]{1,0:T(8,128)(2,1)}, f32[736,1152]{1,0:T(8,128)}, f32[1,896]{1,0:T(1,128)}) custom-call(bf16[736,1152]{1,0:T(8,128)(2,1)} %copy.151.refs_0_, bf16[576,1152]{1,0:T(8,128)(2,1)} %concatenate.36.refs_2_.refs_1_, bf16[576,1152]{1,0:T(8,128)(2,1)} %collective-permute-done.8.refs_3_.refs_2_, ...), custom_call_target="tpu_custom_call", output_to_operand_aliasing={{1}: (7, {})} | custom-call | flops 7500464128 | bytes 16220160 | tf_op jit(solution)/shard_map/back/pallas_call | solution.py:320
  343.1 19.6 %back.6 = (bf16[736,896]{1,0:T(8,128)(2,1)}, f32[736,1152]{1,0:T(8,128)}, f32[1,896]{1,0:T(1,128)}) custom-call(bf16[736,1152]{1,0:T(8,128)(2,1)} %copy.151.refs_0_, bf16[576,1152]{1,0:T(8,128)(2,1)} %collective-permute-done.3.refs_2_.refs_1_, bf16[576,1152]{1,0:T(8,128)(2,1)} %collective-permute-done.5.refs_3_.refs_2_, ...), custom_call_target="tpu_custom_call", output_to_operand_aliasing={{1}: (7, {})} | custom-call | flops 7500464128 | bytes 16220160 | tf_op jit(solution)/shard_map/back/pallas_call | solution.py:320
  362.7 19.4 %back.7 = (bf16[736,896]{1,0:T(8,128)(2,1)}, f32[736,1152]{1,0:T(8,128)}, f32[1,896]{1,0:T(1,128)}) custom-call(bf16[736,1152]{1,0:T(8,128)(2,1)} %copy.151.refs_0_, bf16[576,1152]{1,0:T(8,128)(2,1)} %collective-permute-done.2.refs_2_.refs_1_, bf16[576,1152]{1,0:T(8,128)(2,1)} %collective-permute-done.4.refs_3_.refs_2_, ...), custom_call_target="tpu_custom_call", output_to_operand_aliasing={{1}: (7, {})} | custom-call | flops 7500464128 | bytes 16220160 | tf_op jit(solution)/shard_map/back/pallas_call | solution.py:320
  484.7 11.0 %grads.7 = (bf16[576,1152]{1,0:T(8,128)(2,1)}, bf16[576,1152]{1,0:T(8,128)(2,1)}) custom-call(bf16[1152,736]{1,0:T(8,128)(2,1)} %bitcast.26, bf16[1152,736]{1,0:T(8,128)(2,1)} %copy.157.refs_1_, bf16[736,896]{1,0:T(8,128)(2,1)} %get-tuple-element.125.refs_2_, bf16[736,896]{1,0:T(8,128)(2,1)} %copy-done.44, bf16[1152,736]{1,0:T(8,128)(2,1)} %convert_bitcast_fusion.2.refs_4_, ...), custom_call_target="tpu_custom_call" | custom-call | flops 4341104640 | bytes 9437184 | tf_op jit(solution)/shard_map/grads/pallas_call | solution.py:406
  523.1 11.1 %grads.6 = (bf16[576,1152]{1,0:T(8,128)(2,1)}, bf16[576,1152]{1,0:T(8,128)(2,1)}) custom-call(bf16[1152,736]{1,0:T(8,128)(2,1)} %bitcast.27, bf16[1152,736]{1,0:T(8,128)(2,1)} %copy.157.refs_1_, bf16[736,896]{1,0:T(8,128)(2,1)} %get-tuple-element.121.refs_2_, bf16[736,896]{1,0:T(8,128)(2,1)} %collective-permute-done.30.refs_3_, ...), custom_call_target="tpu_custom_call" | custom-call | flops 4341104640 | bytes 9437184 | tf_op jit(solution)/shard_map/grads/pallas_call | solution.py:406
  542.6 25.2 %collective-permute-done.45 = bf16[576,1152]{1,0:T(8,128)(2,1)} collective-permute-done((bf16[576,1152]{1,0:T(8,128)(2,1)}, bf16[576,1152]{1,0:T(8,128)(2,1)}, u32[]{:S(2)}, u32[]{:S(2)}) %collective-permute-start.45) | collective-permute-done | bytes 1327136 | tf_op jit(solution)/shard_map/ppermute | solution.py:422
  571.6 53.0 %collective-permute-done.55 = bf16[576,1152]{1,0:T(8,128)(2,1)} collective-permute-done((bf16[576,1152]{1,0:T(8,128)(2,1)}, bf16[576,1152]{1,0:T(8,128)(2,1)}, u32[]{:S(2)}, u32[]{:S(2)}) %collective-permute-start.55) | collective-permute-done | bytes 1327136 | tf_op jit(solution)/shard_map/ppermute | solution.py:422
  628.2 24.0 %collective-permute-done.33 = bf16[576,1152]{1,0:T(8,128)(2,1)S(1)} collective-permute-done((bf16[576,1152]{1,0:T(8,128)(2,1)}, bf16[576,1152]{1,0:T(8,128)(2,1)S(1)}, u32[]{:S(2)}, u32[]{:S(2)}) %collective-permute-start.33) | collective-permute-done | bytes 1327136 | tf_op jit(solution)/shard_map/ppermute | solution.py:422
  656.1 14.4 %collective-permute-done.38 = bf16[288,1152]{1,0:T(8,128)(2,1)S(1)} collective-permute-done((bf16[288,1152]{1,0:T(8,128)(2,1)S(1)}, bf16[288,1152]{1,0:T(8,128)(2,1)S(1)}, u32[]{:S(2)}, u32[]{:S(2)}) %collective-permute-start.38) | collective-permute-done | bytes 663584 | tf_op jit(solution)/shard_map/ppermute | solution.py:430
  674.0 21.0 %collective-permute-done.47 = bf16[288,1152]{1,0:T(8,128)(2,1)S(1)} collective-permute-done((bf16[288,1152]{1,0:T(8,128)(2,1)S(1)}, bf16[288,1152]{1,0:T(8,128)(2,1)S(1)}, u32[]{:S(2)}, u32[]{:S(2)}) %collective-permute-start.47) | collective-permute-done | bytes 663584 | tf_op jit(solution)/shard_map/ppermute | solution.py:430
  696.9 35.2 %collective-permute-done.39 = bf16[288,1152]{1,0:T(8,128)(2,1)S(1)} collective-permute-done((bf16[288,1152]{1,0:T(8,128)(2,1)S(1)}, bf16[288,1152]{1,0:T(8,128)(2,1)S(1)}, u32[]{:S(2)}, u32[]{:S(2)}) %collective-permute-start.39) | collective-permute-done | bytes 663584 | tf_op jit(solution)/shard_map/ppermute | solution.py:430
  732.4 14.1 %collective-permute-done.57 = bf16[288,1152]{1,0:T(8,128)(2,1)S(1)} collective-permute-done((bf16[288,1152]{1,0:T(8,128)(2,1)S(1)}, bf16[288,1152]{1,0:T(8,128)(2,1)S(1)}, u32[]{:S(2)}, u32[]{:S(2)}) %collective-permute-start.57) | collective-permute-done | bytes 663584 | tf_op jit(solution)/shard_map/ppermute | solution.py:430
  757.5 13.0 %collective-permute-done.40 = bf16[288,1152]{1,0:T(8,128)(2,1)S(1)} collective-permute-done((bf16[288,1152]{1,0:T(8,128)(2,1)S(1)}, bf16[288,1152]{1,0:T(8,128)(2,1)S(1)}, u32[]{:S(2)}, u32[]{:S(2)}) %collective-permute-start.40) | collective-permute-done | bytes 663584 | tf_op jit(solution)/shard_map/ppermute | solution.py:430
  (310 shorter events, 296.9 us)
Async XLA Ops:
  9.0 51.6 %collective-permute-start.8 = (bf16[576,1152]{1,0:T(8,128)(2,1)}, bf16[576,1152]{1,0:T(8,128)(2,1)}, u32[]{:S(2)}, u32[]{:S(2)}) collective-permute-start(bf16[576,1152]{1,0:T(8,128)(2,1)} %concatenate.36.refs_2_.refs_1_), channel_id=1, source_target_pairs={{0,4},{4,0},{1,5},{5,1},{2,6},{6,2},{3,7},{7,3},{8,12},{12,8},{9,1... | collective-permute-start | bytes 3981320 | tf_op jit(solution)/shard_map/ppermute | solution.py:422
  11.2 48.7 %collective-permute-start.6 = (f32[2,1152]{1,0:T(2,128)}, f32[2,1152]{1,0:T(2,128)}, u32[]{:S(2)}, u32[]{:S(2)}) collective-permute-start(f32[2,1152]{1,0:T(2,128)} %pad_maximum_fusion.5), channel_id=1, source_target_pairs={{0,1},{1,0},{2,3},{3,2},{4,5},{5,4},{6,7},{7,6},{8,9},{9,8},{10,11... | collective-permute-start | bytes 27656 | tf_op jit(solution)/shard_map/ppermute | solution.py:426
  62.4 54.7 %collective-permute-start.3 = (bf16[576,1152]{1,0:T(8,128)(2,1)}, bf16[576,1152]{1,0:T(8,128)(2,1)}, u32[]{:S(2)}, u32[]{:S(2)}) collective-permute-start(bf16[576,1152]{1,0:T(8,128)(2,1)} %collective-permute-done.2.refs_2_.refs_1_), channel_id=1, source_target_pairs={{0,1},{1,0},{2,3},{3,2},{4,5},{5,4},{6,7},{7,6},{8,9},{9,8},{10,11... | collective-permute-start | bytes 3981320 | tf_op jit(solution)/shard_map/ppermute | solution.py:426
  94.0 69.8 %collective-permute-start.20 = (bf16[576,1152]{1,0:T(8,128)(2,1)}, bf16[576,1152]{1,0:T(8,128)(2,1)}, u32[]{:S(2)}, u32[]{:S(2)}) collective-permute-start(bf16[576,1152]{1,0:T(8,128)(2,1)} %pad.34.refs_3_), channel_id=1, source_target_pairs={{0,4},{4,0},{1,5},{5,1},{2,6},{6,2},{3,7},{7,3},{8,12},{12,8},{9,1... | collective-permute-start | bytes 3981320 | tf_op jit(solution)/shard_map/ppermute | solution.py:422
  97.7 66.1 %collective-permute-start.19 = (bf16[576,1152]{1,0:T(8,128)(2,1)}, bf16[576,1152]{1,0:T(8,128)(2,1)}, u32[]{:S(2)}, u32[]{:S(2)}) collective-permute-start(bf16[576,1152]{1,0:T(8,128)(2,1)} %pad.34.refs_3_), channel_id=1, source_target_pairs={{0,1},{1,0},{2,3},{3,2},{4,5},{5,4},{6,7},{7,6},{8,9},{9,8},{10,11... | collective-permute-start | bytes 3981320 | tf_op jit(solution)/shard_map/ppermute | solution.py:426
  97.9 65.2 %collective-permute-start.16 = (bf16[576,1152]{1,0:T(8,128)(2,1)}, bf16[576,1152]{1,0:T(8,128)(2,1)}, u32[]{:S(2)}, u32[]{:S(2)}) collective-permute-start(bf16[576,1152]{1,0:T(8,128)(2,1)} %pad.35.refs_5_), channel_id=1, source_target_pairs={{0,4},{4,0},{1,5},{5,1},{2,6},{6,2},{3,7},{7,3},{8,12},{12,8},{9,1... | collective-permute-start | bytes 3981320 | tf_op jit(solution)/shard_map/ppermute | solution.py:422
  163.7 59.4 %collective-permute-start.17 = (bf16[576,1152]{1,0:T(8,128)(2,1)}, bf16[576,1152]{1,0:T(8,128)(2,1)}, u32[]{:S(2)}, u32[]{:S(2)}) collective-permute-start(bf16[576,1152]{1,0:T(8,128)(2,1)} %collective-permute-done.16.refs_6_), channel_id=1, source_target_pairs={{0,2},{1,3},{2,0},{3,1},{4,6},{5,7},{6,4},{7,5},{8,10},{9,11},{10,... | collective-permute-start | bytes 3981320 | tf_op jit(solution)/shard_map/ppermute | solution.py:426
  165.3 57.8 %collective-permute-start.21 = (bf16[576,1152]{1,0:T(8,128)(2,1)}, bf16[576,1152]{1,0:T(8,128)(2,1)}, u32[]{:S(2)}, u32[]{:S(2)}) collective-permute-start(bf16[576,1152]{1,0:T(8,128)(2,1)} %collective-permute-done.20.refs_4_), channel_id=1, source_target_pairs={{0,1},{1,0},{2,3},{3,2},{4,5},{5,4},{6,7},{7,6},{8,9},{9,8},{10,11... | collective-permute-start | bytes 3981320 | tf_op jit(solution)/shard_map/ppermute | solution.py:426
  195.5 67.7 %collective-permute-start.11 = (bf16[576,1152]{1,0:T(8,128)(2,1)}, bf16[576,1152]{1,0:T(8,128)(2,1)}, u32[]{:S(2)}, u32[]{:S(2)}) collective-permute-start(bf16[576,1152]{1,0:T(8,128)(2,1)} %collective-permute-done.10.refs_3_), channel_id=1, source_target_pairs={{0,1},{1,0},{2,3},{3,2},{4,5},{5,4},{6,7},{7,6},{8,9},{9,8},{10,11... | collective-permute-start | bytes 3981320 | tf_op jit(solution)/shard_map/ppermute | solution.py:426
  195.5 67.7 %collective-permute-start.15 = (bf16[576,1152]{1,0:T(8,128)(2,1)}, bf16[576,1152]{1,0:T(8,128)(2,1)}, u32[]{:S(2)}, u32[]{:S(2)}) collective-permute-start(bf16[576,1152]{1,0:T(8,128)(2,1)} %collective-permute-done.14.refs_5_), channel_id=1, source_target_pairs={{0,1},{1,0},{2,3},{3,2},{4,5},{5,4},{6,7},{7,6},{8,9},{9,8},{10,11... | collective-permute-start | bytes 3981320 | tf_op jit(solution)/shard_map/ppermute | solution.py:426
  197.1 66.1 %collective-permute-start.13 = (bf16[576,1152]{1,0:T(8,128)(2,1)}, bf16[576,1152]{1,0:T(8,128)(2,1)}, u32[]{:S(2)}, u32[]{:S(2)}) collective-permute-start(bf16[576,1152]{1,0:T(8,128)(2,1)} %collective-permute-done.12.refs_4_), channel_id=1, source_target_pairs={{0,1},{1,0},{2,3},{3,2},{4,5},{5,4},{6,7},{7,6},{8,9},{9,8},{10,11... | collective-permute-start | bytes 3981320 | tf_op jit(solution)/shard_map/ppermute | solution.py:426
  422.6 48.8 %collective-permute-start.51 = (bf16[736,1152]{1,0:T(8,128)(2,1)}, bf16[736,1152]{1,0:T(8,128)(2,1)}, u32[]{:S(2)}, u32[]{:S(2)}) collective-permute-start(bf16[736,1152]{1,0:T(8,128)(2,1)} %get-tuple-element.138), channel_id=1, source_target_pairs={{0,1},{1,0},{2,3},{3,2},{4,5},{5,4},{6,7},{7,6},{8,9},{9,8},{10,11... | collective-permute-start | bytes 5087240 | tf_op jit(solution)/shard_map/ppermute | solution.py:426
  446.5 49.3 %collective-permute-start.42 = (bf16[736,1152]{1,0:T(8,128)(2,1)}, bf16[736,1152]{1,0:T(8,128)(2,1)}, u32[]{:S(2)}, u32[]{:S(2)}) collective-permute-start(bf16[736,1152]{1,0:T(8,128)(2,1)} %get-tuple-element.130), channel_id=1, source_target_pairs={{0,1},{1,0},{2,3},{3,2},{4,5},{5,4},{6,7},{7,6},{8,9},{9,8},{10,11... | collective-permute-start | bytes 5087240 | tf_op jit(solution)/shard_map/ppermute | solution.py:426
  451.3 55.7 %collective-permute-start.44 = (bf16[736,1152]{1,0:T(8,128)(2,1)}, bf16[736,1152]{1,0:T(8,128)(2,1)}, u32[]{:S(2)}, u32[]{:S(2)}) collective-permute-start(bf16[736,1152]{1,0:T(8,128)(2,1)} %get-tuple-element.134), channel_id=1, source_target_pairs={{0,1},{1,0},{2,3},{3,2},{4,5},{5,4},{6,7},{7,6},{8,9},{9,8},{10,11... | collective-permute-start | bytes 5087240 | tf_op jit(solution)/shard_map/ppermute | solution.py:426
  495.8 75.2 %collective-permute-start.53 = (bf16[576,1152]{1,0:T(8,128)(2,1)}, bf16[576,1152]{1,0:T(8,128)(2,1)S(1)}, u32[]{:S(2)}, u32[]{:S(2)}) collective-permute-start(bf16[576,1152]{1,0:T(8,128)(2,1)} %get-tuple-element.142), channel_id=1, source_target_pairs={{0,2},{1,3},{2,0},{3,1},{4,6},{5,7},{6,4},{7,5},{8,10},{9,11},{10,... | collective-permute-start | bytes 3981320 | tf_op jit(solution)/shard_map/ppermute | solution.py:426
  519.1 48.6 %collective-permute-start.45 = (bf16[576,1152]{1,0:T(8,128)(2,1)}, bf16[576,1152]{1,0:T(8,128)(2,1)}, u32[]{:S(2)}, u32[]{:S(2)}) collective-permute-start(bf16[576,1152]{1,0:T(8,128)(2,1)} %get-tuple-element.136), channel_id=1, source_target_pairs={{0,4},{4,0},{1,5},{5,1},{2,6},{6,2},{3,7},{7,3},{8,12},{12,8},{9,1... | collective-permute-start | bytes 3981320 | tf_op jit(solution)/shard_map/ppermute | solution.py:422
  521.1 133.3 %collective-permute-start.43 = (bf16[576,1152]{1,0:T(8,128)(2,1)}, bf16[576,1152]{1,0:T(8,128)(2,1)S(1)}, u32[]{:S(2)}, u32[]{:S(2)}) collective-permute-start(bf16[576,1152]{1,0:T(8,128)(2,1)} %get-tuple-element.132), channel_id=1, source_target_pairs={{0,4},{4,0},{1,5},{5,1},{2,6},{6,2},{3,7},{7,3},{8,12},{12,8},{9,1... | collective-permute-start | bytes 3981320 | tf_op jit(solution)/shard_map/ppermute | solution.py:422
  522.6 102.0 %collective-permute-start.55 = (bf16[576,1152]{1,0:T(8,128)(2,1)}, bf16[576,1152]{1,0:T(8,128)(2,1)}, u32[]{:S(2)}, u32[]{:S(2)}) collective-permute-start(bf16[576,1152]{1,0:T(8,128)(2,1)} %add_convert_fusion.3), channel_id=1, source_target_pairs={{0,4},{4,0},{1,5},{5,1},{2,6},{6,2},{3,7},{7,3},{8,12},{12,8},{9,1... | collective-permute-start | bytes 3981320 | tf_op jit(solution)/shard_map/ppermute | solution.py:422
  539.3 112.8 %collective-permute-start.33 = (bf16[576,1152]{1,0:T(8,128)(2,1)}, bf16[576,1152]{1,0:T(8,128)(2,1)S(1)}, u32[]{:S(2)}, u32[]{:S(2)}) collective-permute-start(bf16[576,1152]{1,0:T(8,128)(2,1)} %get-tuple-element.124), channel_id=1, source_target_pairs={{0,4},{4,0},{1,5},{5,1},{2,6},{6,2},{3,7},{7,3},{8,12},{12,8},{9,1... | collective-permute-start | bytes 3981320 | tf_op jit(solution)/shard_map/ppermute | solution.py:422
  567.7 84.4 %collective-permute-start.37 = (bf16[576,1152]{1,0:T(8,128)(2,1)S(1)}, bf16[576,1152]{1,0:T(8,128)(2,1)S(1)}, u32[]{:S(2)}, u32[]{:S(2)}) collective-permute-start(bf16[576,1152]{1,0:T(8,128)(2,1)S(1)} %add_convert_fusion.9), channel_id=1, source_target_pairs={{0,2},{1,3},{2,0},{3,1},{4,6},{5,7},{6,4},{7,5},{8,10},{9,11},{10,... | collective-permute-start | bytes 3981320 | tf_op jit(solution)/shard_map/ppermute | solution.py:426
  571.0 83.3 %collective-permute-start.46 = (bf16[576,1152]{1,0:T(8,128)(2,1)S(1)}, bf16[576,1152]{1,0:T(8,128)(2,1)S(1)}, u32[]{:S(2)}, u32[]{:S(2)}) collective-permute-start(bf16[576,1152]{1,0:T(8,128)(2,1)S(1)} %add_convert_fusion.6), channel_id=1, source_target_pairs={{0,2},{1,3},{2,0},{3,1},{4,6},{5,7},{6,4},{7,5},{8,10},{9,11},{10,... | collective-permute-start | bytes 3981320 | tf_op jit(solution)/shard_map/ppermute | solution.py:426
  670.7 61.4 %collective-permute-start.39 = (bf16[288,1152]{1,0:T(8,128)(2,1)S(1)}, bf16[288,1152]{1,0:T(8,128)(2,1)S(1)}, u32[]{:S(2)}, u32[]{:S(2)}) collective-permute-start(bf16[288,1152]{1,0:T(8,128)(2,1)S(1)} %add_convert_fusion.16), channel_id=1, source_target_pairs={{0,16},{8,24},{16,0},{24,8},{1,17},{9,25},{17,1},{25,9},{2,18},{10... | collective-permute-start | bytes 1990664 | tf_op jit(solution)/shard_map/ppermute | solution.py:430
  671.4 75.1 %collective-permute-start.57 = (bf16[288,1152]{1,0:T(8,128)(2,1)S(1)}, bf16[288,1152]{1,0:T(8,128)(2,1)S(1)}, u32[]{:S(2)}, u32[]{:S(2)}) collective-permute-start(bf16[288,1152]{1,0:T(8,128)(2,1)S(1)} %add_convert_fusion.12), channel_id=1, source_target_pairs={{0,16},{8,24},{16,0},{24,8},{1,17},{9,25},{17,1},{25,9},{2,18},{10... | collective-permute-start | bytes 1990664 | tf_op jit(solution)/shard_map/ppermute | solution.py:430
  695.2 61.3 %collective-permute-start.48 = (bf16[288,1152]{1,0:T(8,128)(2,1)S(1)}, bf16[288,1152]{1,0:T(8,128)(2,1)S(1)}, u32[]{:S(2)}, u32[]{:S(2)}) collective-permute-start(bf16[288,1152]{1,0:T(8,128)(2,1)S(1)} %add_convert_fusion.14), channel_id=1, source_target_pairs={{0,16},{8,24},{16,0},{24,8},{1,17},{9,25},{17,1},{25,9},{2,18},{10... | collective-permute-start | bytes 1990664 | tf_op jit(solution)/shard_map/ppermute | solution.py:430
  (82 other events, 1458.3 us)

commit v2 on v1

--- a/solution.py
+++ b/solution.py
@@ -51,13 +51,19 @@
 
 def load_rows(copies, blocks, dst):
     n = len(blocks)
-    size = blocks[0].shape[0]
+    size = dst.shape[0] // n
     me = lax.axis_index("row")
     out = []
     for s, block in enumerate(blocks):
-        row = lax.rem(me - s + n, n)
-        out.append(copies(block, dst.at[pl.ds(pl.multiple_of(row * size, 16), size), :]))
+        at = lax.rem(me - s + n, n) * size
+        for piece in block if isinstance(block, (list, tuple)) else (block,):
+            out.append(copies(piece, dst.at[pl.ds(pl.multiple_of(at, 8), piece.shape[0]), :]))
+            at += piece.shape[0]
     return out
+
+
+def nested(refs, shape):
+    return jax.tree.unflatten(shape, refs)
 
 
 def wait(copies):
@@ -68,12 +74,13 @@
 GC = math.sqrt(2.0 / math.pi)
 
 
-def ff_kernel(n, *refs):
+def ff_kernel(shape, *refs):
+    n = shape.num_leaves
     in2, cot, bias = refs[:3]
-    eb, sb = refs[3 : 3 + n], refs[3 + n : 3 + 2 * n]
-    res_in, gi_in = refs[3 + 2 * n : 5 + 2 * n]
-    hid_o, gb_o, res_o, gi_o, db = refs[5 + 2 * n : 10 + 2 * n]
-    in2_v, cot_v, e_v, s_v, hid_v, gb_v, res_v, gi_v, sems = refs[10 + 2 * n :]
+    eb, sb = nested(refs[3 : 3 + n], shape)
+    res_in, gi_in = refs[3 + n : 5 + n]
+    hid_o, gb_o, res_o, gi_o, db = refs[5 + n : 10 + n]
+    in2_v, cot_v, e_v, s_v, hid_v, gb_v, res_v, gi_v, sems = refs[10 + n :]
     c = Copies(sems)
     first = [c(in2, in2_v)] + load_rows(c, eb, e_v)
     second = [c(cot, cot_v)] + load_rows(c, sb, s_v)
@@ -84,7 +91,7 @@
 
     def hidden_tile(at):
         cols = pl.ds(at, 256)
-        b = dot(in2_v[...], e_v[:, cols]) + bias[:, cols]
+        b = dot(in2_v[...], e_v[:, cols]) + bias[1:2, cols]
         sq = b * b
         t = jnp.tanh(GC * b * (1.0 + 0.044715 * sq))
         half = 0.5 * (1.0 + t)
@@ -107,13 +114,14 @@
 
 
 def ff(in2, cot, bias, eb, sb, res, gi):
-    n, (t, d) = len(eb), in2.shape
-    w = eb[0].shape[1]
+    blocks, shape = jax.tree.flatten((eb, sb))
+    n, (t, d) = len(blocks), in2.shape
+    w = blocks[0].shape[1]
     o = jax.ShapeDtypeStruct
     return pl.pallas_call(
-        functools.partial(ff_kernel, n),
+        functools.partial(ff_kernel, shape),
         name="ff",
-        in_specs=[ANY, ANY, VM] + [ANY] * (2 * n + 2),
+        in_specs=[ANY, ANY, VM] + [ANY] * (n + 2),
         out_specs=[ANY] * 4 + [VM],
         out_shape=[o((t, w), BF16), o((t, w), BF16), o((t, d), F32), o((t, d), F32), o((1, w), F32)],
         scratch_shapes=[
@@ -121,12 +129,12 @@
             pltpu.VMEM((d, w), BF16), pltpu.VMEM((d, w), BF16),
             pltpu.VMEM((t, w), BF16), pltpu.VMEM((t, w), BF16),
             pltpu.VMEM((t, d), F32), pltpu.VMEM((t, d), F32),
-            pltpu.SemaphoreType.DMA((2 * n + 8,)),
+            pltpu.SemaphoreType.DMA((n + 8,)),
         ],
-        input_output_aliases={3 + 2 * n: 2, 4 + 2 * n: 3},
+        input_output_aliases={3 + n: 2, 4 + n: 3},
         compiler_params=pltpu.CompilerParams(vmem_limit_bytes=VLIM),
         cost_estimate=pl.CostEstimate(flops=8 * t * d * w, bytes_accessed=4 * d * w + 12 * t * d + 8 * t * d, transcendentals=t * w),
-    )(in2, cot, bias, *eb, *sb, res, gi)
+    )(in2, cot, bias, *blocks, res, gi)
 
 
 def lanes(shape):
@@ -162,9 +170,10 @@
 PENALTY = -1e30
 
 
-def attn_kernel(n, heads, length, chunk, *refs):
+def attn_kernel(shape, heads, length, chunk, *refs):
+    n = shape.num_leaves
     in1, bias = refs[:2]
-    ab = refs[2 : 2 + n]
+    ab = nested(refs[2 : 2 + n], shape)
     mid_in = refs[2 + n]
     q_o, k_o, v_o, att_o, mid_o = refs[3 + n : 8 + n]
     in1_v, a_v, qkv_v, q_v, k_v, v_v, o_v, att_v, mid_v, attb_v, sems = refs[8 + n :]
@@ -176,7 +185,7 @@
 
     def proj(at):
         cols = pl.ds(at, 256)
-        qkv_v[:, cols] = dot(in1_v[...], a_v[:, cols]) + bias[:, cols]
+        qkv_v[:, cols] = dot(in1_v[...], a_v[:, cols]) + bias[0:1, cols]
 
     tiles(7 * LANE, 256, proj)
     lane = lanes((t, LANE))
@@ -226,13 +235,14 @@
 
 
 def attn(in1, bias, ab, mid, length, chunk=368):
-    n, (t, d) = len(ab), in1.shape
-    w = ab[0].shape[1]
+    blocks, shape = jax.tree.flatten(ab)
+    n, (t, d) = len(blocks), in1.shape
+    w = blocks[0].shape[1]
     heads = w // 4 // HEAD
     o = jax.ShapeDtypeStruct
     hs = (heads, t, LANE)
     return pl.pallas_call(
-        functools.partial(attn_kernel, n, heads, length, chunk),
+        functools.partial(attn_kernel, shape, heads, length, chunk),
         name="attn",
         in_specs=[ANY, VM] + [ANY] * (n + 1),
         out_specs=[ANY] * 5,
@@ -246,12 +256,13 @@
         input_output_aliases={2 + n: 4},
         compiler_params=pltpu.CompilerParams(vmem_limit_bytes=VLIM),
         cost_estimate=pl.CostEstimate(flops=2 * t * d * w + 8 * heads * t * t * LANE, bytes_accessed=2 * d * w + 10 * t * d, transcendentals=heads * t * t),
-    )(in1, bias, *ab, mid)
-
-
-def back_kernel(n, heads, chunk, *refs):
+    )(in1, bias, *blocks, mid)
+
+
+def back_kernel(shape, heads, chunk, *refs):
+    n = shape.num_leaves
     gm = refs[0]
-    ab = refs[1 : 1 + n]
+    ab = nested(refs[1 : 1 + n], shape)
     q_i, k_i, v_i, att_i, gi_in = refs[1 + n : 6 + n]
     dqkv_o, gi_o, db = refs[6 + n : 9 + n]
     gm_v, a_v, ga_v, q_v, k_v, v_v, g_v, att_v, ds_v, dq_v, dk_v, dv_v, pack_v, packb_v, gi_v, sems = refs[9 + n :]
@@ -270,9 +281,11 @@
     for j in range(heads):
         at = 3 * LANE - part + HEAD * j
         base = min(at // LANE * LANE, LANE)
+
         def grab(ref):
             window = ref[:, base : base + 2 * LANE]
             return pltpu.roll(window, 2 * LANE - (at - base), 1)[:, :LANE] if at > base else window[:, :LANE]
+
         g = jnp.where(lane < HEAD, grab(ga_v), 0.0).astype(BF16).astype(F32)
         delta = jnp.sum(g * grab(att), axis=1, keepdims=True)
         hi = delta.astype(BF16).astype(F32)
@@ -312,13 +325,14 @@
 
 
 def back(gm, ab, q, k, v, att, gi, chunk=368):
-    n, (t, d) = len(ab), gm.shape
-    w = ab[0].shape[1]
+    blocks, shape = jax.tree.flatten(ab)
+    n, (t, d) = len(blocks), gm.shape
+    w = blocks[0].shape[1]
     heads = q.shape[0]
     o = jax.ShapeDtypeStruct
     hs = (heads, t, LANE)
     return pl.pallas_call(
-        functools.partial(back_kernel, n, heads, chunk),
+        functools.partial(back_kernel, shape, heads, chunk),
         name="back",
         in_specs=[ANY] * (n + 6),
         out_specs=[ANY] * 2 + [VM],
@@ -334,7 +348,7 @@
         input_output_aliases={5 + n: 1},
         compiler_params=pltpu.CompilerParams(vmem_limit_bytes=VLIM),
         cost_estimate=pl.CostEstimate(flops=2 * t * d * w + 20 * heads * t * t * LANE, bytes_accessed=2 * d * w + 16 * t * d, transcendentals=heads * t * t),
-    )(gm, *ab, q, k, v, att, gi)
+    )(gm, *blocks, q, k, v, att, gi)
 
 
 def grads_kernel(n, groups, *refs):
@@ -350,6 +364,7 @@
         cps += [c(ins[4 * i + u], (lhs if u < 2 else rhs)[2 * i + u % 2]) for u in range(4)]
     wait(cps)
     size = outs[0].shape[0]
+    t = rhs[0].shape[0]
     me = lax.axis_index("row")
 
     def step(s, _):
@@ -365,7 +380,7 @@
             def body(at):
                 cols = pl.ds(at, 256)
                 tile_v[slot, :, cols] = (
-                    dot(lhs[0][rows, :], rhs[0][:, cols]) + dot(lhs[1][rows, :], rhs[1][:, cols])
+                    dot(lhs[0][rows, :t], rhs[0][:, cols]) + dot(lhs[1][rows, :t], rhs[1][:, cols])
                 ).astype(BF16)
 
             tiles(groups[0][1], 256, body)
@@ -374,8 +389,8 @@
                 done = 0 if i == 0 else groups[i - 1][0] + groups[i - 1][1]
                 for a in range(0, width, 256):
                     w = min(256, width - a)
-                    value = dot(lhs[2 * i][rows, :], rhs[2 * i][:, a : a + w]) + dot(
-                        lhs[2 * i + 1][rows, :], rhs[2 * i + 1][:, a : a + w]
+                    value = dot(lhs[2 * i][rows, :t], rhs[2 * i][:, a : a + w]) + dot(
+                        lhs[2 * i + 1][rows, :t], rhs[2 * i + 1][:, a : a + w]
                     )
                     at = start + a
                     if at < done:
@@ -398,7 +413,7 @@
     k = len(terms)
     groups = tuple((term[0], term[3].shape[1]) for term in terms)
     flat = [array for term in terms for array in term[1:]]
-    d, t = terms[0][1].shape
+    d, t = terms[0][1].shape[0], terms[0][3].shape[0]
     size = d // n
     scratch = [pltpu.VMEM(term[1].shape, BF16) for term in terms for _ in range(2)]
     scratch += [pltpu.VMEM(term[3].shape, BF16) for term in terms for _ in range(2)]
@@ -418,6 +433,222 @@
     )(*flat)
 
 
+EPS = 1e-6
+ROWS = 16
+
+
+def row_loop(count, body, init):
+    return lax.fori_loop(0, count // ROWS, lambda i, carry: body(pl.ds(pl.multiple_of(i * ROWS, ROWS), ROWS), carry), init, unroll=2 if count // ROWS % 2 == 0 else 3 if count // ROWS % 3 == 0 else 1)
+
+
+def stats(x):
+    average = jnp.mean(x, axis=-1, keepdims=True)
+    second = jnp.mean(x * x, axis=-1, keepdims=True)
+    return average, lax.rsqrt(second - average * average + EPS)
+
+
+def turn(dst, src):
+    if dst.shape[1] > src.shape[0]:
+        dst[...] = jnp.zeros_like(dst)
+    for a in range(0, src.shape[1], LANE):
+        w = min(LANE, src.shape[1] - a)
+        dst[a : a + w, : src.shape[0]] = src[:, a : a + w].T
+
+
+def fold(x):
+    return jnp.sum(x.reshape(x.shape[0] // 8, 8, x.shape[1]), axis=0)
+
+
+def weave_kernel(q, k, v, o, out, all_v):
+    part = q.shape[0]
+    for i, ref in enumerate((q, k, v, o)):
+        all_v[i * part : (i + 1) * part, :] = ref[...]
+    turn(out, all_v)
+
+
+def weave(q, k, v, o):
+    part, size = q.shape
+    return pl.pallas_call(
+        weave_kernel,
+        name="weave",
+        in_specs=[VM] * 4,
+        out_specs=VM,
+        out_shape=jax.ShapeDtypeStruct((size, 4 * part), BF16),
+        scratch_shapes=[pltpu.VMEM((4 * part, size), BF16)],
+    )(q, k, v, o)
+
+
+def unweave_kernel(mine, theirs, q, k, v, o):
+    part = q.shape[0]
+    even = lax.rem(lax.axis_index("dp"), 2) == 0
+    for a in range(0, 4 * part, LANE):
+        first = jnp.where(even, mine[:, a : a + LANE], theirs[:, a : a + LANE])
+        last = jnp.where(even, theirs[:, a : a + LANE], mine[:, a : a + LANE])
+        both = jnp.concatenate((first, last)).astype(F32).T
+        for i, ref in enumerate((q, k, v, o)):
+            lo, hi = max(a, i * part), min(a + LANE, (i + 1) * part)
+            if lo < hi:
+                ref[lo - i * part : hi - i * part, :] = both[lo - a : hi - a, :]
+
+
+def unweave(mine, theirs, part):
+    size = 2 * mine.shape[0]
+    return pl.pallas_call(
+        unweave_kernel,
+        name="unweave",
+        in_specs=[VM] * 2,
+        out_specs=[VM] * 4,
+        out_shape=[jax.ShapeDtypeStruct((part, size), F32)] * 4,
+        compiler_params=pltpu.CompilerParams(vmem_limit_bytes=VLIM),
+    )(mine, theirs)
+
+
+def enter_kernel(x, cot, gain, shift, bias, in1, in1_t, cot_p, cot_t, mid):
+    length, t = x.shape[0], in1.shape[0]
+    whole = length // ROWS * ROWS
+
+    def rows(at, value):
+        value = value.astype(F32)
+        average, inverse = stats(value)
+        in1[at, :] = ((value - average) * inverse * gain[...] + shift[...]).astype(BF16)
+        mid[at, :] = value + bias[...]
+
+    def step(at, _):
+        rows(at, x[at, :])
+        cot_p[at, :] = cot[at, :]
+        return 0
+
+    row_loop(whole, step, 0)
+    if whole < t:
+        last = pl.ds(whole, ROWS)
+        pad = jnp.zeros((t - length, x.shape[1]), F32)
+        rows(last, jnp.concatenate((x[whole:length, :].astype(F32), pad)))
+        cot_p[last, :] = jnp.concatenate((cot[whole:length, :].astype(F32), pad)).astype(BF16)
+    turn(in1_t, in1)
+    turn(cot_t, cot_p)
+
+
+def enter(x, cot, gain, shift, bias, t):
+    d = x.shape[1]
+    tp = -(-t // LANE) * LANE
+    o = jax.ShapeDtypeStruct
+    return pl.pallas_call(
+        enter_kernel,
+        name="enter",
+        in_specs=[VM] * 5,
+        out_specs=[VM] * 5,
+        out_shape=[o((t, d), BF16), o((d, tp), BF16), o((t, d), BF16), o((d, tp), BF16), o((t, d), F32)],
+        compiler_params=pltpu.CompilerParams(vmem_limit_bytes=VLIM),
+    )(x, cot, gain, shift, bias)
+
+
+def middle_kernel(mid, gain, shift, bias, in2, in2_t, res):
+    def step(at, _):
+        value = mid[at, :]
+        average, inverse = stats(value)
+        in2[at, :] = ((value - average) * inverse * gain[...] + shift[...]).astype(BF16)
+        res[at, :] = value + bias[...]
+        return 0
+
+    row_loop(mid.shape[0], step, 0)
+    turn(in2_t, in2)
+
+
+def middle_norm(mid, gain, shift, bias):
+    t, d = mid.shape
+    tp = -(-t // LANE) * LANE
+    o = jax.ShapeDtypeStruct
+    return pl.pallas_call(
+        middle_kernel,
+        name="middle",
+        in_specs=[VM] * 4,
+        out_specs=[VM] * 3,
+        out_shape=[o((t, d), BF16), o((d, tp), BF16), o((t, d), F32)],
+        compiler_params=pltpu.CompilerParams(vmem_limit_bytes=VLIM),
+    )(mid, gain, shift, bias)
+
+
+def back_row(x, grad, gain):
+    average, inverse = stats(x)
+    normed = (x - average) * inverse
+    scaled = grad * gain
+    first = jnp.mean(scaled, axis=-1, keepdims=True)
+    second = jnp.mean(scaled * normed, axis=-1, keepdims=True)
+    return inverse * (scaled - first - normed * second), grad * normed
+
+
+def turn_back_kernel(grad2, mid, cot, gain, gm32, gm, gm_t, sums):
+    d = mid.shape[1]
+    zero = jnp.zeros((8, d), F32)
+
+    def step(at, carry):
+        g, c = grad2[at, :], cot[at, :].astype(F32)
+        inner, product = back_row(mid[at, :], g, gain[...])
+        total = c + inner
+        gm32[at, :] = total
+        gm[at, :] = total.astype(BF16)
+        return tuple(a + fold(b) for a, b in zip(carry, (total, product, g, c)))
+
+    carry = row_loop(mid.shape[0], step, (zero,) * 4)
+    for i, value in enumerate(carry):
+        sums[i : i + 1, :] = jnp.sum(value, axis=0, keepdims=True)
+    turn(gm_t, gm)
+
+
+def turn_back(grad2, mid, cot, gain):
+    t, d = mid.shape
+    tp = -(-t // LANE) * LANE
+    o = jax.ShapeDtypeStruct
+    return pl.pallas_call(
+        turn_back_kernel,
+        name="turnback",
+        in_specs=[VM] * 4,
+        out_specs=[VM] * 4,
+        out_shape=[o((t, d), F32), o((t, d), BF16), o((d, tp), BF16), o((4, d), F32)],
+        compiler_params=pltpu.CompilerParams(vmem_limit_bytes=VLIM),
+    )(grad2, mid, cot, gain)
+
+
+def leave_kernel(grad1, x, gm32, gain, out, sums):
+    length, d = x.shape
+    t = grad1.shape[0]
+    whole = length // ROWS * ROWS
+    zero = jnp.zeros((8, d), F32)
+
+    def rows(at, value, carry):
+        g = grad1[at, :]
+        inner, product = back_row(value, g, gain[...])
+        return gm32[at, :] + inner, tuple(a + fold(b) for a, b in zip(carry, (product, g)))
+
+    def step(at, carry):
+        total, carry = rows(at, x[at, :].astype(F32), carry)
+        out[at, :] = total.astype(BF16)
+        return carry
+
+    carry = row_loop(whole, step, (zero,) * 2)
+    if whole < t:
+        pad = jnp.zeros((t - length, d), F32)
+        total, carry = rows(pl.ds(whole, ROWS), jnp.concatenate((x[whole:length, :].astype(F32), pad)), carry)
+        out[whole:length, :] = total[: length - whole, :].astype(BF16)
+    for i, value in enumerate(carry):
+        sums[i : i + 1, :] = jnp.sum(value, axis=0, keepdims=True)
+
+
+def leave(grad1, x, gm32, gain):
+    o = jax.ShapeDtypeStruct
+    return pl.pallas_call(
+        leave_kernel,
+        name="leave",
+        in_specs=[VM] * 4,
+        out_specs=[VM] * 2,
+        out_shape=[o(x.shape, BF16), o((2, x.shape[1]), F32)],
+        compiler_params=pltpu.CompilerParams(vmem_limit_bytes=VLIM),
+    )(grad1, x, gm32, gain)
+
+
+CORE, SIDE = 1, 2
+
+
 def hop_row(value, shift, size):
     return lax.ppermute(value, "row", [(i, (i + shift) % size) for i in range(size)])
 
@@ -430,58 +661,55 @@
     return lax.ppermute(value, "dp", [(i, i ^ flip) for i in range(4)])
 
 
-CORE, SIDE = 1, 2
-
-
-def gather(block, n, by_row):
-    own = [block] + [hop_row(block, s, n) for s in range(1, n)]
-    side = [hop_col(block, SIDE)]
+def after(value, *first):
+    return lax.optimization_barrier((value, *first))[0]
+
+
+def near(block, n):
+    return [block] + [hop_row(block, s, n) for s in range(1, n)], hop_col(block, SIDE)
+
+
+def diagonal(own, side, n, via):
+    parts = [side]
+    half = side.shape[0] // 2
     for s in range(1, n):
-        side.append(hop_row(side[0], s, n) if by_row else hop_col(own[s], SIDE))
-    return [own, side, [hop_col(b, CORE) for b in own], [hop_col(b, CORE) for b in side]]
+        if via == "row":
+            parts.append(hop_row(side, s, n))
+        elif via == "col":
+            parts.append(hop_col(own[s], SIDE))
+        else:
+            parts.append((hop_row(side[:half], s, n), hop_col(own[s][half:], SIDE)))
+    return parts
+
+
+def across(parts):
+    return [jax.tree.map(lambda b: hop_col(b, CORE), part) for part in parts]
 
 
 def add(a, b):
     return (a.astype(F32) + b.astype(F32)).astype(BF16)
 
 
-def scatter(own, side, n, row_first):
-    def over_row(parts):
-        total = parts[0]
-        for s in range(1, n):
-            total = add(total, hop_row(parts[s], s, n))
-        return total
-
-    if row_first:
-        total = add(over_row(own), hop_col(over_row(side), SIDE))
-    else:
-        total = over_row([add(a, hop_col(b, SIDE)) for a, b in zip(own, side)])
+def over_row(parts, n):
+    total = parts[0]
+    for s in range(1, n):
+        total = add(total, hop_row(parts[s], s, n))
+    return total
+
+
+def over_dp(total):
     half = total.shape[0] // 2
-    z = lax.axis_index("dp")
-    low = lax.rem(z, 2)
+    low = lax.rem(lax.axis_index("dp"), 2)
     mine = lax.dynamic_slice_in_dim(total, low * half, half, 0)
     theirs = lax.dynamic_slice_in_dim(total, (1 - low) * half, half, 0)
     mine = add(mine, hop_dp(theirs, 1))
     mine = add(mine, hop_dp(mine, 2))
-    theirs = hop_dp(mine, 1)
-    return jnp.where(low == 0, jnp.concatenate((mine, theirs)), jnp.concatenate((theirs, mine)))
-
-
-def norm(stream, gain, shift):
-    average = jnp.mean(stream, axis=-1, keepdims=True)
-    second = jnp.mean(stream * stream, axis=-1, keepdims=True)
-    inverse = lax.rsqrt(second - average * average + EPS)
-    return average, inverse, ((stream - average) * inverse * gain + shift).astype(BF16)
-
-
-def norm_back(grad, normed, inverse, gain):
-    scaled = grad * gain
-    first = jnp.mean(scaled, axis=-1, keepdims=True)
-    second = jnp.mean(scaled * normed, axis=-1, keepdims=True)
-    return inverse * (scaled - first - normed * second)
-
-
-EPS = 1e-6
+    return mine, hop_dp(mine, 1)
+
+
+def joined_halves(mine, theirs):
+    even = lax.rem(lax.axis_index("dp"), 2) == 0
+    return jnp.where(even, jnp.concatenate((mine, theirs)), jnp.concatenate((theirs, mine))).astype(F32)
 
 
 def layer(n, images, cotangent, first_gain, first_shift, query_weight, query_bias, key_weight, value_weight, value_bias,
@@ -491,71 +719,96 @@
     part, ff_part = query_weight.shape[1], expand_weight.shape[1]
     wide = 4 * part
     pad_ff = ((0, 0), (0, wide - ff_part))
-    a_own = jnp.concatenate((query_weight, key_weight, value_weight, output_weight.T), axis=1)
+    a_own = weave(query_weight.T, key_weight.T, value_weight.T, output_weight)
+    zeros = jnp.zeros((part,), F32)
+    bias_own = jnp.stack((jnp.concatenate((query_bias, zeros, value_bias, zeros)), jnp.pad(expand_bias, pad_ff[1:])))
+    a_near, a_side = near(a_own, n)
+    bias_side = hop_col(bias_own, SIDE)
+    biases = [bias_own, bias_side, hop_col(bias_own, CORE), hop_col(bias_side, CORE)]
+    row = lambda v: v.reshape(1, -1)
+    images, cotangent = images[0], cotangent[0]
+    input1, in1_t, cot, cot_t, middle = enter(
+        after(images, a_own), cotangent, row(first_gain), row(first_shift), row(output_bias), t)
     e_own = jnp.pad(expand_weight, pad_ff)
     s_own = jnp.pad(shrink_weight.T, pad_ff)
-    zeros = jnp.zeros((part,), F32)
-    bias_own = jnp.stack((jnp.concatenate((query_bias, zeros, value_bias, zeros)), jnp.pad(expand_bias, pad_ff[1:])))
-    a_all = gather(a_own, n, True)
-    bias_side = hop_col(bias_own, SIDE)
-    biases = [bias_own, bias_side, hop_col(bias_own, CORE), hop_col(bias_side, CORE)]
-    e_all = gather(e_own, n, True)
-    s_all = gather(s_own, n, False)
-
-    pad_t = ((0, t - length), (0, 0))
-    stream = jnp.pad(images[0], pad_t).astype(F32)
-    cot = jnp.pad(cotangent[0], pad_t)
-    cot_t = cot.T
-    cot_t2 = hop_col(cot_t, CORE)
-    average1, inverse1, input1 = norm(stream, first_gain, first_shift)
-    in1_t = input1.T
-    in1_t2 = hop_col(in1_t, CORE)
-
-    order = (0, 2, 1, 3)
+
+    a_far = diagonal(a_near, a_side, n, "both")
+    a_all = [a_near, a_far, across(a_near), across(a_far)]
+    e_near, e_side = near(after(e_own, a_side), n)
+    s_near, s_side = near(after(s_own, a_side), n)
+    e_far = diagonal(e_near, e_side, n, "row")
+    s_far = diagonal(s_near, s_side, n, "col")
+    e_all = [e_near, e_far, across(e_near), across(e_far)]
+    s_all = [s_near, s_far, across(s_near), across(s_far)]
+    cot_t2 = hop_col(after(cot_t, a_side), CORE)
+    in1_t2 = hop_col(after(in1_t, a_side), CORE)
+
     kept = {}
-    middle = stream + output_bias
-    for slot in order:
-        *kept[slot], middle = attn(input1, biases[slot][:1], a_all[slot], middle, length)
-    average2, inverse2, input2 = norm(middle, second_gain, second_shift)
-    in2_t = input2.T
+    last = middle
+    for slot in (0, 2, 1, 3):
+        *kept[slot], middle = attn(input1, after(biases[slot], last), a_all[slot], middle, length)
+        last = kept[slot][3]
+    input2, in2_t, result = middle_norm(middle, row(second_gain), row(second_shift), row(shrink_bias))
     in2_t2 = hop_col(in2_t, CORE)
-    result = middle + shrink_bias
+    att2 = [hop_col(kept[s + 2][3], CORE) for s in (0, 1)]
     grad2 = jnp.zeros((t, d), F32)
-    hidden, before, expand_sums = {}, {}, {}
-    for slot in order:
+    hidden, before, expand_sums, ge, gs = {}, {}, {}, {}, {}
+
+    def feed(slot, last, result, grad2):
         hidden[slot], before[slot], result, grad2, expand_sums[slot] = ff(
-            input2, cot, biases[slot][1:], e_all[slot], s_all[slot], result, grad2)
-    ge, gs = [], []
-    for slot in (0, 1):
-        ge.append(grads(n, [(0, in2_t, in2_t2, before[slot], hop_col(before[slot + 2], CORE))], wide))
-        gs.append(grads(n, [(0, cot_t, cot_t2, hidden[slot], hop_col(hidden[slot + 2], CORE))], wide))
-    ge = scatter(ge[0], ge[1], n, True)
-    gs = scatter(gs[0], gs[1], n, False)
-
-    cot32 = cot.astype(F32)
-    normed2 = (middle - average2) * inverse2
-    grad_middle = cot32 + norm_back(grad2, normed2, inverse2, second_gain)
-    gm = grad_middle.astype(BF16)
-    gm_t = gm.T
+            input2, cot, after(biases[slot], last), e_all[slot], s_all[slot], result, grad2)
+        return result, grad2
+
+    def expand_grads(slot, last):
+        other = hop_col(before[slot + 2], CORE)
+        ge[slot] = grads(n, [(0, in2_t, in2_t2, after(before[slot], last), other)], wide)
+        return ge[slot][-1]
+
+    def shrink_grads(slot, last):
+        other = hop_col(hidden[slot + 2], CORE)
+        gs[slot] = grads(n, [(0, cot_t, cot_t2, after(hidden[slot], last), other)], wide)
+        return gs[slot][-1]
+
+    result, grad2 = feed(0, in2_t, result, grad2)
+    result, grad2 = feed(2, expand_sums[0], result, grad2)
+    result, grad2 = feed(1, expand_sums[2], result, grad2)
+    last = expand_grads(0, expand_sums[1])
+    result, grad2 = feed(3, last, result, grad2)
+    last = shrink_grads(0, expand_sums[3])
+    last = shrink_grads(1, last)
+    last = expand_grads(1, last)
+    gm32, gm, gm_t, middle_sums = turn_back(grad2, middle, cot, after(row(second_gain), last))
     gm_t2 = hop_col(gm_t, CORE)
     grad1 = jnp.zeros((t, d), F32)
-    joined, joined_sums = {}, {}
-    for slot in (2, 0, 3, 1):
+    joined, joined_sums, ga = {}, {}, {}
+
+    def attend_back(slot, last, grad1):
         q, k, v, att = kept[slot]
-        joined[slot], grad1, joined_sums[slot] = back(gm, a_all[slot], q, k, v, att, grad1)
-    ga = []
-    for slot in (0, 1):
-        ga.append(grads(n, [
-            (0, in1_t, in1_t2, joined[slot], hop_col(joined[slot + 2], CORE)),
-            (wide - 384, gm_t, gm_t2, kept[slot][3], hop_col(kept[slot + 2][3], CORE)),
-        ], wide))
-    ga = scatter(ga[0], ga[1], n, True)
-    normed1 = (stream - average1) * inverse1
-    grad_stream = grad_middle + norm_back(grad1, normed1, inverse1, first_gain)
-
-    features = jnp.stack([jnp.sum(v, axis=0) for v in (
-        grad1 * normed1, grad1, grad_middle, grad2 * normed2, grad2, cot32)])
+        joined[slot], grad1, joined_sums[slot] = back(gm, a_all[slot], q, k, v, after(att, last), grad1)
+        return grad1
+
+    def joined_grads(slot, last):
+        other = hop_col(joined[slot + 2], CORE)
+        ga[slot] = grads(n, [
+            (0, in1_t, in1_t2, after(joined[slot], last), other),
+            (wide - 384, gm_t, gm_t2, kept[slot][3], att2[slot]),
+        ], wide)
+        return ga[slot][-1]
+
+    grad1 = attend_back(3, middle_sums, grad1)
+    grad1 = attend_back(1, joined_sums[3], grad1)
+    grad1 = attend_back(2, joined_sums[1], grad1)
+    last = joined_grads(1, joined_sums[2])
+    grad1 = attend_back(0, last, grad1)
+    last = joined_grads(0, joined_sums[0])
+
+    e_total = over_dp(add(over_row(ge[0], n), hop_col(over_row(ge[1], n), SIDE)))
+    s_total = over_dp(over_row([add(a, hop_col(b, SIDE)) for a, b in zip(gs[0], gs[1])], n))
+    a_total = over_dp(add(over_row(ga[0], n), hop_col(over_row(ga[1], n), SIDE)))
+    grad_stream, first_sums = leave(grad1, images, gm32, after(row(first_gain), last))
+
     sums = {s: jnp.concatenate((jnp.pad(joined_sums[s], ((0, 0), (0, wide - joined_sums[s].shape[1]))), expand_sums[s])) for s in range(4)}
+    features = jnp.concatenate((first_sums, middle_sums))
     pair = jnp.concatenate((features, sums[0], sums[1])) + hop_col(jnp.concatenate((features, sums[2], sums[3])), CORE)
     one = pair[:8] + hop_col(jnp.concatenate((pair[:6], pair[8:])), SIDE)
     total = one
@@ -563,24 +816,24 @@
         total = total + hop_row(one, s, n)
     for flip in (1, 2):
         total = total + hop_dp(total, flip)
-
+    gq, gk, gv, go = unweave(*a_total, part)
     return (
         result[:length].astype(BF16)[None],
-        grad_stream[:length].astype(BF16)[None],
+        grad_stream[None],
         total[0],
         total[1],
-        ga[:, :part].astype(F32),
+        gq.T,
         total[6, :part],
-        ga[:, part : 2 * part].astype(F32),
-        ga[:, 2 * part : 3 * part].astype(F32),
+        gk.T,
+        gv.T,
         total[6, 2 * part : 3 * part],
-        ga[:, 3 * part :].astype(F32).T,
+        go,
         total[2],
         total[3],
         total[4],
-        ge[:, :ff_part].astype(F32),
+        joined_halves(*e_total)[:, :ff_part],
         total[7, :ff_part],
-        gs[:, :ff_part].astype(F32).T,
+        joined_halves(*s_total)[:, :ff_part].T,
         total[5],
     )
 
@@ -588,8 +841,12 @@
 def solution(mesh):
     batch = P(("dp", "row", "col"), None, None)
     into, out, cols, whole = P("row", "col"), P("col", "row"), P("col"), P()
+
+    def step(*args):
+        return layer(mesh.shape["row"], *args)
+
     return jax.shard_map(
-        functools.partial(layer, mesh.shape["row"]),
+        step,
         mesh=mesh,
         in_specs=(batch, batch, whole, whole, into, cols, into, into, cols, out, whole, whole, whole, into, cols, out, whole),
         out_specs=(batch, batch, whole, whole, into, cols, into, into, cols, out, whole, whole, whole, into, cols, out, whole),

time: 806 us -> 753 us (0.934)
  local copies, waits for them, and re-layouts: 101 us -> 23.2 us
  other arithmetic: 68.5 us -> 7.07 us
  Pallas kernels: 296 us -> 341 us
  waiting for transfers between devices: 283 us -> 321 us
    ppermute x37 -> x39, waiting for transfers between devices: 44.2 us -> 94.5 us  [hop_col(): return lax.ppermute(value, 'col', [(i, i ^ flip) for i in range(4)])]
    pallas_call x12 -> x18, Pallas kernels: 232 us -> 277 us  [the longest x4 82.1 us: ff(): pl.pallas_call(functools.partial(ff_kernel, shape), name='ff', in_specs=[...]
    reduce_sum x7 -> x0, other arithmetic: 24.7 us -> none  [the longest x5 18.5 us: layer(): jnp.sum(v, axis=0)]
    convert_element_type x4 -> x0, local copies, waits for them, and re-layouts: 14.9 us -> none  [the longest x2 5.97 us: norm(): ((stream - average) * inverse * gain + shift).astype(BF16)]
    convert_element_type x5 -> x0, other arithmetic: 14.7 us -> none  [the longest x2 6.26 us: norm(): ((stream - average) * inverse * gain + shift).astype(BF16)]
    pallas_call x3 -> x0, local copies, waits for them, and re-layouts: 13.8 us -> none  [the longest x1 5.31 us: back(): pl.pallas_call(functools.partial(back_kernel, n, heads, chunk), name='bac...]
    ppermute x4 -> x0, local copies, waits for them, and re-layouts: 13.8 us -> none  [hop_col(): return lax.ppermute(value, 'col', [(i, i ^ flip) for i in range(4)])]
    unnamed x105 -> x90, local copies, waits for them, and re-layouts: 17.1 us -> 5.29 us
  transfers between devices with their start and end apart: 59 -> 61, of which waited for: 19 -> 22; matrix products, arithmetic and copies ran while one was open for 13% -> 3% of each run, Pallas kernels for 25% -> 42%
where the time goes in v2:
time: 753 us; the launch traced here: 743 us
  Pallas kernels  341 us (45%)
  waiting for transfers between devices  321 us (43%)
  starting transfers between devices  48.6 us (6%)
  local copies, waits for them, and re-layouts  23.2 us (3%)
    ppermute x11, waiting for transfers between devices, hop_dp(): return lax.ppermute(value, 'dp', [(i, i ^ flip) for i in range(4)])  118 us
    ppermute x11, waiting for transfers between devices, hop_row(): lax.ppermute(value, 'row', [(i, (i + shift) % size) for i in range(size)])  108 us
    ppermute x39, waiting for transfers between devices, hop_col(): return lax.ppermute(value, 'col', [(i, i ^ flip) for i in range(4)])  94.5 us
    pallas_call x4, Pallas kernels, ff(): pl.pallas_call(functools.partial(ff_kernel, shape), name='ff', in_specs=[...  82.1 us
    pallas_call x4, Pallas kernels, back(): pl.pallas_call(functools.partial(back_kernel, shape, heads, chunk), name=...  78.4 us
    pallas_call x4, Pallas kernels, attn(): pl.pallas_call(functools.partial(attn_kernel, shape, heads, length, chunk...  73.5 us
    pallas_call x6, Pallas kernels, grads(): pl.pallas_call(functools.partial(grads_kernel, n, groups), name='grads',...  64.4 us
    ppermute x39, starting transfers between devices, hop_col(): return lax.ppermute(value, 'col', [(i, i ^ flip) for i in range(4)])  22.4 us
  transfers between devices with their start and end apart: 61, of which 22 were waited for; matrix products, arithmetic and copies ran while one was open for 3% of the time, Pallas kernels for 42%

profile of v2, /device:TPU:0, one launch (start us, length us, event | category | flops | bytes accessed | tf_op | source)
XLA Modules:
  0.0 742.6 jit_solution(6157110719583786061)
XLA Ops:
  8.1 27.8 %collective-permute-done.6.refs_2_.refs_1_ = bf16[576,1152]{1,0:T(8,128)(2,1)S(1)} collective-permute-done((bf16[576,1152]{1,0:T(8,128)(2,1)}, bf16[576,1152]{1,0:T(8,128)(2,1)S(1)}, u32[]{:S(2)}, u32[]{:S(2)}) %collective-permute-start.6) | collective-permute-done | bytes 1327136 | tf_op jit(solution)/shard_map/ppermute | solution.py:657
  77.4 18.4 %attn.4 = (bf16[4,736,128]{2,1,0:T(8,128)(2,1)}, bf16[4,736,128]{2,1,0:T(8,128)(2,1)}, bf16[4,736,128]{2,1,0:T(8,128)(2,1)}, bf16[736,384]{1,0:T(8,128)(2,1)}, f32[736,1152]{1,0:T(8,128)}) custom-call(bf16[736,1152]{1,0:T(8,128)(2,1)} %get-tuple-element.125.refs_0_, f32[2,1152]{1,0:T(2,128)} %copy-done.15, ...), custom_call_target="tpu_custom_call", output_to_operand_aliasing={{4}: (4, {})} | custom-call | flops 4172283904 | bytes 11132928 | tf_op jit(solution)/shard_map/attn/pallas_call | solution.py:244
  95.8 18.4 %attn.5 = (bf16[4,736,128]{2,1,0:T(8,128)(2,1)}, bf16[4,736,128]{2,1,0:T(8,128)(2,1)}, bf16[4,736,128]{2,1,0:T(8,128)(2,1)}, bf16[736,384]{1,0:T(8,128)(2,1)}, f32[736,1152]{1,0:T(8,128)}) custom-call(bf16[736,1152]{1,0:T(8,128)(2,1)} %get-tuple-element.125.refs_0_, f32[2,1152]{1,0:T(2,128)} %copy-done.44, ...), custom_call_target="tpu_custom_call", output_to_operand_aliasing={{4}: (4, {})} | custom-call | flops 4172283904 | bytes 11132928 | tf_op jit(solution)/shard_map/attn/pallas_call | solution.py:244
  122.1 18.5 %attn.6 = (bf16[4,736,128]{2,1,0:T(8,128)(2,1)}, bf16[4,736,128]{2,1,0:T(8,128)(2,1)}, bf16[4,736,128]{2,1,0:T(8,128)(2,1)}, bf16[736,384]{1,0:T(8,128)(2,1)}, f32[736,1152]{1,0:T(8,128)}) custom-call(bf16[736,1152]{1,0:T(8,128)(2,1)} %get-tuple-element.125.refs_0_, f32[2,1152]{1,0:T(2,128)} %copy-done.43, ...), custom_call_target="tpu_custom_call", output_to_operand_aliasing={{4}: (5, {})} | custom-call | flops 4172283904 | bytes 11132928 | tf_op jit(solution)/shard_map/attn/pallas_call | solution.py:244
  140.6 18.3 %attn.7 = (bf16[4,736,128]{2,1,0:T(8,128)(2,1)}, bf16[4,736,128]{2,1,0:T(8,128)(2,1)}, bf16[4,736,128]{2,1,0:T(8,128)(2,1)}, bf16[736,384]{1,0:T(8,128)(2,1)}, f32[736,1152]{1,0:T(8,128)}) custom-call(bf16[736,1152]{1,0:T(8,128)(2,1)} %get-tuple-element.125.refs_0_, f32[2,1152]{1,0:T(2,128)} %copy-done.42, ...), custom_call_target="tpu_custom_call", output_to_operand_aliasing={{4}: (5, {})} | custom-call | flops 4172283904 | bytes 11132928 | tf_op jit(solution)/shard_map/attn/pallas_call | solution.py:244
  169.3 21.5 %ff.4 = (bf16[736,1152]{1,0:T(8,128)(2,1)}, bf16[736,1152]{1,0:T(8,128)(2,1)}, f32[736,1152]{1,0:T(8,128)}, f32[736,1152]{1,0:T(8,128)}, f32[1,1152]{1,0:T(1,128)}) custom-call(bf16[736,1152]{1,0:T(8,128)(2,1)} %get-tuple-element.138.refs_0_, bf16[736,1152]{1,0:T(8,128)(2,1)} %get-tuple-element.139.refs_1_.cot, ...), custom_call_target="tpu_custom_call", output_to_operand_aliasing={{2}: (7, {}), {3}: (8, {})} | custom-call | flops 7813988352 | bytes 22265856 | tf_op jit(solution)/shard_map/ff/pallas_call | solution.py:121
  194.4 20.1 %ff.5 = (bf16[736,1152]{1,0:T(8,128)(2,1)}, bf16[736,1152]{1,0:T(8,128)(2,1)}, f32[736,1152]{1,0:T(8,128)}, f32[736,1152]{1,0:T(8,128)}, f32[1,1152]{1,0:T(1,128)}) custom-call(bf16[736,1152]{1,0:T(8,128)(2,1)} %get-tuple-element.138.refs_0_, bf16[736,1152]{1,0:T(8,128)(2,1)} %get-tuple-element.139.refs_1_.cot, ...), custom_call_target="tpu_custom_call", output_to_operand_aliasing={{2}: (7, {}), {3}: (8, {})} | custom-call | flops 7813988352 | bytes 22265856 | tf_op jit(solution)/shard_map/ff/pallas_call | solution.py:121
  223.7 26.8 %collective-permute-done.22.refs_6_ = bf16[576,1152]{1,0:T(8,128)(2,1)} collective-permute-done((bf16[576,1152]{1,0:T(8,128)(2,1)}, bf16[576,1152]{1,0:T(8,128)(2,1)}, u32[]{:S(2)}, u32[]{:S(2)}) %collective-permute-start.22) | collective-permute-done | bytes 1327136 | tf_op jit(solution)/shard_map/ppermute | solution.py:657
  251.0 20.1 %ff.6 = (bf16[736,1152]{1,0:T(8,128)(2,1)}, bf16[736,1152]{1,0:T(8,128)(2,1)}, f32[736,1152]{1,0:T(8,128)}, f32[736,1152]{1,0:T(8,128)}, f32[1,1152]{1,0:T(1,128)}) custom-call(bf16[736,1152]{1,0:T(8,128)(2,1)} %get-tuple-element.138.refs_0_, bf16[736,1152]{1,0:T(8,128)(2,1)} %get-tuple-element.139.refs_1_.cot, ...), custom_call_target="tpu_custom_call", output_to_operand_aliasing={{2}: (7, {}), {3}: (8, {})} | custom-call | flops 7813988352 | bytes 22265856 | tf_op jit(solution)/shard_map/ff/pallas_call | solution.py:121
  282.3 20.5 %ff.7 = (bf16[736,1152]{1,0:T(8,128)(2,1)}, bf16[736,1152]{1,0:T(8,128)(2,1)}, f32[736,1152]{1,0:T(8,128)}, f32[736,1152]{1,0:T(8,128)}, f32[1,1152]{1,0:T(1,128)}) custom-call(bf16[736,1152]{1,0:T(8,128)(2,1)} %get-tuple-element.138.refs_0_, bf16[736,1152]{1,0:T(8,128)(2,1)} %get-tuple-element.139.refs_1_.cot, ...), custom_call_target="tpu_custom_call", output_to_operand_aliasing={{2}: (7, {}), {3}: (8, {})} | custom-call | flops 7813988352 | bytes 22265856 | tf_op jit(solution)/shard_map/ff/pallas_call | solution.py:121
  349.1 19.6 %back.4 = (bf16[736,896]{1,0:T(8,128)(2,1)}, f32[736,1152]{1,0:T(8,128)}, f32[1,896]{1,0:T(1,128)}) custom-call(bf16[736,1152]{1,0:T(8,128)(2,1)} %get-tuple-element.179.refs_0_, bf16[576,1152]{1,0:T(8,128)(2,1)} %collective-permute-done.9.refs_2_.refs_1_, ...), custom_call_target="tpu_custom_call", output_to_operand_aliasing={{1}: (8, {})} | custom-call | flops 7500464128 | bytes 16220160 | tf_op jit(solution)/shard_map/back/pallas_call | solution.py:334
  369.2 19.4 %back.5 = (bf16[736,896]{1,0:T(8,128)(2,1)}, f32[736,1152]{1,0:T(8,128)}, f32[1,896]{1,0:T(1,128)}) custom-call(bf16[736,1152]{1,0:T(8,128)(2,1)} %get-tuple-element.179.refs_0_, bf16[576,1152]{1,0:T(8,128)(2,1)} %copy-done.12, bf16[288,1152]{1,0:T(8,128)(2,1)} %collective-permute-done.7.refs_3_.refs_2_, ...), custom_call_target="tpu_custom_call", output_to_operand_aliasing={{1}: (8, {})} | custom-call | flops 7500464128 | bytes 16220160 | tf_op jit(solution)/shard_map/back/pallas_call | solution.py:334
  388.6 19.7 %back.6 = (bf16[736,896]{1,0:T(8,128)(2,1)}, f32[736,1152]{1,0:T(8,128)}, f32[1,896]{1,0:T(1,128)}) custom-call(bf16[736,1152]{1,0:T(8,128)(2,1)} %get-tuple-element.179.refs_0_, bf16[576,1152]{1,0:T(8,128)(2,1)} %collective-permute-done.4.refs_2_.refs_1_, bf16[576,1152]{1,0:T(8,128)(2,1)} %collective-permute-done.5.refs_3_.refs_2_, ...), custom_call_target="tpu_custom_call", output_to_operand_aliasing={{1}: (7, {})} | custom-call | flops 7500464128 | bytes 16220160 | tf_op jit(solution)/shard_map/back/pallas_call | solution.py:334
  422.1 19.7 %back.7 = (bf16[736,896]{1,0:T(8,128)(2,1)}, f32[736,1152]{1,0:T(8,128)}, f32[1,896]{1,0:T(1,128)}) custom-call(bf16[736,1152]{1,0:T(8,128)(2,1)} %get-tuple-element.179.refs_0_, bf16[576,1152]{1,0:T(8,128)(2,1)} %weave.1.refs_2_.refs_1_, bf16[576,1152]{1,0:T(8,128)(2,1)} %collective-permute-done.3.refs_3_.refs_2_, ...), custom_call_target="tpu_custom_call", output_to_operand_aliasing={{1}: (7, {})} | custom-call | flops 7500464128 | bytes 16220160 | tf_op jit(solution)/shard_map/back/pallas_call | solution.py:334
  468.3 27.4 %collective-permute-done.39 = f32[8,1152]{1,0:T(8,128)S(1)} collective-permute-done((f32[8,1152]{1,0:T(8,128)S(1)}, f32[8,1152]{1,0:T(8,128)S(1)}, u32[]{:S(2)}, u32[]{:S(2)}) %collective-permute-start.39) | collective-permute-done | bytes 36896 | tf_op jit(solution)/shard_map/ppermute | solution.py:657
  502.2 24.2 %collective-permute-done.40 = f32[8,1152]{1,0:T(8,128)S(1)} collective-permute-done((f32[8,1152]{1,0:T(8,128)S(1)}, f32[8,1152]{1,0:T(8,128)S(1)}, u32[]{:S(2)}, u32[]{:S(2)}) %collective-permute-start.40) | collective-permute-done | bytes 36896 | tf_op jit(solution)/shard_map/ppermute | solution.py:653
  540.9 17.8 %collective-permute-done.44 = bf16[576,1152]{1,0:T(8,128)(2,1)S(1)} collective-permute-done((bf16[576,1152]{1,0:T(8,128)(2,1)}, bf16[576,1152]{1,0:T(8,128)(2,1)S(1)}, u32[]{:S(2)}, u32[]{:S(2)}) %collective-permute-start.44) | collective-permute-done | bytes 1327136 | tf_op jit(solution)/shard_map/ppermute | solution.py:653
  562.1 25.0 %collective-permute-done.57 = bf16[576,1152]{1,0:T(8,128)(2,1)S(1)} collective-permute-done((bf16[576,1152]{1,0:T(8,128)(2,1)S(1)}, bf16[576,1152]{1,0:T(8,128)(2,1)S(1)}, u32[]{:S(2)}, u32[]{:S(2)}) %collective-permute-start.57) | collective-permute-done | bytes 1327136 | tf_op jit(solution)/shard_map/ppermute | solution.py:653
  591.1 22.5 %collective-permute-done.43 = bf16[576,1152]{1,0:T(8,128)(2,1)S(1)} collective-permute-done((bf16[576,1152]{1,0:T(8,128)(2,1)S(1)}, bf16[576,1152]{1,0:T(8,128)(2,1)S(1)}, u32[]{:S(2)}, u32[]{:S(2)}) %collective-permute-start.43) | collective-permute-done | bytes 1327136 | tf_op jit(solution)/shard_map/ppermute | solution.py:653
  619.2 23.9 %collective-permute-done.46 = bf16[288,1152]{1,0:T(8,128)(2,1)S(1)} collective-permute-done((bf16[288,1152]{1,0:T(8,128)(2,1)S(1)}, bf16[288,1152]{1,0:T(8,128)(2,1)S(1)}, u32[]{:S(2)}, u32[]{:S(2)}) %collective-permute-start.46) | collective-permute-done | bytes 663584 | tf_op jit(solution)/shard_map/ppermute | solution.py:661
  643.8 33.5 %collective-permute-done.59 = bf16[288,1152]{1,0:T(8,128)(2,1)S(1)} collective-permute-done((bf16[288,1152]{1,0:T(8,128)(2,1)S(1)}, bf16[288,1152]{1,0:T(8,128)(2,1)S(1)}, u32[]{:S(2)}, u32[]{:S(2)}) %collective-permute-start.59) | collective-permute-done | bytes 663584 | tf_op jit(solution)/shard_map/ppermute | solution.py:661
  677.6 14.1 %collective-permute-done.53 = bf16[288,1152]{1,0:T(8,128)(2,1)S(1)} collective-permute-done((bf16[288,1152]{1,0:T(8,128)(2,1)S(1)}, bf16[288,1152]{1,0:T(8,128)(2,1)S(1)}, u32[]{:S(2)}, u32[]{:S(2)}) %collective-permute-start.53) | collective-permute-done | bytes 663584 | tf_op jit(solution)/shard_map/ppermute | solution.py:661
  703.1 13.7 %collective-permute-done.60 = bf16[288,1152]{1,0:T(8,128)(2,1)S(1)} collective-permute-done((bf16[288,1152]{1,0:T(8,128)(2,1)S(1)}, bf16[288,1152]{1,0:T(8,128)(2,1)S(1)}, u32[]{:S(2)}, u32[]{:S(2)}) %collective-permute-start.60) | collective-permute-done | bytes 663584 | tf_op jit(solution)/shard_map/ppermute | solution.py:661
  718.6 12.5 %collective-permute-done.54 = bf16[288,1152]{1,0:T(8,128)(2,1)S(1)} collective-permute-done((bf16[288,1152]{1,0:T(8,128)(2,1)S(1)}, bf16[288,1152]{1,0:T(8,128)(2,1)S(1)}, u32[]{:S(2)}, u32[]{:S(2)}) %collective-permute-start.54) | collective-permute-done | bytes 663584 | tf_op jit(solution)/shard_map/ppermute | solution.py:661
  (265 shorter events, 237.4 us)
Async XLA Ops:
  8.1 54.5 %collective-permute-start.4 = (bf16[576,1152]{1,0:T(8,128)(2,1)}, bf16[576,1152]{1,0:T(8,128)(2,1)}, u32[]{:S(2)}, u32[]{:S(2)}) collective-permute-start(bf16[576,1152]{1,0:T(8,128)(2,1)} %weave.1.refs_2_.refs_1_), channel_id=1, source_target_pairs={{0,1},{1,0},{2,3},{3,2},{4,5},{5,4},{6,7},{7,6},{8,9},{9,8},{10,11... | collective-permute-start | bytes 3981320 | tf_op jit(solution)/shard_map/ppermute | solution.py:657
  64.0 58.1 %collective-permute-start.13 = (bf16[576,1152]{1,0:T(8,128)(2,1)}, bf16[576,1152]{1,0:T(8,128)(2,1)S(1)}, u32[]{:S(2)}, u32[]{:S(2)}) collective-permute-start(bf16[576,1152]{1,0:T(8,128)(2,1)} %pad.25.refs_3_), channel_id=1, source_target_pairs={{0,4},{4,0},{1,5},{5,1},{2,6},{6,2},{3,7},{7,3},{8,12},{12,8},{9,1... | collective-permute-start | bytes 3981320 | tf_op jit(solution)/shard_map/ppermute | solution.py:653
  76.9 89.9 %collective-permute-start.15 = (bf16[576,1152]{1,0:T(8,128)(2,1)}, bf16[576,1152]{1,0:T(8,128)(2,1)}, u32[]{:S(2)}, u32[]{:S(2)}) collective-permute-start(bf16[576,1152]{1,0:T(8,128)(2,1)} %pad.25.refs_3_), channel_id=1, source_target_pairs={{0,1},{1,0},{2,3},{3,2},{4,5},{5,4},{6,7},{7,6},{8,9},{9,8},{10,11... | collective-permute-start | bytes 3981320 | tf_op jit(solution)/shard_map/ppermute | solution.py:657
  114.1 76.7 %collective-permute-start.17 = (bf16[576,1152]{1,0:T(8,128)(2,1)S(1)}, bf16[576,1152]{1,0:T(8,128)(2,1)}, u32[]{:S(2)}, u32[]{:S(2)}) collective-permute-start(bf16[576,1152]{1,0:T(8,128)(2,1)S(1)} %pad.26.refs_5_), channel_id=1, source_target_pairs={{0,1},{1,0},{2,3},{3,2},{4,5},{5,4},{6,7},{7,6},{8,9},{9,8},{10,11... | collective-permute-start | bytes 3981320 | tf_op jit(solution)/shard_map/ppermute | solution.py:657
  114.3 78.1 %collective-permute-start.19 = (bf16[576,1152]{1,0:T(8,128)(2,1)}, bf16[576,1152]{1,0:T(8,128)(2,1)}, u32[]{:S(2)}, u32[]{:S(2)}) collective-permute-start(bf16[576,1152]{1,0:T(8,128)(2,1)} %pad.25.refs_3_), channel_id=1, source_target_pairs={{0,2},{1,3},{2,0},{3,1},{4,6},{5,7},{6,4},{7,5},{8,10},{9,11},{10,... | collective-permute-start | bytes 3981320 | tf_op jit(solution)/shard_map/ppermute | solution.py:657
  115.8 77.1 %collective-permute-start.18 = (bf16[576,1152]{1,0:T(8,128)(2,1)}, bf16[576,1152]{1,0:T(8,128)(2,1)}, u32[]{:S(2)}, u32[]{:S(2)}) collective-permute-start(bf16[576,1152]{1,0:T(8,128)(2,1)} %collective-permute-done.14.refs_6_), channel_id=1, source_target_pairs={{0,1},{1,0},{2,3},{3,2},{4,5},{5,4},{6,7},{7,6},{8,9},{9,8},{10,11... | collective-permute-start | bytes 3981320 | tf_op jit(solution)/shard_map/ppermute | solution.py:657
  122.1 72.3 %collective-permute-start.16 = (bf16[576,1152]{1,0:T(8,128)(2,1)S(1)}, bf16[576,1152]{1,0:T(8,128)(2,1)}, u32[]{:S(2)}, u32[]{:S(2)}) collective-permute-start(bf16[576,1152]{1,0:T(8,128)(2,1)S(1)} %collective-permute-done.13.refs_4_), channel_id=1, source_target_pairs={{0,1},{1,0},{2,3},{3,2},{4,5},{5,4},{6,7},{7,6},{8,9},{9,8},{10,11... | collective-permute-start | bytes 3981320 | tf_op jit(solution)/shard_map/ppermute | solution.py:657
  166.8 83.7 %collective-permute-start.12 = (bf16[1152,768]{1,0:T(8,128)(2,1)}, bf16[1152,768]{1,0:T(8,128)(2,1)}, u32[]{:S(2)}, u32[]{:S(2)}) collective-permute-start(bf16[1152,768]{1,0:T(8,128)(2,1)} %get-tuple-element.140.refs_0_), channel_id=1, source_target_pairs={{0,1},{1,0},{2,3},{3,2},{4,5},{5,4},{6,7},{7,6},{8,9},{9,8},{10,11... | collective-permute-start | bytes 5308424 | tf_op jit(solution)/shard_map/ppermute | solution.py:657
  192.4 58.1 %collective-permute-start.22 = (bf16[576,1152]{1,0:T(8,128)(2,1)}, bf16[576,1152]{1,0:T(8,128)(2,1)}, u32[]{:S(2)}, u32[]{:S(2)}) collective-permute-start(bf16[576,1152]{1,0:T(8,128)(2,1)} %collective-permute-done.14.refs_6_), channel_id=1, source_target_pairs={{0,2},{1,3},{2,0},{3,1},{4,6},{5,7},{6,4},{7,5},{8,10},{9,11},{10,... | collective-permute-start | bytes 3981320 | tf_op jit(solution)/shard_map/ppermute | solution.py:657
  214.5 56.6 %collective-permute-start.23 = (bf16[736,1152]{1,0:T(8,128)(2,1)}, bf16[736,1152]{1,0:T(8,128)(2,1)}, u32[]{:S(2)}, u32[]{:S(2)}) collective-permute-start(bf16[736,1152]{1,0:T(8,128)(2,1)} %get-tuple-element.156), channel_id=1, source_target_pairs={{0,1},{1,0},{2,3},{3,2},{4,5},{5,4},{6,7},{7,6},{8,9},{9,8},{10,11... | collective-permute-start | bytes 5087240 | tf_op jit(solution)/shard_map/ppermute | solution.py:657
  222.9 58.8 %collective-permute-start.24 = (bf16[576,1152]{1,0:T(8,128)(2,1)}, bf16[576,1152]{1,0:T(8,128)(2,1)}, u32[]{:S(2)}, u32[]{:S(2)}) collective-permute-start(bf16[576,1152]{1,0:T(8,128)(2,1)} %collective-permute-done.19.refs_3_), channel_id=1, source_target_pairs={{0,1},{1,0},{2,3},{3,2},{4,5},{5,4},{6,7},{7,6},{8,9},{9,8},{10,11... | collective-permute-start | bytes 3981320 | tf_op jit(solution)/shard_map/ppermute | solution.py:657
  223.7 58.6 %collective-permute-start.26 = (bf16[576,1152]{1,0:T(8,128)(2,1)S(1)}, bf16[576,1152]{1,0:T(8,128)(2,1)}, u32[]{:S(2)}, u32[]{:S(2)}) collective-permute-start(bf16[576,1152]{1,0:T(8,128)(2,1)S(1)} %collective-permute-done.21.refs_5_), channel_id=1, source_target_pairs={{0,1},{1,0},{2,3},{3,2},{4,5},{5,4},{6,7},{7,6},{8,9},{9,8},{10,11... | collective-permute-start | bytes 3981320 | tf_op jit(solution)/shard_map/ppermute | solution.py:657
  303.4 105.9 %collective-permute-start.32 = (bf16[1152,768]{1,0:T(8,128)(2,1)S(1)}, bf16[1152,768]{1,0:T(8,128)(2,1)}, u32[]{:S(2)}, u32[]{:S(2)}) collective-permute-start(bf16[1152,768]{1,0:T(8,128)(2,1)S(1)} %copy-done.32), channel_id=1, source_target_pairs={{0,1},{1,0},{2,3},{3,2},{4,5},{5,4},{6,7},{7,6},{8,9},{9,8},{10,11... | collective-permute-start | bytes 5308424 | tf_op jit(solution)/shard_map/ppermute | solution.py:657
  303.4 106.3 %collective-permute-start.35 = (bf16[736,384]{1,0:T(8,128)(2,1)}, bf16[736,384]{1,0:T(8,128)(2,1)}, u32[]{:S(2)}, u32[]{:S(2)}) collective-permute-start(bf16[736,384]{1,0:T(8,128)(2,1)} %get-tuple-element.193.refs_7_), channel_id=1, source_target_pairs={{0,1},{1,0},{2,3},{3,2},{4,5},{5,4},{6,7},{7,6},{8,9},{9,8},{10,11... | collective-permute-start | bytes 1695752 | tf_op jit(solution)/shard_map/ppermute | solution.py:657
  347.0 62.7 %collective-permute-start.34 = (bf16[1152,768]{1,0:T(8,128)(2,1)}, bf16[1152,768]{1,0:T(8,128)(2,1)S(1)}, u32[]{:S(2)}, u32[]{:S(2)}) collective-permute-start(bf16[1152,768]{1,0:T(8,128)(2,1)} %get-tuple-element.207.refs_4_), channel_id=1, source_target_pairs={{0,1},{1,0},{2,3},{3,2},{4,5},{5,4},{6,7},{7,6},{8,9},{9,8},{10,11... | collective-permute-start | bytes 5308424 | tf_op jit(solution)/shard_map/ppermute | solution.py:657
  463.3 64.6 %collective-permute-start.56 = (bf16[576,1152]{1,0:T(8,128)(2,1)}, bf16[576,1152]{1,0:T(8,128)(2,1)S(1)}, u32[]{:S(2)}, u32[]{:S(2)}) collective-permute-start(bf16[576,1152]{1,0:T(8,128)(2,1)} %get-tuple-element.174), channel_id=1, source_target_pairs={{0,2},{1,3},{2,0},{3,1},{4,6},{5,7},{6,4},{7,5},{8,10},{9,11},{10,... | collective-permute-start | bytes 3981320 | tf_op jit(solution)/shard_map/ppermute | solution.py:657
  466.3 123.0 %collective-permute-start.49 = (bf16[576,1152]{1,0:T(8,128)(2,1)S(1)}, bf16[576,1152]{1,0:T(8,128)(2,1)S(1)}, u32[]{:S(2)}, u32[]{:S(2)}) collective-permute-start(bf16[576,1152]{1,0:T(8,128)(2,1)S(1)} %copy-done.35), channel_id=1, source_target_pairs={{0,4},{4,0},{1,5},{5,1},{2,6},{6,2},{3,7},{7,3},{8,12},{12,8},{9,1... | collective-permute-start | bytes 3981320 | tf_op jit(solution)/shard_map/ppermute | solution.py:653
  467.7 64.8 %collective-permute-start.50 = (bf16[576,1152]{1,0:T(8,128)(2,1)}, bf16[576,1152]{1,0:T(8,128)(2,1)S(1)}, u32[]{:S(2)}, u32[]{:S(2)}) collective-permute-start(bf16[576,1152]{1,0:T(8,128)(2,1)} %get-tuple-element.177), channel_id=1, source_target_pairs={{0,4},{4,0},{1,5},{5,1},{2,6},{6,2},{3,7},{7,3},{8,12},{12,8},{9,1... | collective-permute-start | bytes 3981320 | tf_op jit(solution)/shard_map/ppermute | solution.py:653
  500.7 59.8 %collective-permute-start.55 = (bf16[576,1152]{1,0:T(8,128)(2,1)S(1)}, bf16[576,1152]{1,0:T(8,128)(2,1)S(1)}, u32[]{:S(2)}, u32[]{:S(2)}) collective-permute-start(bf16[576,1152]{1,0:T(8,128)(2,1)S(1)} %copy-done.36), channel_id=1, source_target_pairs={{0,2},{1,3},{2,0},{3,1},{4,6},{5,7},{6,4},{7,5},{8,10},{9,11},{10,... | collective-permute-start | bytes 3981320 | tf_op jit(solution)/shard_map/ppermute | solution.py:657
  531.9 55.2 %collective-permute-start.57 = (bf16[576,1152]{1,0:T(8,128)(2,1)S(1)}, bf16[576,1152]{1,0:T(8,128)(2,1)S(1)}, u32[]{:S(2)}, u32[]{:S(2)}) collective-permute-start(bf16[576,1152]{1,0:T(8,128)(2,1)S(1)} %add_convert_fusion.1), channel_id=1, source_target_pairs={{0,4},{4,0},{1,5},{5,1},{2,6},{6,2},{3,7},{7,3},{8,12},{12,8},{9,1... | collective-permute-start | bytes 3981320 | tf_op jit(solution)/shard_map/ppermute | solution.py:653
  558.7 54.9 %collective-permute-start.43 = (bf16[576,1152]{1,0:T(8,128)(2,1)S(1)}, bf16[576,1152]{1,0:T(8,128)(2,1)S(1)}, u32[]{:S(2)}, u32[]{:S(2)}) collective-permute-start(bf16[576,1152]{1,0:T(8,128)(2,1)S(1)} %copy-done.37), channel_id=1, source_target_pairs={{0,4},{4,0},{1,5},{5,1},{2,6},{6,2},{3,7},{7,3},{8,12},{12,8},{9,1... | collective-permute-start | bytes 3981320 | tf_op jit(solution)/shard_map/ppermute | solution.py:653
  615.9 61.4 %collective-permute-start.59 = (bf16[288,1152]{1,0:T(8,128)(2,1)S(1)}, bf16[288,1152]{1,0:T(8,128)(2,1)S(1)}, u32[]{:S(2)}, u32[]{:S(2)}) collective-permute-start(bf16[288,1152]{1,0:T(8,128)(2,1)S(1)} %add_convert_fusion.10), channel_id=1, source_target_pairs={{0,16},{8,24},{16,0},{24,8},{1,17},{9,25},{17,1},{25,9},{2,18},{10... | collective-permute-start | bytes 1990664 | tf_op jit(solution)/shard_map/ppermute | solution.py:661
  618.8 72.9 %collective-permute-start.53 = (bf16[288,1152]{1,0:T(8,128)(2,1)S(1)}, bf16[288,1152]{1,0:T(8,128)(2,1)S(1)}, u32[]{:S(2)}, u32[]{:S(2)}) collective-permute-start(bf16[288,1152]{1,0:T(8,128)(2,1)S(1)} %add_convert_fusion.12), channel_id=1, source_target_pairs={{0,16},{8,24},{16,0},{24,8},{1,17},{9,25},{17,1},{25,9},{2,18},{10... | collective-permute-start | bytes 1990664 | tf_op jit(solution)/shard_map/ppermute | solution.py:661
  643.2 59.6 %collective-permute-start.47 = (bf16[288,1152]{1,0:T(8,128)(2,1)S(1)}, bf16[288,1152]{1,0:T(8,128)(2,1)S(1)}, u32[]{:S(2)}, u32[]{:S(2)}) collective-permute-start(bf16[288,1152]{1,0:T(8,128)(2,1)S(1)} %add_convert_fusion.14), channel_id=1, source_target_pairs={{0,16},{8,24},{16,0},{24,8},{1,17},{9,25},{17,1},{25,9},{2,18},{10... | collective-permute-start | bytes 1990664 | tf_op jit(solution)/shard_map/ppermute | solution.py:661
  (82 other events, 1740.8 us)

commit v3 on v1

v3 whole, which is shorter than its diff:
```python
import functools, math
import jax
import jax.numpy as jnp
from jax import lax
from jax.experimental import pallas as pl
from jax.experimental.pallas import tpu as pltpu
from jax.sharding import PartitionSpec as P

HEAD = 72
LANE = 128
F32, BF16 = jnp.float32, jnp.bfloat16
NT = (((1,), (1,)), ((), ()))
TN = (((0,), (0,)), ((), ()))
ANY = pl.BlockSpec(memory_space=pl.ANY)
VM = pl.BlockSpec(memory_space=pltpu.VMEM)
VLIM = 60 * 1024 * 1024


def dot(a, b):
    return jnp.dot(a, b, preferred_element_type=F32)


def dot_nt(a, b):
    return lax.dot_general(a, b, NT, preferred_element_type=F32)


def dot_tn(a, b):
    return lax.dot_general(a, b, TN, preferred_element_type=F32)


def tiles(total, width, body):
    count = -(-total // width)

    def step(i, _):
        body(pl.multiple_of(jnp.minimum(i * width, total - width), LANE))
        return 0

    lax.fori_loop(0, count, step, 0)


class Copies:
    def __init__(self, sems):
        self.sems, self.n = sems, 0

    def __call__(self, src, dst):
        copy = pltpu.make_async_copy(src, dst, self.sems.at[self.n])
        self.n += 1
        copy.start()
        return copy


def load_rows(copies, blocks, dst):
    n = len(blocks)
    size = dst.shape[0] // n
    me = lax.axis_index("row")
    out = []
    for s, block in enumerate(blocks):
        at = lax.rem(me - s + n, n) * size
        for piece in block if isinstance(block, (list, tuple)) else (block,):
            out.append(copies(piece, dst.at[pl.ds(pl.multiple_of(at, 8), piece.shape[0]), :]))
            at += piece.shape[0]
    return out


def nested(refs, shape):
    return jax.tree.unflatten(shape, refs)


def wait(copies):
    for copy in copies:
        copy.wait()


EPS = 1e-6
ROWS = 16


def row_loop(count, body, init):
    return lax.fori_loop(0, count // ROWS, lambda i, carry: body(pl.ds(pl.multiple_of(i * ROWS, ROWS), ROWS), carry), init, unroll=2 if count // ROWS % 2 == 0 else 3 if count // ROWS % 3 == 0 else 1)


def stats(x):
    average = jnp.mean(x, axis=-1, keepdims=True)
    second = jnp.mean(x * x, axis=-1, keepdims=True)
    return average, lax.rsqrt(second - average * average + EPS)


def turn(dst, src):
    if dst.shape[1] > src.shape[0]:
        dst[...] = jnp.zeros_like(dst)
    for a in range(0, src.shape[1], LANE):
        w = min(LANE, src.shape[1] - a)
        dst[a : a + w, : src.shape[0]] = src[:, a : a + w].T


def fold(x):
    return jnp.sum(x.reshape(x.shape[0] // 8, 8, x.shape[1]), axis=0)


def weave_kernel(q, k, v, o, out, all_v):
    part = q.shape[0]
    for i, ref in enumerate((q, k, v, o)):
        all_v[i * part : (i + 1) * part, :] = ref[...]
    turn(out, all_v)


def weave(q, k, v, o):
    part, size = q.shape
    return pl.pallas_call(
        weave_kernel,
        name="weave",
        in_specs=[VM] * 4,
        out_specs=VM,
        out_shape=jax.ShapeDtypeStruct((size, 4 * part), BF16),
        scratch_shapes=[pltpu.VMEM((4 * part, size), BF16)],
    )(q, k, v, o)


def unweave_kernel(*refs):
    pieces, (q, k, v, o) = refs[:-4], refs[-4:]
    part = q.shape[0]
    even = lax.rem(lax.axis_index("dp"), 2) == 0
    for a in range(0, 4 * part, LANE):
        cols = slice(a, a + LANE)
        rows = []
        for i in range(0, len(pieces), 2):
            mine, theirs = pieces[i][:, cols].astype(F32), pieces[i + 1][:, cols].astype(F32)
            rows += [jnp.where(even, mine, theirs), jnp.where(even, theirs, mine)]
        both = jnp.concatenate(rows).T
        for i, ref in enumerate((q, k, v, o)):
            lo, hi = max(a, i * part), min(a + LANE, (i + 1) * part)
            if lo < hi:
                ref[lo - i * part : hi - i * part, :] = both[lo - a : hi - a, :]


def unweave(pieces, part):
    flat = [piece for pair in pieces for piece in pair]
    return pl.pallas_call(
        unweave_kernel,
        name="unweave",
        in_specs=[VM] * len(flat),
        out_specs=[VM] * 4,
        out_shape=[jax.ShapeDtypeStruct((part, sum(piece.shape[0] for piece in flat)), F32)] * 4,
        compiler_params=pltpu.CompilerParams(vmem_limit_bytes=VLIM),
    )(*flat)


def enter_kernel(x, cot, gain, shift, bias, in1, in1_t, cot_p, cot_t, mid):
    length, t = x.shape[0], in1.shape[0]
    whole = length // ROWS * ROWS

    def rows(at, value):
        value = value.astype(F32)
        average, inverse = stats(value)
        in1[at, :] = ((value - average) * inverse * gain[...] + shift[...]).astype(BF16)
        mid[at, :] = value + bias[...]

    def step(at, _):
        rows(at, x[at, :])
        cot_p[at, :] = cot[at, :]
        return 0

    row_loop(whole, step, 0)
    if whole < t:
        last = pl.ds(whole, ROWS)
        pad = jnp.zeros((t - length, x.shape[1]), F32)
        rows(last, jnp.concatenate((x[whole:length, :].astype(F32), pad)))
        cot_p[last, :] = jnp.concatenate((cot[whole:length, :].astype(F32), pad)).astype(BF16)
    turn(in1_t, in1)
    turn(cot_t, cot_p)


def enter(x, cot, gain, shift, bias, t):
    d = x.shape[1]
    tp = -(-t // LANE) * LANE
    o = jax.ShapeDtypeStruct
    return pl.pallas_call(
        enter_kernel,
        name="enter",
        in_specs=[VM] * 5,
        out_specs=[VM] * 5,
        out_shape=[o((t, d), BF16), o((d, tp), BF16), o((t, d), BF16), o((d, tp), BF16), o((t, d), F32)],
        compiler_params=pltpu.CompilerParams(vmem_limit_bytes=VLIM),
    )(x, cot, gain, shift, bias)


def back_row(x, grad, gain):
    average, inverse = stats(x)
    normed = (x - average) * inverse
    scaled = grad * gain
    first = jnp.mean(scaled, axis=-1, keepdims=True)
    second = jnp.mean(scaled * normed, axis=-1, keepdims=True)
    return inverse * (scaled - first - normed * second), grad * normed


def leave_body(grad1, x, gm32, gain, out, sums):
    length, d = x.shape
    t = grad1.shape[0]
    whole = length // ROWS * ROWS
    zero = jnp.zeros((8, d), F32)

    def rows(at, value, carry):
        g = grad1[at, :]
        inner, product = back_row(value, g, gain[...])
        return gm32[at, :] + inner, tuple(a + fold(b) for a, b in zip(carry, (product, g)))

    def step(at, carry):
        total, carry = rows(at, x[at, :].astype(F32), carry)
        out[at, :] = total.astype(BF16)
        return carry

    carry = row_loop(whole, step, (zero,) * 2)
    if whole < t:
        pad = jnp.zeros((t - length, d), F32)
        total, carry = rows(pl.ds(whole, ROWS), jnp.concatenate((x[whole:length, :].astype(F32), pad)), carry)
        out[whole:length, :] = total[: length - whole, :].astype(BF16)
    for i, value in enumerate(carry):
        sums[i : i + 1, :] = jnp.sum(value, axis=0, keepdims=True)


def lanes(shape):
    return lax.broadcasted_iota(jnp.int32, shape, 1)


def pick(ref, at):
    base = min(at // LANE * LANE, ref.shape[1] - 2 * LANE)
    window = ref[:, base : base + 2 * LANE]
    shift = at - base
    if shift:
        window = pltpu.roll(window, 2 * LANE - shift, 1)
    return window[:, :LANE]


def put(ref, at, value):
    base = min(at // LANE * LANE, ref.shape[1] - 2 * LANE)
    wide = jnp.concatenate((value, jnp.zeros_like(value)), axis=1)
    if at - base:
        wide = pltpu.roll(wide, at - base, 1)
    ref[:, base : base + 2 * LANE] += wide


def split3(value):
    hi = value.astype(BF16).astype(F32)
    rest = value - hi
    mid = rest.astype(BF16).astype(F32)
    return hi, mid, rest - mid


SCALE = HEAD ** -0.5
C2 = SCALE * math.log2(math.e)
PENALTY = -1e30


def attn_kernel(shapes, heads, length, chunk, group, final, *refs):
    n = shapes.num_leaves
    in1, mid_in, gain, shift = refs[:4]
    bias = refs[4:6]
    ab = nested(refs[6 : 6 + n], shapes)
    rest = refs[6 + n :]
    q_o, k_o, v_o, att_o = rest[0:2], rest[2:4], rest[4:6], rest[6:8]
    mid_o = rest[8]
    outs = 11 if final else 9
    in2_o, in2t_o = rest[9:11] if final else (None, None)
    in1_v, a_v, qkv_v, q_v, k_v, v_v, o_v, att_v, mid_v, attb_v, in2t_v, sems = rest[outs:]
    t, d = mid_v.shape
    c = Copies(sems)
    load_in = c(in1, in1_v)
    loads = [load_rows(c, ab[u], a_v.at[u]) for u in range(2)]
    load_mid = c(mid_in, mid_v)
    load_in.wait()
    part = HEAD * heads
    stores = [[pltpu.make_async_copy(src.at[u], dst[u], sems.at[c.n + 4 * u + i])
               for i, (src, dst) in enumerate(((k_v, k_o), (v_v, v_o), (q_v, q_o), (attb_v, att_o)))] for u in range(2)]

    def slot(u, _):
        for k in range(2):
            @pl.when(u == k)
            def _():
                wait(loads[k])

        bias_row = jnp.where(u == 0, bias[0][0:1, :], bias[1][0:1, :])
        for a in range(0, 7 * LANE, 512):
            w = min(512, 7 * LANE - a)
            qkv_v[:, a : a + w] = (dot(in1_v[...], a_v[u, :, a : a + w]) + bias_row[:, a : a + w]).astype(BF16)
        lane = lanes((t, LANE))
        row = lax.broadcasted_iota(jnp.int32, (t, LANE), 0)
        tail_k = jnp.where(lane < HEAD + 3, 1.0, jnp.where((lane == HEAD + 3) & (row >= length), 1.0, 0.0))
        tail_q = jnp.where(lane == HEAD + 3, PENALTY, 0.0)
        tail_v = jnp.where(lane < HEAD + 2, 1.0, 0.0)
        for j in range(heads):
            q_v[u, j] = jnp.where(lane < HEAD, pick(qkv_v, HEAD * j).astype(F32), tail_q).astype(BF16)
            k_v[u, j] = jnp.where(lane < HEAD, pick(qkv_v, part + HEAD * j).astype(F32), tail_k).astype(BF16)
            v_v[u, j] = jnp.where(lane < HEAD, pick(qkv_v, 2 * part + HEAD * j).astype(F32), tail_v).astype(BF16)
        for k in range(2):
            @pl.when(u == k)
            def _():
                stores[k][0].start()
                stores[k][1].start()

        ln = lanes((chunk, LANE))

        def head(g, _):
            def rows(i, _):
                at = pl.ds(pl.multiple_of(i * chunk, 16), chunk)
                for r in range(group):
                    j = g * group + r
                    q = q_v[u, j, at, :]
                    s = dot_nt(q, k_v[u, j])
                    m = jnp.max(s, axis=1, keepdims=True)
                    p = jnp.exp2((s - m) * C2)
                    o = dot(p.astype(BF16), v_v[u, j])
                    total = jnp.sum(jnp.where(ln == HEAD, o, 0.0), axis=1, keepdims=True)
                    o_v[j, at, :] = jnp.where(ln < HEAD, o / total, 0.0).astype(BF16)
                    hi, mid, lo = split3(m + jnp.log2(total) * (1.0 / C2))
                    aug = jnp.where(ln == HEAD, -hi, jnp.where(ln == HEAD + 1, -mid, jnp.where(ln == HEAD + 2, -lo, q.astype(F32))))
                    q_v[u, j, at, :] = aug.astype(BF16)
                return 0

            return lax.fori_loop(0, t // chunk, rows, 0)

        lax.fori_loop(0, heads // group, head, 0)
        att_v[...] = jnp.zeros_like(att_v)
        for j in range(heads):
            put(att_v, 3 * LANE - part + HEAD * j, o_v[j])
        attb_v[u] = att_v[...]
        for k in range(2):
            @pl.when(u == k)
            def _():
                stores[k][2].start()
                stores[k][3].start()

        @pl.when(u == 0)
        def _():
            load_mid.wait()

        for a in range(0, d, 512):
            w = min(512, d - a)
            mid_v[:, a : a + w] += dot_nt(attb_v[u], a_v[u, a : a + w, 6 * LANE : 9 * LANE])
        return 0

    lax.fori_loop(0, 2, slot, 0)
    last = Copies(sems)
    last.n = c.n + 8
    done = [last(mid_v, mid_o)]
    if final:
        def norm(at, _):
            value = mid_v[at, :]
            average, inverse = stats(value)
            in1_v[at, :] = ((value - average) * inverse * gain[...] + shift[...]).astype(BF16)
            return 0

        row_loop(t, norm, 0)
        done.append(last(in1_v, in2_o))
        turn(in2t_v, in1_v)
        done.append(last(in2t_v, in2t_o))
    wait(done)
    for k in range(2):
        wait(stores[k])


def attn(in1, biases, ab, mid, gain, shift, length, final, chunk=368, group=1):
    blocks, shapes = jax.tree.flatten(ab)
    n, (t, d) = len(blocks), in1.shape
    w = blocks[0].shape[1]
    heads = w // 4 // HEAD
    tp = -(-t // LANE) * LANE
    o = jax.ShapeDtypeStruct
    hs = (heads, t, LANE)
    return pl.pallas_call(
        functools.partial(attn_kernel, shapes, heads, length, chunk, group, final),
        name="attn",
        in_specs=[ANY, ANY, VM, VM, VM, VM] + [ANY] * n,
        out_specs=[ANY] * (11 if final else 9),
        out_shape=[o(hs, BF16)] * 6 + [o((t, 3 * LANE), BF16)] * 2 + [o((t, d), F32)] + ([o((t, d), BF16), o((d, tp), BF16)] if final else []),
        scratch_shapes=[
            pltpu.VMEM((t, d), BF16), pltpu.VMEM((2, d, w), BF16), pltpu.VMEM((t, 8 * LANE), BF16),
            pltpu.VMEM((2, *hs), BF16), pltpu.VMEM((2, *hs), BF16), pltpu.VMEM((2, *hs), BF16), pltpu.VMEM(hs, BF16),
            pltpu.VMEM((t, 3 * LANE), BF16), pltpu.VMEM((t, d), F32), pltpu.VMEM((2, t, 3 * LANE), BF16),
            pltpu.VMEM((d, tp) if final else (16, LANE), BF16),
            pltpu.SemaphoreType.DMA((n + 14,)),
        ],
        input_output_aliases={1: 8},
        compiler_params=pltpu.CompilerParams(vmem_limit_bytes=VLIM),
        cost_estimate=pl.CostEstimate(flops=4 * t * d * w + 16 * heads * t * t * LANE, bytes_accessed=4 * d * w + 20 * t * d, transcendentals=2 * heads * t * t),
    )(in1, mid, gain, shift, *biases, *blocks)


GC = math.sqrt(2.0 / math.pi)


def ff_kernel(shapes, length, final, *refs):
    n = shapes.num_leaves
    in2, cot, mid, last, gain, sbias = refs[:6]
    bias = refs[6:8]
    eb, sb = nested(refs[8 : 8 + n], shapes)
    rest = refs[8 + n :]
    hid_o, gb_o, db = rest[0:2], rest[2:4], rest[4]
    if final:
        res_in, gi_in = mid, last
        result, gm32_o, gm_o, gmt_o, sums = rest[5:10]
        rest = rest[10:]
    else:
        res_o, gi_o = rest[5:7]
        rest = rest[7:]
    in2_v, cot_v, e_v, s_v, hid_v, gb_v, res_v, gi_v, mid_v, gmt_v, sems = rest
    t, d = in2_v.shape
    width = e_v.shape[2]
    c = Copies(sems)
    load_in = c(in2, in2_v)
    loads_e = [load_rows(c, eb[0], e_v.at[0])]
    load_cot = c(cot, cot_v)
    loads_s = [load_rows(c, sb[0], s_v.at[0])]
    loads_e.append(load_rows(c, eb[1], e_v.at[1]))
    loads_s.append(load_rows(c, sb[1], s_v.at[1]))
    if final:
        load_acc = [c(res_in[0], res_v), c(gi_in, gi_v)]
        load_mid = c(res_in[1], mid_v)
    else:
        load_acc = [c(mid, res_v)]
        gi_v[...] = jnp.zeros_like(gi_v)
    stores = [[pltpu.make_async_copy(src.at[u], dst[u], sems.at[c.n + 2 * u + i])
               for i, (src, dst) in enumerate(((hid_v, hid_o), (gb_v, gb_o)))] for u in range(2)]
    load_in.wait()

    def slot(u, _):
        for k in range(2):
            @pl.when(u == k)
            def _():
                wait(loads_e[k])
                if k == 0:
                    load_cot.wait()
                wait(loads_s[k])

        bias_row = jnp.where(u == 0, bias[0][1:2, :], bias[1][1:2, :])
        for a in range(0, width, 256):
            w = min(256, width - a)
            b = dot(in2_v[...], e_v[u, :, a : a + w]) + bias_row[:, a : a + w]
            sq = b * b
            th = jnp.tanh(GC * b * (1.0 + 0.044715 * sq))
            half = 0.5 * (1.0 + th)
            hid_v[u, :, a : a + w] = (b * half).astype(BF16)
            slope = half + (0.5 * GC) * b * (1.0 - th * th) * (1.0 + (3 * 0.044715) * sq)
            g = dot(cot_v[...], s_v[u, :, a : a + w]) * slope
            gb_v[u, :, a : a + w] = g.astype(BF16)
            db[u, :, a : a + w] = jnp.sum(g, axis=0, keepdims=True)
        for k in range(2):
            @pl.when(u == k)
            def _():
                for copy in stores[k]:
                    copy.start()
                if k == 0:
                    wait(load_acc)

        for a, w in ((0, d // 256 * 128), (d // 256 * 128, d - d // 256 * 128)):
            res_v[:, a : a + w] += dot_nt(hid_v[u], s_v[u, a : a + w, :])
            gi_v[:, a : a + w] += dot_nt(gb_v[u], e_v[u, a : a + w, :])
        return 0

    lax.fori_loop(0, 2, slot, 0)
    more = Copies(sems)
    more.n = c.n + 4
    if not final:
        done = [more(res_v, res_o), more(gi_v, gi_o)]
    else:
        load_mid.wait()
        whole = length // ROWS * ROWS
        zero = jnp.zeros((8, d), F32)

        def rows(at, carry):
            g, ct = gi_v[at, :], cot_v[at, :].astype(F32)
            inner, product = back_row(mid_v[at, :], g, gain[...])
            total = ct + inner
            mid_v[at, :] = total
            in2_v[at, :] = total.astype(BF16)
            return tuple(x + fold(y) for x, y in zip(carry, (total, product, g, ct)))

        def step(at, carry):
            result[at, :] = (res_v[at, :] + sbias[...]).astype(BF16)
            return rows(at, carry)

        carry = row_loop(whole, step, (zero,) * 4)
        if whole < t:
            value = (res_v[whole:t, :] + sbias[...]).astype(BF16)
            result[whole:length, :] = value[: length - whole, :]
            carry = rows(pl.ds(whole, ROWS), carry)
        for i, value in enumerate(carry):
            sums[i : i + 1, :] = jnp.sum(value, axis=0, keepdims=True)
        done = [more(mid_v, gm32_o), more(in2_v, gm_o)]
        turn(gmt_v, in2_v)
        done.append(more(gmt_v, gmt_o))
    wait(done)
    for k in range(2):
        wait(stores[k])


def ff(in2, cot, mid, acc, gain, sbias, biases, eb, sb, length):
    final = acc is not None
    blocks, shapes = jax.tree.flatten((eb, sb))
    n, (t, d) = len(blocks), in2.shape
    w = blocks[0].shape[1]
    tp = -(-t // LANE) * LANE
    o = jax.ShapeDtypeStruct
    outs = [o((t, w), BF16)] * 4 + [o((2, 1, w), F32)]
    specs = [ANY] * 4 + [VM]
    if final:
        outs += [o((length, d), BF16), o((t, d), F32), o((t, d), BF16), o((d, tp), BF16), o((4, d), F32)]
        specs += [VM, ANY, ANY, ANY, VM]
        args = (in2, cot, acc[0], mid, acc[1], gain, sbias)
    else:
        outs += [o((t, d), F32)] * 2
        specs += [ANY] * 2
        args = (in2, cot, mid, gain, sbias)

    def body(*refs):
        if final:
            ff_kernel(shapes, length, True, refs[0], refs[1], (refs[2], refs[3]), refs[4], *refs[5:])
        else:
            ff_kernel(shapes, length, False, refs[0], refs[1], refs[2], None, *refs[3:])

    return pl.pallas_call(
        body,
        name="ff",
        in_specs=[ANY] * (len(args) - 2) + [VM] * 4 + [ANY] * n,
        out_specs=specs,
        out_shape=outs,
        scratch_shapes=[
            pltpu.VMEM((t, d), BF16), pltpu.VMEM((t, d), BF16),
            pltpu.VMEM((2, d, w), BF16), pltpu.VMEM((2, d, w), BF16),
            pltpu.VMEM((2, t, w), BF16), pltpu.VMEM((2, t, w), BF16),
            pltpu.VMEM((t, d), F32), pltpu.VMEM((t, d), F32),
            pltpu.VMEM((t, d) if final else (8, LANE), F32), pltpu.VMEM((d, tp) if final else (16, LANE), BF16),
            pltpu.SemaphoreType.DMA((n + 14,)),
        ],
        compiler_params=pltpu.CompilerParams(vmem_limit_bytes=VLIM),
        cost_estimate=pl.CostEstimate(flops=16 * t * d * w, bytes_accessed=8 * d * w + 24 * t * d, transcendentals=2 * t * w),
    )(*args, *biases, *blocks)


def back_kernel(shape, heads, chunk, group, first, final, *refs):
    n = shape.num_leaves
    gm = refs[0]
    ab = nested(refs[1 : 1 + n], shape)
    q_i, k_i, v_i, att_i = refs[1 + n : 5 + n]
    rest = refs[5 + n :]
    if not first:
        gi_in, rest = rest[0], rest[1:]
    if final:
        x, gm32, gain = rest[:3]
        rest = rest[3:]
    dqkv_o, db = rest[:2]
    if final:
        out, sums = rest[2:4]
    else:
        gi_o = rest[2]
    rest = rest[4:] if final else rest[3:]
    gm_v, a_v, ga_v, q_v, k_v, v_v, g_v, att_v, ds_v, dq_v, dk_v, dv_v, pack_v, gi_v, gm32_v, sems = rest
    t, d = gi_v.shape
    c = Copies(sems)
    begin = [c(gm, gm_v)] + load_rows(c, ab, a_v)
    second = [c(att_i, att_v), c(q_i, q_v), c(k_i, k_v), c(v_i, v_v)]
    if first:
        third = []
        gi_v[...] = jnp.zeros_like(gi_v)
    else:
        third = [c(gi_in, gi_v)]
    if final:
        third.append(c(gm32, gm32_v))
    pack_v[...] = jnp.zeros_like(pack_v)
    wait(begin)
    ga_v[...] = dot(gm_v[...], a_v[:, 6 * LANE : 9 * LANE]).astype(BF16)
    lane = lanes((t, LANE))
    wide = lanes((t, 2 * LANE))
    part = HEAD * heads
    wait(second)
    for j in range(heads):
        at = 3 * LANE - part + HEAD * j
        base = min(at // LANE * LANE, LANE)
        window = ga_v[:, base : base + 2 * LANE].astype(F32) * att_v[:, base : base + 2 * LANE].astype(F32)
        inside = (wide >= at - base) & (wide < at - base + HEAD)
        delta = jnp.sum(jnp.where(inside, window, 0.0), axis=1, keepdims=True)
        hi = delta.astype(BF16).astype(F32)
        g = pick(ga_v, at).astype(F32)
        g_v[j] = jnp.where(lane < HEAD, g, jnp.where(lane == HEAD, -hi, jnp.where(lane == HEAD + 1, hi - delta, 0.0))).astype(BF16)

    def head(h, _):
        def rows(i, _):
            at = pl.ds(pl.multiple_of(i * chunk, 16), chunk)
            for r in range(group):
                j = h * group + r
                p = jnp.exp2(dot_nt(k_v[j, at, :], q_v[j]) * C2)
                ds = (p * dot_nt(v_v[j, at, :], g_v[j])).astype(BF16)
                dv_v[j, at, :] = dot(p.astype(BF16), g_v[j]).astype(BF16)
                dk_v[j, at, :] = (dot(ds, q_v[j]) * SCALE).astype(BF16)
                ds_v[r, at, :] = ds
            return 0

        lax.fori_loop(0, t // chunk, rows, 0)
        for r in range(group):
            j = h * group + r
            dq_v[j] = (dot_tn(ds_v[r], k_v[j]) * SCALE).astype(BF16)
        return 0

    lax.fori_loop(0, heads // group, head, 0)
    for j in range(heads):
        for i, ref in enumerate((dq_v, dk_v, dv_v)):
            put(pack_v, i * part + HEAD * j, jnp.where(lane < HEAD, ref[j].astype(F32), 0.0).astype(BF16))
    more = Copies(sems)
    more.n = c.n
    done = [more(pack_v, dqkv_o)]
    db[...] = jnp.sum(pack_v[...].astype(F32), axis=0, keepdims=True)
    wait(third)
    for a in range(0, d, 512):
        w = min(512, d - a)
        gi_v[:, a : a + w] += dot_nt(pack_v[...], a_v[a : a + w, : 7 * LANE])
    if final:
        leave_body(gi_v, x, gm32_v, gain, out, sums)
    else:
        done.append(more(gi_v, gi_o))
    wait(done)


def back(gm, ab, q, k, v, att, gi, leaving=None, chunk=368, group=4):
    blocks, shape = jax.tree.flatten(ab)
    n, (t, d) = len(blocks), gm.shape
    w = blocks[0].shape[1]
    heads = q.shape[0]
    first, final = gi is None, leaving is not None
    o = jax.ShapeDtypeStruct
    hs = (heads, t, LANE)
    args, specs = (gm, *blocks, q, k, v, att), [ANY] * (n + 5)
    if not first:
        args, specs = (*args, gi), specs + [ANY]
    outs, out_specs = [o((t, 7 * LANE), BF16), o((1, 7 * LANE), F32)], [ANY, VM]
    if final:
        args, specs = (*args, *leaving), specs + [VM, ANY, VM]
        outs, out_specs = outs + [o(leaving[0].shape, BF16), o((2, d), F32)], out_specs + [VM, VM]
    else:
        outs, out_specs = outs + [o((t, d), F32)], out_specs + [ANY]
    return pl.pallas_call(
        functools.partial(back_kernel, shape, heads, chunk, group, first, final),
        name="back",
        in_specs=specs,
        out_specs=out_specs,
        out_shape=outs,
        scratch_shapes=[
            pltpu.VMEM((t, d), BF16), pltpu.VMEM((d, w), BF16), pltpu.VMEM((t, 3 * LANE), BF16),
            pltpu.VMEM(hs, BF16), pltpu.VMEM(hs, BF16), pltpu.VMEM(hs, BF16), pltpu.VMEM(hs, BF16),
            pltpu.VMEM((t, 3 * LANE), BF16), pltpu.VMEM((group, t, t), BF16),
            pltpu.VMEM(hs, BF16), pltpu.VMEM(hs, BF16), pltpu.VMEM(hs, BF16),
            pltpu.VMEM((t, 7 * LANE), BF16), pltpu.VMEM((t, d), F32), pltpu.VMEM((t, d) if final else (8, LANE), F32),
            pltpu.SemaphoreType.DMA((n + 10,)),
        ],
        compiler_params=pltpu.CompilerParams(vmem_limit_bytes=VLIM),
        cost_estimate=pl.CostEstimate(flops=2 * t * d * w + 20 * heads * t * t * LANE, bytes_accessed=2 * d * w + 16 * t * d, transcendentals=heads * t * t),
    )(*args)


def grads_kernel(n, split, groups, *refs):
    k = len(groups)
    ins = refs[: 4 * k]
    outs = refs[4 * k : 4 * k + n]
    scratch = refs[4 * k + n :]
    lhs, rhs = scratch[: 2 * k], scratch[2 * k : 4 * k]
    acc, tile_v, sems, osem = scratch[4 * k :]
    c = Copies(sems)
    cps = []
    for i in range(k):
        cps += [c(ins[4 * i + u], (lhs if u < 2 else rhs)[2 * i + u % 2]) for u in range(4)]
    wait(cps)
    size = outs[0].shape[0]
    t = rhs[0].shape[0]
    me = lax.axis_index("row")

    def step(s, _):
        slot = lax.rem(s, 2)
        row = pl.multiple_of(lax.rem(me * split + s, n) * size, 16)
        rows = pl.ds(row, size)

        @pl.when(s >= 2)
        def _():
            pltpu.make_async_copy(tile_v.at[slot], outs[0], osem.at[slot]).wait()

        if k == 1:
            def body(at):
                cols = pl.ds(at, 256)
                tile_v[slot, :, cols] = (
                    dot(lhs[0][rows, :t], rhs[0][:, cols]) + dot(lhs[1][rows, :t], rhs[1][:, cols])
                ).astype(BF16)

            tiles(groups[0][1], 256, body)
        else:
            for i, (start, width) in enumerate(groups):
                done = 0 if i == 0 else groups[i - 1][0] + groups[i - 1][1]
                for a in range(0, width, 256):
                    w = min(256, width - a)
                    value = dot(lhs[2 * i][rows, :t], rhs[2 * i][:, a : a + w]) + dot(
                        lhs[2 * i + 1][rows, :t], rhs[2 * i + 1][:, a : a + w]
                    )
                    at = start + a
                    if at < done:
                        o = done - at
                        value = jnp.concatenate((value[:, :o] + acc[:, at : at + o], value[:, o:]), axis=1) if o < w else value + acc[:, at : at + w]
                    acc[:, at : at + w] = value
            tile_v[slot] = acc[...].astype(BF16)
        for u in range(n):
            @pl.when(s == u)
            def _():
                pltpu.make_async_copy(tile_v.at[slot], outs[u], osem.at[slot]).start()
        return 0

    lax.fori_loop(0, n, step, 0)
    for u in range(max(0, n - 2), n):
        pltpu.make_async_copy(tile_v.at[u % 2], outs[u], osem.at[u % 2]).wait()


def grads(n, terms, width, split=1):
    k = len(terms)
    groups = tuple((term[0], term[3].shape[1]) for term in terms)
    flat = [array for term in terms for array in term[1:]]
    d, t = terms[0][1].shape[0], terms[0][3].shape[0]
    n = n * split
    size = d // n
    scratch = [pltpu.VMEM(term[1].shape, BF16) for term in terms for _ in range(2)]
    scratch += [pltpu.VMEM(term[3].shape, BF16) for term in terms for _ in range(2)]
    flops = sum(4 * d * t * w for _, w in groups)
    return pl.pallas_call(
        functools.partial(grads_kernel, n, split, groups),
        name="grads",
        in_specs=[ANY] * (4 * k),
        out_specs=[ANY] * n,
        out_shape=[jax.ShapeDtypeStruct((size, width), BF16)] * n,
        scratch_shapes=scratch + [
            pltpu.VMEM((size, width if k > 1 else LANE), F32), pltpu.VMEM((2, size, width), BF16),
            pltpu.SemaphoreType.DMA((4 * k,)), pltpu.SemaphoreType.DMA((2,)),
        ],
        compiler_params=pltpu.CompilerParams(vmem_limit_bytes=VLIM),
        cost_estimate=pl.CostEstimate(flops=flops, bytes_accessed=2 * d * width + 8 * t * d, transcendentals=0),
    )(*flat)


CORE, SIDE = 1, 2


def hop_row(value, shift, size):
    return lax.ppermute(value, "row", [(i, (i + shift) % size) for i in range(size)])


def hop_col(value, flip):
    return lax.ppermute(value, "col", [(i, i ^ flip) for i in range(4)])


def hop_dp(value, flip):
    return lax.ppermute(value, "dp", [(i, i ^ flip) for i in range(4)])


def after(value, *first):
    return lax.optimization_barrier((value, *first))[0]


def near(block, n):
    return [block] + [hop_row(block, s, n) for s in range(1, n)], hop_col(block, SIDE)


def diagonal(own, side, n, via):
    parts = [side]
    half = side.shape[0] // 2
    for s in range(1, n):
        if via == "row":
            parts.append(hop_row(side, s, n))
        elif via == "col":
            parts.append(hop_col(own[s], SIDE))
        else:
            parts.append((hop_row(side[:half], s, n), hop_col(own[s][half:], SIDE)))
    return parts


def across(parts):
    return [jax.tree.map(lambda b: hop_col(b, CORE), part) for part in parts]


def add(a, b):
    return (a.astype(F32) + b.astype(F32)).astype(BF16)


def over_row(parts, n):
    total = parts[0]
    for s in range(1, n):
        total = add(total, hop_row(parts[s], s, n))
    return total


def over_dp(total):
    half = total.shape[0] // 2
    low = lax.rem(lax.axis_index("dp"), 2)
    mine = lax.dynamic_slice_in_dim(total, low * half, half, 0)
    theirs = lax.dynamic_slice_in_dim(total, (1 - low) * half, half, 0)
    mine = add(mine, hop_dp(theirs, 1))
    mine = add(mine, hop_dp(mine, 2))
    return mine, hop_dp(mine, 1)


def joined_halves(mine, theirs):
    even = lax.rem(lax.axis_index("dp"), 2) == 0
    return jnp.where(even, jnp.concatenate((mine, theirs)), jnp.concatenate((theirs, mine))).astype(F32)


def layer(n, images, cotangent, first_gain, first_shift, query_weight, query_bias, key_weight, value_weight, value_bias,
          output_weight, output_bias, second_gain, second_shift, expand_weight, expand_bias, shrink_weight, shrink_bias):
    length, d = images.shape[1:]
    t = -(-length // 16) * 16
    part, ff_part = query_weight.shape[1], expand_weight.shape[1]
    wide = 4 * part
    pad_ff = ((0, 0), (0, wide - ff_part))
    a_own = weave(query_weight.T, key_weight.T, value_weight.T, output_weight)
    zeros = jnp.zeros((part,), F32)
    bias_own = jnp.stack((jnp.concatenate((query_bias, zeros, value_bias, zeros)), jnp.pad(expand_bias, pad_ff[1:])))
    a_near, a_side = near(a_own, n)
    bias_side = hop_col(bias_own, SIDE)
    biases = [bias_own, bias_side, hop_col(bias_own, CORE), hop_col(bias_side, CORE)]
    row = lambda v: v.reshape(1, -1)
    images, cotangent = images[0], cotangent[0]
    input1, in1_t, cot, cot_t, middle = enter(
        after(images, a_own), cotangent, row(first_gain), row(first_shift), row(output_bias), t)
    e_own = jnp.pad(expand_weight, pad_ff)
    s_own = jnp.pad(shrink_weight.T, pad_ff)

    a_far = diagonal(a_near, a_side, n, "both")
    a_all = [a_near, a_far, across(a_near), across(a_far)]
    e_near, e_side = near(after(e_own, a_side), n)
    s_near, s_side = near(after(s_own, a_side), n)
    e_far = diagonal(e_near, e_side, n, "row")
    s_far = diagonal(s_near, s_side, n, "col")
    e_all = [e_near, e_far, across(e_near), across(e_far)]
    s_all = [s_near, s_far, across(s_near), across(s_far)]
    cot_t2 = hop_col(after(cot_t, a_side), CORE)
    in1_t2 = hop_col(after(in1_t, a_side), CORE)

    gain2, shift2 = row(second_gain), row(second_shift)
    kept = {}

    def attend(pair, last, middle, final):
        out = attn(input1, [after(biases[pair], last), biases[pair + 2]], [a_all[pair], a_all[pair + 2]],
                  middle, gain2, shift2, length, final)
        for i in range(2):
            kept[pair + 2 * i] = (out[i], out[2 + i], out[4 + i], out[6 + i])
        return out[8:]

    middle, = attend(0, middle, middle, False)
    middle, input2, in2_t = attend(1, kept[0][3], middle, True)
    in2_t2 = hop_col(in2_t, CORE)
    att2 = [hop_col(kept[s + 2][3], CORE) for s in (0, 1)]
    hidden, before, expand_sums, ge, gs = {}, {}, {}, {}, {}

    def feed(pair, last, acc):
        out = ff(input2, cot, middle, acc, gain2, row(shrink_bias), [after(biases[pair], last), biases[pair + 2]],
                  [e_all[pair], e_all[pair + 2]], [s_all[pair], s_all[pair + 2]], length)
        for i in range(2):
            hidden[pair + 2 * i], before[pair + 2 * i], expand_sums[pair + 2 * i] = out[i], out[2 + i], out[4][i]
        return out[5:]

    def expand_grads(slot, last):
        other = hop_col(before[slot + 2], CORE)
        ge[slot] = grads(n, [(0, in2_t, in2_t2, after(before[slot], last), other)], wide)
        return ge[slot][-1]

    def shrink_grads(slot, last):
        other = hop_col(hidden[slot + 2], CORE)
        gs[slot] = grads(n, [(0, cot_t, cot_t2, after(hidden[slot], last), other)], wide)
        return gs[slot][-1]

    acc = feed(0, in2_t, None)
    last = expand_grads(0, expand_sums[0])
    result, gm32, gm, gm_t, middle_sums = feed(1, last, acc)
    gm_t2 = hop_col(gm_t, CORE)
    last = expand_grads(1, middle_sums)
    last = shrink_grads(0, last)
    last = shrink_grads(1, last)
    joined, joined_sums, ga = {}, {}, {}

    def attend_back(slot, last, grad1, leaving=None):
        q, k, v, att = kept[slot]
        joined[slot], joined_sums[slot], *out = back(
            gm, a_all[slot], q, k, v, after(att, last), grad1, leaving)
        return out

    def joined_grads(slot, last, split=1):
        other = hop_col(joined[slot + 2], CORE)
        ga[slot] = grads(n, [
            (0, in1_t, in1_t2, after(joined[slot], last), other),
            (wide - 384, gm_t, gm_t2, kept[slot][3], att2[slot]),
        ], wide, split)
        return ga[slot][-1]

    grad1, = attend_back(3, last, None)
    grad1, = attend_back(1, joined_sums[3], grad1)
    grad1, = attend_back(2, joined_sums[1], grad1)
    last = joined_grads(1, joined_sums[2])
    grad_stream, first_sums = attend_back(0, last, grad1, (images, gm32, row(first_gain)))
    split = 2 if d // n % 32 == 0 else 1
    joined_grads(0, first_sums, split)

    e_total = over_dp(add(over_row(ge[0], n), hop_col(over_row(ge[1], n), SIDE)))
    s_total = over_dp(add(over_row(gs[0], n), hop_col(over_row(gs[1], n), SIDE)))
    a_side = hop_col(over_row(ga[1], n), SIDE)
    piece = a_side.shape[0] // split
    a_total = []
    for i in range(split):
        total = add(ga[0][i], a_side[i * piece : (i + 1) * piece])
        for s in range(1, n):
            total = add(total, hop_row(ga[0][s * split + i], s, n))
        a_total.append(over_dp(total))
    fill = lambda rows, count: jnp.pad(rows, ((0, count - rows.shape[0]), (0, 0)))
    sums = [jnp.concatenate((jnp.pad(joined_sums[s], ((0, 0), (0, wide - joined_sums[s].shape[1]))), expand_sums[s])) for s in range(4)]
    features = fill(jnp.concatenate((first_sums, middle_sums)), 6)
    two = jnp.concatenate((features, sums[0], sums[1])) + hop_col(jnp.concatenate((features, sums[2], sums[3])), CORE)
    one = two[:8] + hop_col(jnp.concatenate((two[:6], two[8:])), SIDE)
    total = one
    for s in range(1, n):
        total = total + hop_row(one, s, n)
    for flip in (1, 2):
        total = total + hop_dp(total, flip)
    biases = total[6:]
    gq, gk, gv, go = unweave(a_total, part)
    return (
        result[None],
        grad_stream[None],
        total[0],
        total[1],
        gq.T,
        biases[0, :part],
        gk.T,
        gv.T,
        biases[0, 2 * part : 3 * part],
        go,
        total[2],
        total[3],
        total[4],
        joined_halves(*e_total)[:, :ff_part],
        biases[1, :ff_part],
        joined_halves(*s_total)[:, :ff_part].T,
        total[5],
    )


def solution(mesh):
    batch = P(("dp", "row", "col"), None, None)
    into, out, cols, whole = P("row", "col"), P("col", "row"), P("col"), P()

    def step(*args):
        return layer(mesh.shape["row"], *args)

    return jax.shard_map(
        step,
        mesh=mesh,
        in_specs=(batch, batch, whole, whole, into, cols, into, into, cols, out, whole, whole, whole, into, cols, out, whole),
        out_specs=(batch, batch, whole, whole, into, cols, into, into, cols, out, whole, whole, whole, into, cols, out, whole),
        check_vma=False,
    )
```

time: 806 us -> 693 us (0.86)
  local copies, waits for them, and re-layouts: 101 us -> 19 us
  other arithmetic: 68.5 us -> 9.83 us
  waiting for transfers between devices: 283 us -> 306 us
  starting transfers between devices: 45.1 us -> 67.8 us
  Pallas kernels: 296 us -> 279 us
    ppermute x11 -> x13, waiting for transfers between devices: 117 us -> 161 us  [hop_row(): lax.ppermute(value, 'row', [(i, (i + shift) % size) for i in range(size)])]
    ppermute x11 -> x14, waiting for transfers between devices: 121 us -> 78.6 us  [hop_dp(): return lax.ppermute(value, 'dp', [(i, i ^ flip) for i in range(4)])]
    reduce_sum x7 -> x0, other arithmetic: 24.7 us -> none  [the longest x5 18.5 us: layer(): jnp.sum(v, axis=0)]
    ppermute x11 -> x14, starting transfers between devices: 13.5 us -> 36.4 us  [hop_dp(): return lax.ppermute(value, 'dp', [(i, i ^ flip) for i in range(4)])]
    ppermute x37 -> x38, waiting for transfers between devices: 44.2 us -> 66.6 us  [hop_col(): return lax.ppermute(value, 'col', [(i, i ^ flip) for i in range(4)])]
    pallas_call x18 -> x17, Pallas kernels: 296 us -> 279 us  [the longest x4 70.7 us: back(): pl.pallas_call(functools.partial(back_kernel, shape, heads, chunk, group,...]
    convert_element_type x4 -> x0, local copies, waits for them, and re-layouts: 14.9 us -> none  [the longest x2 5.97 us: norm(): ((stream - average) * inverse * gain + shift).astype(BF16)]
    convert_element_type x5 -> x0, other arithmetic: 14.7 us -> none  [the longest x2 6.26 us: norm(): ((stream - average) * inverse * gain + shift).astype(BF16)]
  transfers between devices with their start and end apart: 59 -> 65, of which waited for: 19 -> 25; matrix products, arithmetic and copies ran while one was open for 13% -> 3% of each run, Pallas kernels for 25% -> 34%
where the time goes in v3:
time: 693 us; the launch traced here: 683 us
  waiting for transfers between devices  306 us (44%)
  Pallas kernels  279 us (40%)
  starting transfers between devices  67.8 us (10%)
  local copies, waits for them, and re-layouts  19 us (3%)
  other arithmetic  9.83 us (1%)
    ppermute x13, waiting for transfers between devices, hop_row(): lax.ppermute(value, 'row', [(i, (i + shift) % size) for i in range(size)])  161 us
    ppermute x14, waiting for transfers between devices, hop_dp(): return lax.ppermute(value, 'dp', [(i, i ^ flip) for i in range(4)])  78.6 us
    pallas_call x4, Pallas kernels, back(): pl.pallas_call(functools.partial(back_kernel, shape, heads, chunk, group,...  70.7 us
    pallas_call x2, Pallas kernels, ff(): pl.pallas_call(body, name='ff', in_specs=[ANY] * (len(args) - 2) + [VM] *...  69 us
    ppermute x38, waiting for transfers between devices, hop_col(): return lax.ppermute(value, 'col', [(i, i ^ flip) for i in range(4)])  66.6 us
    pallas_call x6, Pallas kernels, grads(): pl.pallas_call(functools.partial(grads_kernel, n, split, groups), name='g...  64.2 us
    pallas_call x2, Pallas kernels, attn(): pl.pallas_call(functools.partial(attn_kernel, shapes, heads, length, chun...  60 us
    ppermute x14, starting transfers between devices, hop_dp(): return lax.ppermute(value, 'dp', [(i, i ^ flip) for i in range(4)])  36.4 us
  transfers between devices with their start and end apart: 65, of which 25 were waited for; matrix products, arithmetic and copies ran while one was open for 3% of the time, Pallas kernels for 34%

profile of v3, /device:TPU:0, one launch (start us, length us, event | category | flops | bytes accessed | tf_op | source)
XLA Modules:
  0.0 682.6 jit_solution(11650465747297719294)
XLA Ops:
  8.0 27.9 %collective-permute-done.1.refs_7_.refs_2_ = bf16[576,1152]{1,0:T(8,128)(2,1)} collective-permute-done((bf16[576,1152]{1,0:T(8,128)(2,1)}, bf16[576,1152]{1,0:T(8,128)(2,1)}, u32[]{:S(2)}, u32[]{:S(2)}) %collective-permute-start.1) | collective-permute-done | bytes 1327136 | tf_op jit(solution)/shard_map/ppermute | solution.py:745
  84.9 26.4 %collective-permute-done.12.refs_8_ = bf16[576,1152]{1,0:T(8,128)(2,1)S(1)} collective-permute-done((bf16[576,1152]{1,0:T(8,128)(2,1)S(1)}, bf16[576,1152]{1,0:T(8,128)(2,1)S(1)}, u32[]{:S(2)}, u32[]{:S(2)}) %collective-permute-start.12) | collective-permute-done | bytes 1327136 | tf_op jit(solution)/shard_map/ppermute | solution.py:745
  111.4 28.7 %attn.2 = (bf16[4,736,128]{2,1,0:T(8,128)(2,1)}, bf16[4,736,128]{2,1,0:T(8,128)(2,1)}, bf16[4,736,128]{2,1,0:T(8,128)(2,1)}, bf16[4,736,128]{2,1,0:T(8,128)(2,1)...) custom-call(bf16[736,1152]{1,0:T(8,128)(2,1)} %get-tuple-element.110, ...), custom_call_target="tpu_custom_call", output_to_operand_aliasing={{8}: (1, {})} | custom-call | flops 8344567808 | bytes 22265856 | tf_op jit(solution)/shard_map/attn/pallas_call | solution.py:369
  140.1 31.3 %attn.3 = (bf16[4,736,128]{2,1,0:T(8,128)(2,1)}, bf16[4,736,128]{2,1,0:T(8,128)(2,1)}, bf16[4,736,128]{2,1,0:T(8,128)(2,1)}, bf16[4,736,128]{2,1,0:T(8,128)(2,1)...) custom-call(bf16[736,1152]{1,0:T(8,128)(2,1)} %get-tuple-element.110, ...), custom_call_target="tpu_custom_call", output_to_operand_aliasing={{8}: (1, {})} | custom-call | flops 8344567808 | bytes 22265856 | tf_op jit(solution)/shard_map/attn/pallas_call | solution.py:369
  175.3 28.9 %ff.2 = (bf16[736,1152]{1,0:T(8,128)(2,1)}, bf16[736,1152]{1,0:T(8,128)(2,1)}, bf16[736,1152]{1,0:T(8,128)(2,1)}, bf16[736,1152]{1,0:T(8,128)(2,1)}, f32[2,1,115...) custom-call(bf16[736,1152]{1,0:T(8,128)(2,1)} %get-tuple-element.116.refs_0_, ...), custom_call_target="tpu_custom_call" | custom-call | flops 15627976704 | bytes 30965760 | tf_op jit(solution)/shard_map/ff/pallas_call | solution.py:520
  205.2 26.3 %collective-permute-done.25.refs_14_ = bf16[576,1152]{1,0:T(8,128)(2,1)} collective-permute-done((bf16[576,1152]{1,0:T(8,128)(2,1)}, bf16[576,1152]{1,0:T(8,128)(2,1)}, u32[]{:S(2)}, u32[]{:S(2)}) %collective-permute-start.25) | collective-permute-done | bytes 1327136 | tf_op jit(solution)/shard_map/ppermute | solution.py:749
  233.9 10.5 %grads.6 = (bf16[576,1152]{1,0:T(8,128)(2,1)}, bf16[576,1152]{1,0:T(8,128)(2,1)}) custom-call(bf16[1152,768]{1,0:T(8,128)(2,1)} %get-tuple-element.119.refs_0_, bf16[1152,768]{1,0:T(8,128)(2,1)} %collective-permute-done.18.refs_1_, bf16[736,1152]{1,0:T(8,128)(2,1)} %get-tuple-element.127.refs_2_, bf16[736,1152]{1,0:T(8,128)(2,1)} %copy-done.28), custom_call_target="tpu_custom_call" | custom-call | flops 3906994176 | bytes 9437184 | tf_op jit(solution)/shard_map/grads/pallas_call | solution.py:726
  244.4 40.1 %ff.3 = (bf16[736,1152]{1,0:T(8,128)(2,1)}, bf16[736,1152]{1,0:T(8,128)(2,1)}, bf16[736,1152]{1,0:T(8,128)(2,1)}, bf16[736,1152]{1,0:T(8,128)(2,1)}, f32[2,1,115...) custom-call(bf16[736,1152]{1,0:T(8,128)(2,1)} %get-tuple-element.116, ...), custom_call_target="tpu_custom_call" | custom-call | flops 15627976704 | bytes 30965760 | tf_op jit(solution)/shard_map/ff/pallas_call | solution.py:520
  299.6 10.5 %grads.8 = (bf16[576,1152]{1,0:T(8,128)(2,1)}, bf16[576,1152]{1,0:T(8,128)(2,1)}) custom-call(bf16[1152,768]{1,0:T(8,128)(2,1)} %get-tuple-element.147.refs_0_, bf16[1152,768]{1,0:T(8,128)(2,1)} %collective-permute-done.29.refs_1_, bf16[736,1152]{1,0:T(8,128)(2,1)} %get-tuple-element.155.refs_2_, bf16[736,1152]{1,0:T(8,128)(2,1)} %collective-permute-done.31.refs_3_), custom_call_target="tpu_custom_call" | custom-call | flops 3906994176 | bytes 9437184 | tf_op jit(solution)/shard_map/grads/pallas_call | solution.py:726
  310.1 10.5 %grads.9 = (bf16[576,1152]{1,0:T(8,128)(2,1)}, bf16[576,1152]{1,0:T(8,128)(2,1)}) custom-call(bf16[1152,768]{1,0:T(8,128)(2,1)} %get-tuple-element.147.refs_0_, bf16[1152,768]{1,0:T(8,128)(2,1)} %collective-permute-done.29.refs_1_, bf16[736,1152]{1,0:T(8,128)(2,1)} %get-tuple-element.158.refs_2_, bf16[736,1152]{1,0:T(8,128)(2,1)} %collective-permute-done.32.refs_3_), custom_call_target="tpu_custom_call" | custom-call | flops 3906994176 | bytes 9437184 | tf_op jit(solution)/shard_map/grads/pallas_call | solution.py:726
  322.4 16.1 %back.4 = (bf16[736,896]{1,0:T(8,128)(2,1)}, f32[1,896]{1,0:T(1,128)}, f32[736,1152]{1,0:T(8,128)}) custom-call(bf16[736,1152]{1,0:T(8,128)(2,1)} %get-tuple-element.132.refs_0_, bf16[576,1152]{1,0:T(8,128)(2,1)} %collective-permute-done.9.refs_9_.refs_1_, bf16[288,1152]{1,0:T(8,128)(2,1)} %collective-permute-done.10.refs_10_.refs_2_, ...), custom_call_target="tpu_custom_call" | custom-call | flops 7500464128 | bytes 16220160 | tf_op jit(solution)/shard_map/back/pallas_call | solution.py:639
  339.3 17.0 %back.5 = (bf16[736,896]{1,0:T(8,128)(2,1)}, f32[1,896]{1,0:T(1,128)}, f32[736,1152]{1,0:T(8,128)}) custom-call(bf16[736,1152]{1,0:T(8,128)(2,1)} %get-tuple-element.132.refs_0_, bf16[576,1152]{1,0:T(8,128)(2,1)} %collective-permute-done.6.refs_6_.refs_1_, bf16[288,1152]{1,0:T(8,128)(2,1)} %collective-permute-done.7.refs_7_.refs_2_, ...), custom_call_target="tpu_custom_call" | custom-call | flops 7500464128 | bytes 16220160 | tf_op jit(solution)/shard_map/back/pallas_call | solution.py:639
  356.3 16.7 %back.6 = (bf16[736,896]{1,0:T(8,128)(2,1)}, f32[1,896]{1,0:T(1,128)}, f32[736,1152]{1,0:T(8,128)}) custom-call(bf16[736,1152]{1,0:T(8,128)(2,1)} %get-tuple-element.132.refs_0_, bf16[576,1152]{1,0:T(8,128)(2,1)} %collective-permute-done.2.refs_8_.refs_1_, bf16[576,1152]{1,0:T(8,128)(2,1)} %collective-permute-done.3.refs_9_.refs_2_, ...), custom_call_target="tpu_custom_call" | custom-call | flops 7500464128 | bytes 16220160 | tf_op jit(solution)/shard_map/back/pallas_call | solution.py:639
  375.3 11.1 %grads.10 = (bf16[576,1152]{1,0:T(8,128)(2,1)}, bf16[576,1152]{1,0:T(8,128)(2,1)}) custom-call(bf16[1152,768]{1,0:T(8,128)(2,1)} %get-tuple-element.137.refs_0_, bf16[1152,768]{1,0:T(8,128)(2,1)} %collective-permute-done.28.refs_1_, bf16[736,896]{1,0:T(8,128)(2,1)} %get-tuple-element.174.refs_2_, bf16[736,896]{1,0:T(8,128)(2,1)} %copy-done.30, ...), custom_call_target="tpu_custom_call" | custom-call | flops 4341104640 | bytes 9437184 | tf_op jit(solution)/shard_map/grads/pallas_call | solution.py:726
  386.4 20.9 %back.7 = (bf16[736,896]{1,0:T(8,128)(2,1)}, f32[1,896]{1,0:T(1,128)}, bf16[729,1152]{1,0:T(8,128)(2,1)}, f32[2,1152]{1,0:T(2,128)}) custom-call(bf16[736,1152]{1,0:T(8,128)(2,1)} %get-tuple-element.132.refs_0_, bf16[576,1152]{1,0:T(8,128)(2,1)} %weave.1.refs_6_.refs_1_, bf16[576,1152]{1,0:T(8,128)(2,1)} %collective-permute-done.1.refs_7_.refs_2_, ...), custom_call_target="tpu_custom_call" | custom-call | flops 7500464128 | bytes 16220160 | tf_op jit(solution)/shard_map/back/pallas_call | solution.py:639
  416.6 11.1 %grads.11 = (bf16[288,1152]{1,0:T(8,128)(2,1)}, bf16[288,1152]{1,0:T(8,128)(2,1)}, bf16[288,1152]{1,0:T(8,128)(2,1)}, bf16[288,1152]{1,0:T(8,128)(2,1)}) custom-call(bf16[1152,768]{1,0:T(8,128)(2,1)} %get-tuple-element.137.refs_0_, bf16[1152,768]{1,0:T(8,128)(2,1)} %collective-permute-done.28.refs_1_, bf16[736,896]{1,0:T(8,128)(2,1)} %get-tuple-element.186.refs_2_, ...), custom_call_target="tpu_custom_call" | custom-call | flops 4341104640 | bytes 9437184 | tf_op jit(solution)/shard_map/grads/pallas_call | solution.py:726
  427.8 72.7 %collective-permute-done.38 = f32[8,1152]{1,0:T(8,128)S(1)} collective-permute-done((f32[8,1152]{1,0:T(8,128)S(1)}, f32[8,1152]{1,0:T(8,128)S(1)}, u32[]{:S(2)}, u32[]{:S(2)}) %collective-permute-start.38) | collective-permute-done | bytes 36896 | tf_op jit(solution)/shard_map/ppermute | solution.py:745
  512.6 20.1 %collective-permute-done.43 = bf16[576,1152]{1,0:T(8,128)(2,1)S(1)} collective-permute-done((bf16[576,1152]{1,0:T(8,128)(2,1)}, bf16[576,1152]{1,0:T(8,128)(2,1)S(1)}, u32[]{:S(2)}, u32[]{:S(2)}) %collective-permute-start.43) | collective-permute-done | bytes 1327136 | tf_op jit(solution)/shard_map/ppermute | solution.py:745
  539.9 24.8 %collective-permute-done.55 = bf16[576,1152]{1,0:T(8,128)(2,1)S(1)} collective-permute-done((bf16[576,1152]{1,0:T(8,128)(2,1)S(1)}, bf16[576,1152]{1,0:T(8,128)(2,1)S(1)}, u32[]{:S(2)}, u32[]{:S(2)}) %collective-permute-start.55) | collective-permute-done | bytes 1327136 | tf_op jit(solution)/shard_map/ppermute | solution.py:749
  571.1 18.5 %collective-permute-done.56 = bf16[288,1152]{1,0:T(8,128)(2,1)S(1)} collective-permute-done((bf16[288,1152]{1,0:T(8,128)(2,1)S(1)}, bf16[288,1152]{1,0:T(8,128)(2,1)S(1)}, u32[]{:S(2)}, u32[]{:S(2)}) %collective-permute-start.56) | collective-permute-done | bytes 663584 | tf_op jit(solution)/shard_map/ppermute | solution.py:753
  593.7 17.6 %collective-permute-done.63 = bf16[288,1152]{1,0:T(8,128)(2,1)S(1)} collective-permute-done((bf16[288,1152]{1,0:T(8,128)(2,1)S(1)}, bf16[288,1152]{1,0:T(8,128)(2,1)S(1)}, u32[]{:S(2)}, u32[]{:S(2)}) %collective-permute-start.63) | collective-permute-done | bytes 663584 | tf_op jit(solution)/shard_map/ppermute | solution.py:753
  612.3 11.5 %collective-permute-done.57 = bf16[288,1152]{1,0:T(8,128)(2,1)S(1)} collective-permute-done((bf16[288,1152]{1,0:T(8,128)(2,1)S(1)}, bf16[288,1152]{1,0:T(8,128)(2,1)S(1)}, u32[]{:S(2)}, u32[]{:S(2)}) %collective-permute-start.57) | collective-permute-done | bytes 663584 | tf_op jit(solution)/shard_map/ppermute | solution.py:753
  627.3 11.3 %collective-permute-start.47 = (bf16[144,1152]{1,0:T(8,128)(2,1)S(1)}, bf16[144,1152]{1,0:T(8,128)(2,1)S(1)}, u32[]{:S(2)}, u32[]{:S(2)}) collective-permute-start(bf16[144,1152]{1,0:T(8,128)(2,1)S(1)} %add_convert_fusion.18), channel_id=1, source_target_pairs={{0,16},{8,24},{16,0},{24,8},{1,17},{9,25},{17,1},{25,9},{2,18},{10... | collective-permute-start | bytes 995336 | tf_op jit(solution)/shard_map/ppermute | solution.py:753
  638.6 18.5 %collective-permute-done.51 = bf16[144,1152]{1,0:T(8,128)(2,1)S(1)} collective-permute-done((bf16[144,1152]{1,0:T(8,128)(2,1)S(1)}, bf16[144,1152]{1,0:T(8,128)(2,1)S(1)}, u32[]{:S(2)}, u32[]{:S(2)}) %collective-permute-start.51) | collective-permute-done | bytes 331808 | tf_op jit(solution)/shard_map/ppermute | solution.py:753
  (252 shorter events, 152.0 us)
Async XLA Ops:
  8.0 40.1 %collective-permute-start.2 = (bf16[576,1152]{1,0:T(8,128)(2,1)}, bf16[576,1152]{1,0:T(8,128)(2,1)}, u32[]{:S(2)}, u32[]{:S(2)}) collective-permute-start(bf16[576,1152]{1,0:T(8,128)(2,1)} %weave.1.refs_6_.refs_1_), channel_id=1, source_target_pairs={{0,1},{1,0},{2,3},{3,2},{4,5},{5,4},{6,7},{7,6},{8,9},{9,8},{10,11... | collective-permute-start | bytes 3981320 | tf_op jit(solution)/shard_map/ppermute | solution.py:749
  56.5 54.9 %collective-permute-start.12 = (bf16[576,1152]{1,0:T(8,128)(2,1)S(1)}, bf16[576,1152]{1,0:T(8,128)(2,1)S(1)}, u32[]{:S(2)}, u32[]{:S(2)}) collective-permute-start(bf16[576,1152]{1,0:T(8,128)(2,1)S(1)} %pad.25.refs_7_), channel_id=1, source_target_pairs={{0,4},{4,0},{1,5},{5,1},{2,6},{6,2},{3,7},{7,3},{8,12},{12,8},{9,1... | collective-permute-start | bytes 3981320 | tf_op jit(solution)/shard_map/ppermute | solution.py:745
  76.5 94.9 %collective-permute-start.13 = (bf16[576,1152]{1,0:T(8,128)(2,1)S(1)}, bf16[576,1152]{1,0:T(8,128)(2,1)}, u32[]{:S(2)}, u32[]{:S(2)}) collective-permute-start(bf16[576,1152]{1,0:T(8,128)(2,1)S(1)} %pad.25.refs_7_), channel_id=1, source_target_pairs={{0,1},{1,0},{2,3},{3,2},{4,5},{5,4},{6,7},{7,6},{8,9},{9,8},{10,11... | collective-permute-start | bytes 3981320 | tf_op jit(solution)/shard_map/ppermute | solution.py:749
  76.5 96.7 %collective-permute-start.16 = (bf16[576,1152]{1,0:T(8,128)(2,1)S(1)}, bf16[576,1152]{1,0:T(8,128)(2,1)}, u32[]{:S(2)}, u32[]{:S(2)}) collective-permute-start(bf16[576,1152]{1,0:T(8,128)(2,1)S(1)} %pad.26.refs_11_), channel_id=1, source_target_pairs={{0,1},{1,0},{2,3},{3,2},{4,5},{5,4},{6,7},{7,6},{8,9},{9,8},{10,11... | collective-permute-start | bytes 3981320 | tf_op jit(solution)/shard_map/ppermute | solution.py:749
  77.0 96.3 %collective-permute-start.20 = (bf16[576,1152]{1,0:T(8,128)(2,1)S(1)}, bf16[576,1152]{1,0:T(8,128)(2,1)}, u32[]{:S(2)}, u32[]{:S(2)}) collective-permute-start(bf16[576,1152]{1,0:T(8,128)(2,1)S(1)} %pad.25.refs_7_), channel_id=1, source_target_pairs={{0,2},{1,3},{2,0},{3,1},{4,6},{5,7},{6,4},{7,5},{8,10},{9,11},{10,... | collective-permute-start | bytes 3981320 | tf_op jit(solution)/shard_map/ppermute | solution.py:749
  84.9 88.8 %collective-permute-start.17 = (bf16[576,1152]{1,0:T(8,128)(2,1)}, bf16[576,1152]{1,0:T(8,128)(2,1)}, u32[]{:S(2)}, u32[]{:S(2)}) collective-permute-start(bf16[576,1152]{1,0:T(8,128)(2,1)} %collective-permute-done.15.refs_12_), channel_id=1, source_target_pairs={{0,1},{1,0},{2,3},{3,2},{4,5},{5,4},{6,7},{7,6},{8,9},{9,8},{10,11... | collective-permute-start | bytes 3981320 | tf_op jit(solution)/shard_map/ppermute | solution.py:749
  111.4 64.0 %collective-permute-start.14 = (bf16[576,1152]{1,0:T(8,128)(2,1)S(1)}, bf16[576,1152]{1,0:T(8,128)(2,1)}, u32[]{:S(2)}, u32[]{:S(2)}) collective-permute-start(bf16[576,1152]{1,0:T(8,128)(2,1)S(1)} %collective-permute-done.12.refs_8_), channel_id=1, source_target_pairs={{0,1},{1,0},{2,3},{3,2},{4,5},{5,4},{6,7},{7,6},{8,9},{9,8},{10,11... | collective-permute-start | bytes 3981320 | tf_op jit(solution)/shard_map/ppermute | solution.py:749
  173.2 58.2 %collective-permute-start.18 = (bf16[1152,768]{1,0:T(8,128)(2,1)}, bf16[1152,768]{1,0:T(8,128)(2,1)}, u32[]{:S(2)}, u32[]{:S(2)}) collective-permute-start(bf16[1152,768]{1,0:T(8,128)(2,1)} %get-tuple-element.119.refs_0_), channel_id=1, source_target_pairs={{0,1},{1,0},{2,3},{3,2},{4,5},{5,4},{6,7},{7,6},{8,9},{9,8},{10,11... | collective-permute-start | bytes 5308424 | tf_op jit(solution)/shard_map/ppermute | solution.py:749
  173.3 58.1 %collective-permute-start.25 = (bf16[576,1152]{1,0:T(8,128)(2,1)}, bf16[576,1152]{1,0:T(8,128)(2,1)}, u32[]{:S(2)}, u32[]{:S(2)}) collective-permute-start(bf16[576,1152]{1,0:T(8,128)(2,1)} %collective-permute-done.15.refs_12_), channel_id=1, source_target_pairs={{0,2},{1,3},{2,0},{3,1},{4,6},{5,7},{6,4},{7,5},{8,10},{9,11},{10,... | collective-permute-start | bytes 3981320 | tf_op jit(solution)/shard_map/ppermute | solution.py:749
  285.6 88.1 %collective-permute-start.28 = (bf16[1152,768]{1,0:T(8,128)(2,1)}, bf16[1152,768]{1,0:T(8,128)(2,1)}, u32[]{:S(2)}, u32[]{:S(2)}) collective-permute-start(bf16[1152,768]{1,0:T(8,128)(2,1)} %get-tuple-element.137.refs_0_), channel_id=1, source_target_pairs={{0,1},{1,0},{2,3},{3,2},{4,5},{5,4},{6,7},{7,6},{8,9},{9,8},{10,11... | collective-permute-start | bytes 5308424 | tf_op jit(solution)/shard_map/ppermute | solution.py:749
  288.5 85.7 %collective-permute-start.35 = (bf16[736,384]{1,0:T(8,128)(2,1)S(1)}, bf16[736,384]{1,0:T(8,128)(2,1)}, u32[]{:S(2)}, u32[]{:S(2)}) collective-permute-start(bf16[736,384]{1,0:T(8,128)(2,1)S(1)} %copy-done.33), channel_id=1, source_target_pairs={{0,1},{1,0},{2,3},{3,2},{4,5},{5,4},{6,7},{7,6},{8,9},{9,8},{10,11... | collective-permute-start | bytes 1695752 | tf_op jit(solution)/shard_map/ppermute | solution.py:749
  299.1 75.1 %collective-permute-start.34 = (bf16[1152,768]{1,0:T(8,128)(2,1)}, bf16[1152,768]{1,0:T(8,128)(2,1)}, u32[]{:S(2)}, u32[]{:S(2)}) collective-permute-start(bf16[1152,768]{1,0:T(8,128)(2,1)} %get-tuple-element.176.refs_4_), channel_id=1, source_target_pairs={{0,1},{1,0},{2,3},{3,2},{4,5},{5,4},{6,7},{7,6},{8,9},{9,8},{10,11... | collective-permute-start | bytes 5308424 | tf_op jit(solution)/shard_map/ppermute | solution.py:749
  320.6 180.4 %collective-permute-start.60 = (bf16[576,1152]{1,0:T(8,128)(2,1)}, bf16[576,1152]{1,0:T(8,128)(2,1)S(1)}, u32[]{:S(2)}, u32[]{:S(2)}) collective-permute-start(bf16[576,1152]{1,0:T(8,128)(2,1)} %get-tuple-element.160), channel_id=1, source_target_pairs={{0,4},{4,0},{1,5},{5,1},{2,6},{6,2},{3,7},{7,3},{8,12},{12,8},{9,1... | collective-permute-start | bytes 3981320 | tf_op jit(solution)/shard_map/ppermute | solution.py:745
  373.7 42.7 %collective-permute-start.41 = (bf16[736,896]{1,0:T(8,128)(2,1)}, bf16[736,896]{1,0:T(8,128)(2,1)}, u32[]{:S(2)}, u32[]{:S(2)}) collective-permute-start(bf16[736,896]{1,0:T(8,128)(2,1)} %get-tuple-element.187), channel_id=1, source_target_pairs={{0,1},{1,0},{2,3},{3,2},{4,5},{5,4},{6,7},{7,6},{8,9},{9,8},{10,11... | collective-permute-start | bytes 3956744 | tf_op jit(solution)/shard_map/ppermute | solution.py:749
  411.8 126.5 %collective-permute-start.53 = (bf16[576,1152]{1,0:T(8,128)(2,1)}, bf16[576,1152]{1,0:T(8,128)(2,1)S(1)}, u32[]{:S(2)}, u32[]{:S(2)}) collective-permute-start(bf16[576,1152]{1,0:T(8,128)(2,1)} %get-tuple-element.129), channel_id=1, source_target_pairs={{0,4},{4,0},{1,5},{5,1},{2,6},{6,2},{3,7},{7,3},{8,12},{12,8},{9,1... | collective-permute-start | bytes 3981320 | tf_op jit(solution)/shard_map/ppermute | solution.py:745
  414.2 91.2 %collective-permute-start.54 = (bf16[576,1152]{1,0:T(8,128)(2,1)}, bf16[576,1152]{1,0:T(8,128)(2,1)}, u32[]{:S(2)}, u32[]{:S(2)}) collective-permute-start(bf16[576,1152]{1,0:T(8,128)(2,1)} %get-tuple-element.154), channel_id=1, source_target_pairs={{0,4},{4,0},{1,5},{5,1},{2,6},{6,2},{3,7},{7,3},{8,12},{12,8},{9,1... | collective-permute-start | bytes 3981320 | tf_op jit(solution)/shard_map/ppermute | solution.py:745
  414.5 119.0 %collective-permute-start.59 = (bf16[576,1152]{1,0:T(8,128)(2,1)}, bf16[576,1152]{1,0:T(8,128)(2,1)}, u32[]{:S(2)}, u32[]{:S(2)}) collective-permute-start(bf16[576,1152]{1,0:T(8,128)(2,1)} %get-tuple-element.157), channel_id=1, source_target_pairs={{0,4},{4,0},{1,5},{5,1},{2,6},{6,2},{3,7},{7,3},{8,12},{12,8},{9,1... | collective-permute-start | bytes 3981320 | tf_op jit(solution)/shard_map/ppermute | solution.py:745
  416.3 84.2 %collective-permute-start.38 = (f32[8,1152]{1,0:T(8,128)S(1)}, f32[8,1152]{1,0:T(8,128)S(1)}, u32[]{:S(2)}, u32[]{:S(2)}) collective-permute-start(f32[8,1152]{1,0:T(8,128)S(1)} %slice_add_fusion), channel_id=1, source_target_pairs={{0,4},{4,0},{1,5},{5,1},{2,6},{6,2},{3,7},{7,3},{8,12},{12,8},{9,1... | collective-permute-start | bytes 110600 | tf_op jit(solution)/shard_map/ppermute | solution.py:745
  510.4 80.1 %collective-permute-start.45 = (bf16[288,1152]{1,0:T(8,128)(2,1)S(1)}, bf16[288,1152]{1,0:T(8,128)(2,1)S(1)}, u32[]{:S(2)}, u32[]{:S(2)}) collective-permute-start(bf16[288,1152]{1,0:T(8,128)(2,1)S(1)} %copy-done.32), channel_id=1, source_target_pairs={{0,4},{4,0},{1,5},{5,1},{2,6},{6,2},{3,7},{7,3},{8,12},{12,8},{9,1... | collective-permute-start | bytes 1990664 | tf_op jit(solution)/shard_map/ppermute | solution.py:745
  534.3 56.2 %collective-permute-start.49 = (bf16[288,1152]{1,0:T(8,128)(2,1)S(1)}, bf16[288,1152]{1,0:T(8,128)(2,1)S(1)}, u32[]{:S(2)}, u32[]{:S(2)}) collective-permute-start(bf16[288,1152]{1,0:T(8,128)(2,1)S(1)} %copy-done.31), channel_id=1, source_target_pairs={{0,4},{4,0},{1,5},{5,1},{2,6},{6,2},{3,7},{7,3},{8,12},{12,8},{9,1... | collective-permute-start | bytes 1990664 | tf_op jit(solution)/shard_map/ppermute | solution.py:745
  535.9 54.7 %collective-permute-start.44 = (bf16[576,1152]{1,0:T(8,128)(2,1)S(1)}, bf16[576,1152]{1,0:T(8,128)(2,1)S(1)}, u32[]{:S(2)}, u32[]{:S(2)}) collective-permute-start(bf16[576,1152]{1,0:T(8,128)(2,1)S(1)} %add_convert_fusion.6), channel_id=1, source_target_pairs={{0,2},{1,3},{2,0},{3,1},{4,6},{5,7},{6,4},{7,5},{8,10},{9,11},{10,... | collective-permute-start | bytes 3981320 | tf_op jit(solution)/shard_map/ppermute | solution.py:749
  568.5 42.8 %collective-permute-start.63 = (bf16[288,1152]{1,0:T(8,128)(2,1)S(1)}, bf16[288,1152]{1,0:T(8,128)(2,1)S(1)}, u32[]{:S(2)}, u32[]{:S(2)}) collective-permute-start(bf16[288,1152]{1,0:T(8,128)(2,1)S(1)} %add_convert_fusion.8), channel_id=1, source_target_pairs={{0,16},{8,24},{16,0},{24,8},{1,17},{9,25},{17,1},{25,9},{2,18},{10... | collective-permute-start | bytes 1990664 | tf_op jit(solution)/shard_map/ppermute | solution.py:753
  611.5 56.7 %collective-permute-start.64 = (bf16[288,1152]{1,0:T(8,128)(2,1)S(1)}, bf16[288,1152]{1,0:T(8,128)(2,1)S(1)}, u32[]{:S(2)}, u32[]{:S(2)}) collective-permute-start(bf16[288,1152]{1,0:T(8,128)(2,1)S(1)} %add_convert_fusion.7), channel_id=1, source_target_pairs={{0,8},{8,0},{16,24},{24,16},{1,9},{9,1},{17,25},{25,17},{2,10},{10... | collective-permute-start | bytes 1990664 | tf_op jit(solution)/shard_map/ppermute | solution.py:753
  624.0 45.9 %collective-permute-start.58 = (bf16[288,1152]{1,0:T(8,128)(2,1)S(1)}, bf16[288,1152]{1,0:T(8,128)(2,1)S(1)}, u32[]{:S(2)}, u32[]{:S(2)}) collective-permute-start(bf16[288,1152]{1,0:T(8,128)(2,1)S(1)} %add_convert_fusion.9), channel_id=1, source_target_pairs={{0,8},{8,0},{16,24},{24,16},{1,9},{9,1},{17,25},{25,17},{2,10},{10... | collective-permute-start | bytes 1990664 | tf_op jit(solution)/shard_map/ppermute | solution.py:753
  (78 other events, 1734.9 us)
